TPU v7x, 16 devices: a whole 2x2x2 slice. The times are simulated.
16 devices in a mesh: fsdp: 16 (over z, y, x, core).
Axes of the slice: x: 2, y: 2, z: 2, core: 2. Of those that a mesh axis runs over, the one named last changes fastest.
Arguments:
- act_in: bfloat16 [512, 49, 512], P('fsdp')
- labels: int32 [512], P('fsdp')
- layer_p: float32 [2, 2127872], P(None, 'fsdp')
- head_w: float32 [512, 1000], P('fsdp')
- small_p: float32 [2048], P('fsdp')
- layer_m: float32 [2, 2127872], P(None, 'fsdp')
- head_m: float32 [512, 1000], P('fsdp')
- small_m: float32 [2048], P('fsdp')
- layer_v: float32 [2, 2127872], P(None, 'fsdp')
- head_v: float32 [512, 1000], P('fsdp')
- small_v: float32 [2048], P('fsdp')
Outputs:
- output 1: float32 [], replicated
- output 2: float32 [2, 2127872], P(None, 'fsdp')
- output 3: float32 [512, 1000], P('fsdp')
- output 4: float32 [2048], P('fsdp')
- output 5: float32 [2, 2127872], P(None, 'fsdp')
- output 6: float32 [512, 1000], P('fsdp')
- output 7: float32 [2048], P('fsdp')
- output 8: float32 [2, 2127872], P(None, 'fsdp')
- output 9: float32 [512, 1000], P('fsdp')
- output 10: float32 [2048], P('fsdp')
All inputs are finite; a program needn't handle non-finite values.
Results may differ from a plain program's by a relative error of at most 0.001.
Values are sent between devices in bfloat16 or wider.
A program may use at most 1 GiB of HBM per device.

v0:
```python
import math
import jax
import jax.numpy as jnp
from jax import lax
from jax.sharding import PartitionSpec as P

LN_EPS = 1e-6
LEARN_RATE = 0.003
BETA_ONE = 0.9
BETA_TWO = 0.999
ADAM_EPS = 1e-8
WEIGHT_DECAY = 0.03
ADAM_STEP = 10


def piece_shapes(num_tokens, num_chans):
    tok_hid = num_chans // 2
    ch_hid = 4 * num_chans
    return [(num_tokens, tok_hid), (tok_hid, num_tokens), (num_chans, ch_hid), (ch_hid, num_chans), (num_chans,), (num_chans,), (tok_hid,), (num_tokens,), (num_chans,), (num_chans,), (ch_hid,), (num_chans,)]


def layer_length(num_tokens, num_chans):
    return sum(math.prod(shape_one) for shape_one in piece_shapes(num_tokens, num_chans))


def unpack_layer(flat, num_tokens, num_chans):
    pieces = []
    piece_start = 0
    for shape_one in piece_shapes(num_tokens, num_chans):
        piece_len = math.prod(shape_one)
        pieces.append(flat[piece_start:piece_start + piece_len].reshape(shape_one))
        piece_start = piece_start + piece_len
    return pieces


def layer_norm(x_in, ln_gain, ln_shift):
    x_f = x_in.astype(jnp.float32)
    mean_val = jnp.mean(x_f, axis=-1, keepdims=True)
    var_val = jnp.mean(jnp.square(x_f - mean_val), axis=-1, keepdims=True)
    normed = (x_f - mean_val) * lax.rsqrt(var_val + LN_EPS)
    return (normed * ln_gain.astype(jnp.float32) + ln_shift.astype(jnp.float32)).astype(jnp.bfloat16)


def gelu_bf16(hidden):
    return jax.nn.gelu(hidden).astype(jnp.bfloat16)


def gelu_grad(hidden, d_act):
    _, pullback = jax.vjp(gelu_bf16, hidden)
    return pullback(d_act.astype(jnp.bfloat16))[0]


def norm_grad(x_in, ln_gain, ln_shift, d_normed):
    _, pullback = jax.vjp(layer_norm, x_in, ln_gain.astype(jnp.float32), ln_shift.astype(jnp.float32))
    d_x, d_gain, d_shift = pullback(d_normed.astype(jnp.bfloat16))
    return d_x.astype(jnp.float32), d_gain, d_shift


def layer_forward(x_in, flat, num_tokens, num_chans):
    w_tok1, w_tok2, w_ch1, w_ch2, ln1_g, ln1_b, b_tok1, b_tok2, ln2_g, ln2_b, b_ch1, b_ch2 = unpack_layer(flat, num_tokens, num_chans)
    normed = layer_norm(x_in, ln1_g, ln1_b)
    hid_tok = jnp.einsum('bsc,sj->bcj', normed, w_tok1, preferred_element_type=jnp.float32) + b_tok1.astype(jnp.float32)
    act_tok = gelu_bf16(hid_tok)
    tok_out = jnp.einsum('bcj,js->bsc', act_tok, w_tok2, preferred_element_type=jnp.float32) + b_tok2.astype(jnp.float32)[:, None]
    after_tok = (x_in.astype(jnp.float32) + tok_out).astype(jnp.bfloat16)
    normed2 = layer_norm(after_tok, ln2_g, ln2_b)
    hid_ch = jnp.einsum('bsc,cd->bsd', normed2, w_ch1, preferred_element_type=jnp.float32) + b_ch1.astype(jnp.float32)
    act_ch = gelu_bf16(hid_ch)
    ch_out = jnp.einsum('bsd,dc->bsc', act_ch, w_ch2, preferred_element_type=jnp.float32) + b_ch2.astype(jnp.float32)
    layer_out = (after_tok.astype(jnp.float32) + ch_out).astype(jnp.bfloat16)
    return layer_out, (x_in, normed, hid_tok, act_tok, after_tok, normed2, hid_ch, act_ch)


def layer_backward(d_out, flat, cache, num_tokens, num_chans):
    w_tok1, w_tok2, w_ch1, w_ch2, ln1_g, ln1_b, b_tok1, b_tok2, ln2_g, ln2_b, b_ch1, b_ch2 = unpack_layer(flat, num_tokens, num_chans)
    x_in, normed, hid_tok, act_tok, after_tok, normed2, hid_ch, act_ch = cache
    d_out_bf = d_out.astype(jnp.bfloat16)
    g_b_ch2 = jnp.sum(d_out, axis=(0, 1))
    g_w_ch2 = jnp.einsum('bsd,bsc->dc', act_ch, d_out_bf, preferred_element_type=jnp.float32)
    d_act_ch = jnp.einsum('bsc,dc->bsd', d_out_bf, w_ch2, preferred_element_type=jnp.float32)
    d_hid_ch = gelu_grad(hid_ch, d_act_ch)
    d_hid_ch_bf = d_hid_ch.astype(jnp.bfloat16)
    g_b_ch1 = jnp.sum(d_hid_ch, axis=(0, 1))
    g_w_ch1 = jnp.einsum('bsc,bsd->cd', normed2, d_hid_ch_bf, preferred_element_type=jnp.float32)
    d_normed2 = jnp.einsum('bsd,cd->bsc', d_hid_ch_bf, w_ch1, preferred_element_type=jnp.float32)
    d_after_ln, g_ln2_g, g_ln2_b = norm_grad(after_tok, ln2_g, ln2_b, d_normed2)
    d_after = d_after_ln + d_out
    d_after_bf = d_after.astype(jnp.bfloat16)
    g_b_tok2 = jnp.sum(d_after, axis=(0, 2))
    g_w_tok2 = jnp.einsum('bcj,bsc->js', act_tok, d_after_bf, preferred_element_type=jnp.float32)
    d_act_tok = jnp.einsum('bsc,js->bcj', d_after_bf, w_tok2, preferred_element_type=jnp.float32)
    d_hid_tok = gelu_grad(hid_tok, d_act_tok)
    d_hid_tok_bf = d_hid_tok.astype(jnp.bfloat16)
    g_b_tok1 = jnp.sum(d_hid_tok, axis=(0, 1))
    g_w_tok1 = jnp.einsum('bsc,bcj->sj', normed, d_hid_tok_bf, preferred_element_type=jnp.float32)
    d_normed = jnp.einsum('bcj,sj->bsc', d_hid_tok_bf, w_tok1, preferred_element_type=jnp.float32)
    d_in_ln, g_ln1_g, g_ln1_b = norm_grad(x_in, ln1_g, ln1_b, d_normed)
    d_in = d_in_ln + d_after
    pad_len = flat.shape[0] - layer_length(num_tokens, num_chans)
    flat_grad = jnp.concatenate([g_w_tok1.reshape(-1), g_w_tok2.reshape(-1), g_w_ch1.reshape(-1), g_w_ch2.reshape(-1), g_ln1_g, g_ln1_b, g_b_tok1, g_b_tok2, g_ln2_g, g_ln2_b, g_b_ch1, g_b_ch2, jnp.zeros((pad_len,), jnp.float32)])
    return d_in, flat_grad


def head_step(hidden, labels, small_full, head_full, global_b):
    num_tokens = hidden.shape[1]
    num_chans = hidden.shape[2]
    num_classes = head_full.shape[1]
    lnf_g = small_full[:num_chans]
    lnf_b = small_full[num_chans:2 * num_chans]
    head_b = small_full[2 * num_chans:2 * num_chans + num_classes]
    normed = layer_norm(hidden, lnf_g, lnf_b)
    pooled = (jnp.sum(normed, axis=1, dtype=jnp.float32) / num_tokens).astype(jnp.bfloat16)
    logits = jnp.dot(pooled, head_full, preferred_element_type=jnp.float32) + head_b.astype(jnp.float32)
    log_norm = jax.nn.logsumexp(logits, axis=-1)
    is_label = jnp.arange(num_classes)[None, :] == labels[:, None]
    picked = jnp.sum(jnp.where(is_label, logits, 0.0), axis=-1)
    loss_sum = jnp.sum(log_norm - picked)
    d_logits = (jnp.exp(logits - log_norm[:, None]) - is_label.astype(jnp.float32)) / global_b
    d_logits_bf = d_logits.astype(jnp.bfloat16)
    g_head_b = jnp.sum(d_logits, axis=0)
    g_head_w = jnp.einsum('bc,bk->ck', pooled, d_logits_bf, preferred_element_type=jnp.float32)
    d_pooled = jnp.einsum('bk,ck->bc', d_logits_bf, head_full, preferred_element_type=jnp.float32)
    d_normed = jnp.broadcast_to((d_pooled / num_tokens)[:, None, :], normed.shape)
    d_hidden, g_lnf_g, g_lnf_b = norm_grad(hidden, lnf_g, lnf_b, d_normed)
    g_small = jnp.concatenate([g_lnf_g, g_lnf_b, g_head_b])
    return loss_sum, d_hidden, g_head_w, g_small


def adam_update(master, gradient, moment, second, decay_rate):
    moment_new = BETA_ONE * moment + (1.0 - BETA_ONE) * gradient
    second_new = BETA_TWO * second + (1.0 - BETA_TWO) * gradient * gradient
    m_hat = moment_new / (1.0 - BETA_ONE ** ADAM_STEP)
    v_hat = second_new / (1.0 - BETA_TWO ** ADAM_STEP)
    master_new = master - LEARN_RATE * (m_hat / (jnp.sqrt(v_hat) + ADAM_EPS) + decay_rate * master)
    return master_new, moment_new, second_new


def solution(mesh):
    group = mesh.shape['fsdp']
    row_spec = P('fsdp')
    layer_spec = P(None, 'fsdp')
    in_specs = (row_spec, row_spec, layer_spec, row_spec, row_spec, layer_spec, row_spec, row_spec, layer_spec, row_spec, row_spec)
    out_specs = (P(),) + in_specs[2:]

    def device_step(act_in, labels, layer_p, head_w, small_p, layer_m, head_m, small_m, layer_v, head_v, small_v):
        local_b, num_tokens, num_chans = act_in.shape
        global_b = local_b * group
        num_layers = layer_p.shape[0]
        mat_len = 2 * num_tokens * (num_chans // 2) + 8 * num_chans * num_chans
        caches = []
        hidden = act_in
        for layer_idx in range(num_layers):
            flat_full = lax.all_gather(layer_p[layer_idx].astype(jnp.bfloat16), 'fsdp', tiled=True)
            hidden, cache = layer_forward(hidden, flat_full, num_tokens, num_chans)
            caches.append(cache)
        small_full = lax.all_gather(small_p.astype(jnp.bfloat16), 'fsdp', tiled=True)
        head_full = lax.all_gather(head_w.astype(jnp.bfloat16), 'fsdp', tiled=True)
        loss_sum, d_hidden, g_head_w, g_small = head_step(hidden, labels, small_full, head_full, global_b)
        layer_shards = [None] * num_layers
        for layer_idx in reversed(range(num_layers)):
            flat_full = lax.all_gather(layer_p[layer_idx].astype(jnp.bfloat16), 'fsdp', tiled=True)
            d_hidden, flat_grad = layer_backward(d_hidden, flat_full, caches[layer_idx], num_tokens, num_chans)
            layer_shards[layer_idx] = lax.psum_scatter(flat_grad, 'fsdp', scatter_dimension=0, tiled=True)
        layer_g = jnp.stack(layer_shards)
        head_g = lax.psum_scatter(g_head_w, 'fsdp', scatter_dimension=0, tiled=True)
        small_flat = jnp.concatenate([g_small, jnp.zeros((small_full.shape[0] - g_small.shape[0],), jnp.float32)])
        small_g = lax.psum_scatter(small_flat, 'fsdp', scatter_dimension=0, tiled=True)
        loss_value = lax.psum(loss_sum, 'fsdp') / global_b
        sq_local = jnp.sum(jnp.square(layer_g)) + jnp.sum(jnp.square(head_g)) + jnp.sum(jnp.square(small_g))
        grad_norm = jnp.sqrt(lax.psum(sq_local, 'fsdp'))
        clip_scale = 1.0 / jnp.maximum(1.0, grad_norm)
        shard_len = layer_p.shape[1]
        flat_pos = lax.axis_index('fsdp') * shard_len + jnp.arange(shard_len)
        layer_decay = jnp.where(flat_pos < mat_len, WEIGHT_DECAY, 0.0)[None, :]
        new_lp, new_lm, new_lv = adam_update(layer_p, layer_g * clip_scale, layer_m, layer_v, layer_decay)
        new_hw, new_hm, new_hv = adam_update(head_w, head_g * clip_scale, head_m, head_v, WEIGHT_DECAY)
        new_sp, new_sm, new_sv = adam_update(small_p, small_g * clip_scale, small_m, small_v, 0.0)
        return (loss_value, new_lp, new_hw, new_sp, new_lm, new_hm, new_sm, new_lv, new_hv, new_sv)

    return jax.shard_map(device_step, mesh=mesh, in_specs=in_specs, out_specs=out_specs, check_vma=False)
```

profile of v0, /device:TPU:0, one launch (start us, length us, event | category | flops | bytes accessed | tf_op | source)
XLA Modules:
  0.0 832.0 jit_solution(10621342949329260159)
XLA Ops:
  7.2 1.6 convert.4
  8.8 1.6 fusion.208
  11.2 1.2 convert_reduce_fusion.5
  12.4 1.4 fusion.103
  13.9 14.4 %all-gather.2 = bf16[16,1,128]{2,1,0:T(2,128)(2,1)S(1)} all-gather(bf16[1,1,128]{2,1,0:T(2,128)(2,1)S(1)} %convert_bitcast_fusion.2), channel_id=1, replica_groups=mesh['fsdp'=16] {'fsdp'}, dimensions={0}, use_global_device_ids=true | all-gather | bytes 4352 | tf_op jit(solution)/shard_map/all_gather | solution.py:156
  28.3 16.0 %all_gather.17 = bf16[512,1000]{1,0:T(8,128)(2,1)S(1)} all-gather(bf16[32,1000]{1,0:T(8,128)(2,1)S(1)} %convert_element_type.303), channel_id=1, replica_groups=mesh['fsdp'=16] {'fsdp'}, dimensions={0}, use_global_device_ids=true | all-gather | bytes 1088000 | tf_op jit(solution)/shard_map/all_gather | solution.py:157
  44.3 21.6 %all-gather.6.cloned.1.call-done = bf16[1,2127872]{1,0:T(2,128)(2,1)} async-done(((bf16[1,132992]{1,0:T(2,128)(2,1)}), bf16[1,2127872]{1,0:T(2,128)(2,1)}) %all-gather.6.cloned.1.call-update) | async-done | bytes 4255760 | tf_op jit(solution)/shard_map/all_gather | solution.py:153
  65.9 1.1 slice_reduce_fusion.6
  67.3 47.4 %slice_reduce_fusion.2 = (bf16[1048576]{0:T(1024)(128)(2,1)}, bf16[1048576]{0:T(1024)(128)(2,1)}) fusion(bf16[1,2127872]{1,0:T(2,128)(2,1)} %all-gather.6.cloned.1.call-done), kind=kLoop, calls=%fused_computation.110 | loop fusion | bytes 8388608 | tf_op jit(solution)/shard_map/slice | solution.py:31
  114.7 4.2 reshape.360
  118.8 4.4 reshape.361
  125.3 10.7 %multiply_convert_fusion.1 = (bf16[32,512,256]{2,1,0:T(8,128)(2,1)S(1)}, f32[32,512,256]{2,1,0:T(8,128)}) fusion(f32[256]{0:T(256)S(1)} %bitcast.181, bf16[49,256,1]{1,0,2:T(8,128)(2,1)S(1)} %reshape.358, f32[512]{0:T(512)S(1)} %bitcast.169, f32[512]{0:T(512)S(1)} %bitcast.171, f32[32,49]{1,0:T(8,128)S(1)} %add_rsqrt_fusion, ...), kind=kOutput, calls=%fused_computation.35 | convolution fusion | flops 457801728 | bytes 26814208 | tf_op jit(solution)/shard_map/bsc,sj->bcj/dot_general | solution.py:62
  136.1 3.3 convert_reduce_fusion.4
  141.3 10.5 %multiply_convert_fusion.3 = (bf16[32,49,2048]{2,1,0:T(8,128)(2,1)S(1)}, f32[32,49,2048]{2,1,0:T(8,128)}) fusion(f32[2048]{0:T(1024)S(1)} %bitcast.164, bf16[512,2048,1]{1,0,2:T(8,128)(2,1)S(1)} %copy-done.25, bf16[32,49,512]{2,1,0:T(8,128)(2,1)S(1)} %get-tuple-element.71, f32[512]{0:T(512)S(1)} %bitcast.177, f32[512]{0:T(512)S(1)} %bitcast.156, ...), kind=kOutput, calls=%fused_computation.55 | convolution fusion | flops 3325263872 | bytes 22995200 | tf_op jit(solution)/shard_map/bsc,cd->bsd/dot_general | solution.py:67
  151.8 4.5 convert_reduce_fusion.3
  157.3 1.1 slice_reduce_fusion.4
  160.2 10.0 %multiply_convert_fusion = (bf16[32,512,256]{2,1,0:T(8,128)(2,1)S(1)}, f32[32,512,256]{2,1,0:T(8,128)}) fusion(f32[256]{0:T(256)S(1)} %bitcast.183, bf16[49,256,1]{1,0,2:T(8,128)(2,1)S(1)} %reshape.362, bf16[32,49,512]{2,1,0:T(8,128)(2,1)S(1)} %get-tuple-element.75, f32[512]{0:T(512)S(1)} %bitcast.173, f32[512]{0:T(512)S(1)} %bitcast.152, ...), kind=kOutput, calls=%fused_computation.34 | convolution fusion | flops 457801728 | bytes 26814208 | tf_op jit(solution)/shard_map/bsc,sj->bcj/dot_general | solution.py:62
  170.9 2.7 convert_reduce_fusion.2
  173.6 1.2 copy-done.5
  175.7 47.4 %slice_reduce_fusion = (bf16[1048576]{0:T(1024)(128)(2,1)}, bf16[1048576]{0:T(1024)(128)(2,1)}) fusion(bf16[1,2127872]{1,0:T(2,128)(2,1)} %all-gather.8.cloned.1.call-done), kind=kLoop, calls=%fused_computation.108 | loop fusion | bytes 8388608 | tf_op jit(solution)/shard_map/slice | solution.py:31
  223.1 4.3 reshape.364
  227.4 4.4 reshape.365
  232.6 12.1 %multiply_convert_fusion.2 = (bf16[32,49,2048]{2,1,0:T(8,128)(2,1)S(1)}, f32[32,49,2048]{2,1,0:T(8,128)}) fusion(f32[2048]{0:T(1024)S(1)} %bitcast.166, bf16[512,2048,1]{1,0,2:T(8,128)(2,1)} %reshape.364, bf16[32,49,512]{2,1,0:T(8,128)(2,1)S(1)} %copy-done.6, f32[512]{0:T(512)S(1)} %bitcast.175, f32[512]{0:T(512)S(1)} %bitcast.160, ...), kind=kOutput, calls=%fused_computation.54 | convolution fusion | flops 3325263872 | bytes 22995200 | tf_op jit(solution)/shard_map/bsc,cd->bsd/dot_general | solution.py:67
  244.8 4.4 convert_reduce_fusion.9
  250.0 1.1 convert_reduce_fusion.10
  252.2 1.8 fusion.188
  254.0 1.4 fusion.48
  256.4 17.0 %fusion.211 = (f32[2048]{0:T(1024)}, bf16[32,49,2048]{2,1,0:T(8,128)(2,1)S(1)}) fusion(f32[32,49,2048]{2,1,0:T(8,128)} %get-tuple-element.81, f32[2048]{0:T(1024)S(1)} %bitcast.167, bf16[2048,512,1]{1,0,2:T(8,128)(2,1)S(1)} %copy-done.31, bf16[32,49,512]{2,1,0:T(8,128)(2,1)S(1)} %get-tuple-element.83, f32[32,49]{1,0:T(8,128)S(1)} %add_multiply_fusion.3, ...), kind=kOutput, calls=%fused_computation.298 | convolution fusion | flops 3371825152 | bytes 23079424 | tf_op jit(solution)/shard_map/bsc,dc->bsd/dot_general | solution.py:80
  273.4 6.1 fusion.119
  279.5 1.0 fusion.84
  280.6 4.2 convert_reduce_fusion.8
  284.7 18.4 %fusion.210 = (f32[256]{0:T(256)}, bf16[32,512,256]{2,1,0:T(8,128)(2,1)S(1)}) fusion(f32[32,512,256]{2,1,0:T(8,128)} %get-tuple-element.77, f32[256]{0:T(256)S(1)} %bitcast.184, bf16[256,49]{1,0:T(8,128)(2,1)S(1)} %reshape.292, bf16[32,49,512]{2,1,0:T(8,128)(2,1)S(1)} %get-tuple-element.53, f32[32,49]{1,0:T(8,128)S(1)} %add_multiply_fusion.3, ...), kind=kOutput, calls=%fused_computation.297 | convolution fusion | flops 521338624 | bytes 28496896 | tf_op jit(solution)/shard_map/bsc,js->bcj/dot_general | solution.py:91
  303.1 3.8 fusion.114
  307.9 2.8 convert_add_fusion.6
  310.8 6.5 convolution_bitcast_fusion.1
  317.3 17.3 %fusion.213 = (f32[2048]{0:T(1024)}, bf16[32,49,2048]{2,1,0:T(8,128)(2,1)}) fusion(f32[32,49,2048]{2,1,0:T(8,128)} %get-tuple-element.73, f32[2048]{0:T(1024)S(1)} %bitcast.165, bf16[2048,512,1]{1,0,2:T(8,128)(2,1)S(1)} %copy-done.28, f32[32,49,512]{2,1,0:T(8,128)S(1)} %convert_add_fusion.6), kind=kOutput, calls=%fused_computation.300 | convolution fusion | flops 3366205440 | bytes 24592384 | tf_op jit(solution)/shard_map/bsc,dc->bsd/dot_general | solution.py:80
  334.7 9.5 %fusion.136 = f32[64,16,8,128]{3,2,1,0:T(8,128)} fusion(bf16[32,49,2048]{2,1,0:T(8,128)(2,1)} %get-tuple-element.98, bf16[32,49,512]{2,1,0:T(8,128)(2,1)S(1)} %copy-done.11, f32[512]{0:T(512)S(1)} %bitcast.178, f32[512]{0:T(512)S(1)} %bitcast.157, f32[32,49]{1,0:T(8,128)S(1)} %copy-done.57, f32[32,49]{1,0:T(8,128)S(1)} %copy-done.38), kind=kOutput, calls=%fused_computation.189 | convolution fusion | flops 3293151232 | bytes 12239104 | tf_op jit(solution)/shard_map/bsc,bsd->cd/dot_general | solution.py:84
  344.2 6.9 fusion.120
  351.1 6.3 convolution_bitcast_fusion
  357.6 5.5 copy.49
  363.0 3.1 copy.48
  367.2 2.5 fusion.202
  369.8 3.1 convolution_bitcast_fusion.3
  372.8 19.7 %fusion.212 = (f32[256]{0:T(256)}, bf16[32,512,256]{2,1,0:T(8,128)(2,1)}) fusion(f32[32,512,256]{2,1,0:T(8,128)} %get-tuple-element.69, f32[256]{0:T(256)S(1)} %bitcast.182, bf16[256,49]{1,0:T(8,128)(2,1)S(1)} %copy-done.42, f32[32,49,512]{2,1,0:T(8,128)S(1)} %copy-done.2, bf16[32,49,512]{2,1,0:T(8,128)(2,1)} %copy-done.20), kind=kOutput, calls=%fused_computation.299 | convolution fusion | flops 514113280 | bytes 30009856 | tf_op jit(solution)/shard_map/bsc,js->bcj/dot_general | solution.py:91
  392.5 1.7 reshape.295
  394.3 6.5 fusion.154
  400.7 1.4 reshape.294
  402.2 5.4 copy.51
  407.6 7.5 fusion.133
  415.2 2.9 copy.50
  418.1 4.5 convolution_bitcast_fusion.2
  422.6 1.7 reshape.299
  424.3 5.6 fusion.151
  430.1 7.3 fusion.98
  437.8 79.1 %concatenate.9 = f32[2127872]{0:T(1024)} concatenate(f32[12544]{0:T(1024)S(1)} %copy-done.43, f32[12544]{0:T(1024)} %reshape.295, f32[1048576]{0:T(1024)} %bitcast.138, f32[1048576]{0:T(1024)} %bitcast.137, f32[512]{0:T(512)} %get-tuple-element.93, f32[512]{0:T(512)S(1)} %convert_reduce_fusion.6, f32[256]{0:T(256)} %get-tuple-element.95, f32[49]{0:T(128)} %get-tuple-element.25, ...), dimensions={0} | concatenate | bytes 17022976 | tf_op jit(solution)/shard_map/concatenate | solution.py:100
  517.3 74.3 %concatenate.10 = f32[2127872]{0:T(1024)} concatenate(f32[12544]{0:T(1024)S(1)} %reshape.298, f32[12544]{0:T(1024)S(1)} %copy-done.44, f32[1048576]{0:T(1024)} %bitcast.140, f32[1048576]{0:T(1024)} %bitcast.139, f32[512]{0:T(512)S(1)} %copy-done.92, f32[512]{0:T(512)S(1)} %convert_reduce_fusion.7, f32[256]{0:T(256)S(1)} %copy-done.95, f32[49]{0:T(128)S(1)} %copy-done.82, ...), dimensions={0} | concatenate | bytes 17022976 | tf_op jit(solution)/shard_map/concatenate | solution.py:100
  592.9 32.6 %all-reduce.2 = f32[2048]{0:T(1024)S(1)} all-reduce(f32[2048]{0:T(1024)S(1)} %concatenate.11), channel_id=7, replica_groups=mesh['fsdp'=16] {'fsdp'}, use_global_device_ids=true, to_apply=%region_52.53.clone | all-reduce | flops 2048 | bytes 16384
  626.8 1.5 multiply_reduce_fusion.1
  628.3 147.5 %all-reduce.7.cloned.1.call-done = (f32[2127872]{0:T(1024)}, f32[2127872]{0:T(1024)}) async-done(((f32[2127872]{0:T(1024)}, f32[2127872]{0:T(1024)}), (f32[2127872]{0:T(1024)}, f32[2127872]{0:T(1024)})) %all-reduce.7.cloned.1.call-update) | async-done | bytes 17022992
  775.8 1.2 dynamic-slice.1
  777.6 1.3 dynamic-slice
  779.4 1.7 multiply_reduce_fusion
  783.2 31.4 %all-reduce.3 = (f32[]{:T(128)}, f32[]{:T(128)}) all-reduce(f32[]{:T(128)} %subtract_reduce_fusion, f32[]{:T(128)S(6)} %add.360), channel_id=1, replica_groups=mesh['fsdp'=16] {'fsdp'}, use_global_device_ids=true, to_apply=%region_15.16 | all-reduce | flops 2 | bytes 16 | tf_op jit(solution)/shard_map/psum | solution.py:168
  816.7 6.6 multiply_subtract_fusion
  (300 shorter events, 21.1 us)
Async XLA Ops:
  7.2 58.7 %all-gather.6.cloned.1.call-start = ((), (), s32[]{:S(2)}) async-start(), calls=%async_computation.2 | async-start | bytes 9043456 | tf_op jit(solution)/shard_map/all_gather | solution.py:153
  8.8 19.5 %copy-start.33 = (f32[32,1000]{1,0:T(8,128)S(1)}, f32[32,1000]{1,0:T(8,128)}, u32[]{:S(2)}) copy-start(f32[32,1000]{1,0:T(8,128)} %param.14) | copy-start | bytes 384004
  10.4 146.8 %all-gather.8.cloned.1.call-start = ((), (), s32[]{:S(2)}) async-start(), calls=%async_computation.3 | async-start | bytes 9043456 | tf_op jit(solution)/shard_map/all_gather | solution.py:153
  11.2 615.6 %reduce-scatter.2.cloned.1.call-start = ((), (), s32[]{:S(2)}) async-start(), calls=%async_computation.1 | async-start | bytes 2228224 | tf_op jit(solution)/shard_map/reduce_scatter | solution.py:165
  12.4 112.9 %copy-start.53 = (f32[32,49]{1,0:T(8,128)}, f32[32,49]{1,0:T(8,128)S(1)}, u32[]{:S(2)}) copy-start(f32[32,49]{1,0:T(8,128)S(1)} %broadcast_multiply_fusion.4) | copy-start | bytes 18820
  13.8 111.4 %copy-start.64 = (f32[32,49]{1,0:T(8,128)}, f32[32,49]{1,0:T(8,128)S(1)}, u32[]{:S(2)}) copy-start(f32[32,49]{1,0:T(8,128)S(1)} %add_rsqrt_fusion) | copy-start | bytes 18820
  28.3 322.8 %copy-start.60 = (f32[4,1,128]{2,1,0:T(1,128)}, f32[4,1,128]{2,1,0:T(1,128)S(1)}, u32[]{:S(2)}) copy-start(f32[4,1,128]{2,1,0:T(1,128)S(1)} %get-tuple-element.66) | copy-start | bytes 6148
  67.1 58.2 %copy-start.62 = (bf16[49,256,1]{1,0,2:T(8,128)(2,1)}, bf16[49,256,1]{1,0,2:T(8,128)(2,1)S(1)}, u32[]{:S(2)}) copy-start(bf16[49,256,1]{1,0,2:T(8,128)(2,1)S(1)} %reshape.358) | copy-start | bytes 75268
  67.3 68.8 %copy-start.41 = (bf16[256,49]{1,0:T(8,128)(2,1)}, bf16[256,49]{1,0:T(8,128)(2,1)S(1)}, u32[]{:S(2)}) copy-start(bf16[256,49]{1,0:T(8,128)(2,1)S(1)} %reshape.290) | copy-start | bytes 75268
  124.4 11.6 %copy-start.93 = (f32[1,256]{1,0:T(1,128)}, f32[1,256]{1,0:T(1,128)S(1)}, u32[]{:S(2)}) copy-start(f32[1,256]{1,0:T(1,128)S(1)} %slice_convert_fusion.16) | copy-start | bytes 3076
  125.2 10.8 %copy-start.83 = (f32[1,512]{1,0:T(1,128)}, f32[1,512]{1,0:T(1,128)S(1)}, u32[]{:S(2)}) copy-start(f32[1,512]{1,0:T(1,128)S(1)} %get-tuple-element.61) | copy-start | bytes 6148
  125.2 10.8 %copy-start.84 = (f32[1,512]{1,0:T(1,128)}, f32[1,512]{1,0:T(1,128)S(1)}, u32[]{:S(2)}) copy-start(f32[1,512]{1,0:T(1,128)S(1)} %get-tuple-element.62) | copy-start | bytes 6148
  125.2 16.0 %copy-start.71 = (f32[1,512]{1,0:T(1,128)}, f32[1,512]{1,0:T(1,128)S(1)}, u32[]{:S(2)}) copy-start(f32[1,512]{1,0:T(1,128)S(1)} %get-tuple-element.59) | copy-start | bytes 6148
  125.3 16.0 %copy-start.88 = (f32[1,512]{1,0:T(1,128)}, f32[1,512]{1,0:T(1,128)S(1)}, u32[]{:S(2)}) copy-start(f32[1,512]{1,0:T(1,128)S(1)} %get-tuple-element.60) | copy-start | bytes 6148
  139.6 12.2 %copy-start.10 = (bf16[32,49,512]{2,1,0:T(8,128)(2,1)}, bf16[32,49,512]{2,1,0:T(8,128)(2,1)S(1)}, u32[]{:S(2)}) copy-start(bf16[32,49,512]{2,1,0:T(8,128)(2,1)S(1)} %get-tuple-element.71) | copy-start | bytes 4816900
  139.6 12.2 %copy-start.37 = (f32[32,49]{1,0:T(8,128)}, f32[32,49]{1,0:T(8,128)S(1)}, u32[]{:S(2)}) copy-start(f32[32,49]{1,0:T(8,128)S(1)} %broadcast_multiply_fusion.3) | copy-start | bytes 18820
  140.5 11.3 %copy-start.47 = (f32[32,49]{1,0:T(8,128)}, f32[32,49]{1,0:T(8,128)S(1)}, u32[]{:S(2)}) copy-start(f32[32,49]{1,0:T(8,128)S(1)} %fusion.110) | copy-start | bytes 18820
  140.5 11.3 %copy-start.56 = (f32[32,49]{1,0:T(8,128)}, f32[32,49]{1,0:T(8,128)S(1)}, u32[]{:S(2)}) copy-start(f32[32,49]{1,0:T(8,128)S(1)} %fusion.184) | copy-start | bytes 18820
  141.3 10.5 %copy-start.75 = (f32[1,2048]{1,0:T(1,128)}, f32[1,2048]{1,0:T(1,128)S(1)}, u32[]{:S(2)}) copy-start(f32[1,2048]{1,0:T(1,128)S(1)} %slice_convert_fusion.1) | copy-start | bytes 24580
  141.3 10.5 %copy-start.27 = (bf16[2048,512,1]{1,0,2:T(8,128)(2,1)S(1)}, bf16[2048,512,1]{1,0,2:T(8,128)(2,1)}, u32[]{:S(2)}) copy-start(bf16[2048,512,1]{1,0,2:T(8,128)(2,1)} %reshape.361) | copy-start | bytes 6291460
  156.4 14.5 %copy-start.3 = (bf16[32,49,512]{2,1,0:T(8,128)(2,1)}, bf16[32,49,512]{2,1,0:T(8,128)(2,1)S(1)}, u32[]{:S(2)}) copy-start(bf16[32,49,512]{2,1,0:T(8,128)(2,1)S(1)} %get-tuple-element.75) | copy-start | bytes 4816900
  156.4 151.5 %copy-start.36 = (f32[32,49]{1,0:T(8,128)}, f32[32,49]{1,0:T(8,128)S(1)}, u32[]{:S(2)}) copy-start(f32[32,49]{1,0:T(8,128)S(1)} %broadcast_multiply_fusion.2) | copy-start | bytes 18820
  157.2 13.0 %copy-start.49 = (f32[32,49]{1,0:T(8,128)}, f32[32,49]{1,0:T(8,128)S(1)}, u32[]{:S(2)}) copy-start(f32[32,49]{1,0:T(8,128)S(1)} %fusion.113) | copy-start | bytes 18820
  157.2 150.7 %copy-start.55 = (f32[32,49]{1,0:T(8,128)}, f32[32,49]{1,0:T(8,128)S(1)}, u32[]{:S(2)}) copy-start(f32[32,49]{1,0:T(8,128)S(1)} %fusion.185) | copy-start | bytes 18820
  159.5 10.7 %copy-start.85 = (f32[1,512]{1,0:T(1,128)}, f32[1,512]{1,0:T(1,128)S(1)}, u32[]{:S(2)}) copy-start(f32[1,512]{1,0:T(1,128)S(1)} %get-tuple-element.56) | copy-start | bytes 6148
  159.5 73.1 %copy-start.86 = (f32[1,512]{1,0:T(1,128)}, f32[1,512]{1,0:T(1,128)S(1)}, u32[]{:S(2)}) copy-start(f32[1,512]{1,0:T(1,128)S(1)} %get-tuple-element.55) | copy-start | bytes 6148
  159.5 121.0 %copy-start.73 = (f32[1,512]{1,0:T(1,128)}, f32[1,512]{1,0:T(1,128)S(1)}, u32[]{:S(2)}) copy-start(f32[1,512]{1,0:T(1,128)S(1)} %get-tuple-element.54) | copy-start | bytes 6148
  159.5 148.4 %copy-start.68 = (f32[1,512]{1,0:T(1,128)}, f32[1,512]{1,0:T(1,128)S(1)}, u32[]{:S(2)}) copy-start(f32[1,512]{1,0:T(1,128)S(1)} %get-tuple-element.57) | copy-start | bytes 6148
  173.6 106.9 %copy-start.39 = (f32[32,49]{1,0:T(8,128)}, f32[32,49]{1,0:T(8,128)S(1)}, u32[]{:S(2)}) copy-start(f32[32,49]{1,0:T(8,128)S(1)} %broadcast_multiply_fusion.1) | copy-start | bytes 18820
  175.7 104.9 %copy-start.58 = (f32[32,49]{1,0:T(8,128)}, f32[32,49]{1,0:T(8,128)S(1)}, u32[]{:S(2)}) copy-start(f32[32,49]{1,0:T(8,128)S(1)} %fusion.186) | copy-start | bytes 18820
  232.6 12.1 %copy-start.7 = (bf16[32,49,512]{2,1,0:T(8,128)(2,1)S(1)}, bf16[32,49,512]{2,1,0:T(8,128)(2,1)}, u32[]{:S(2)}) copy-start(bf16[32,49,512]{2,1,0:T(8,128)(2,1)} %copy-done.5) | copy-start | bytes 4816900
  232.6 12.1 %copy-start.30 = (bf16[2048,512,1]{1,0,2:T(8,128)(2,1)S(1)}, bf16[2048,512,1]{1,0,2:T(8,128)(2,1)}, u32[]{:S(2)}) copy-start(bf16[2048,512,1]{1,0,2:T(8,128)(2,1)} %reshape.365) | copy-start | bytes 6291460
  256.4 94.7 %copy-start.45 = (f32[32,49]{1,0:T(8,128)}, f32[32,49]{1,0:T(8,128)S(1)}, u32[]{:S(2)}) copy-start(f32[32,49]{1,0:T(8,128)S(1)} %add_multiply_fusion.3) | copy-start | bytes 18820
  256.4 17.0 %copy-start.8 = (bf16[32,49,512]{2,1,0:T(8,128)(2,1)S(1)}, bf16[32,49,512]{2,1,0:T(8,128)(2,1)}, u32[]{:S(2)}) copy-start(bf16[32,49,512]{2,1,0:T(8,128)(2,1)} %copy-done.5) | copy-start | bytes 4816900
  256.4 17.0 %copy-start.29 = (bf16[512,2048,1]{1,0,2:T(8,128)(2,1)S(1)}, bf16[512,2048,1]{1,0,2:T(8,128)(2,1)}, u32[]{:S(2)}) copy-start(bf16[512,2048,1]{1,0,2:T(8,128)(2,1)} %reshape.364) | copy-start | bytes 6291460
  280.6 30.2 %slice-start.4 = ((s8[7340032]{0:T(1024)(128)(4,1)}), s8[3145728]{0:T(1024)(128)(4,1)S(1)}, s32[]{:S(2)}) async-start(s8[7340032]{0:T(1024)(128)(4,1)} %bitcast.185), calls=%async_computation.9 | async-start | bytes 6291456
  284.7 23.2 %copy-start.16 = (bf16[32,49,512]{2,1,0:T(8,128)(2,1)}, bf16[32,49,512]{2,1,0:T(8,128)(2,1)S(1)}, u32[]{:S(2)}) copy-start(bf16[32,49,512]{2,1,0:T(8,128)(2,1)S(1)} %get-tuple-element.53) | copy-start | bytes 4816900
  284.7 18.4 %copy-start.4 = (bf16[32,49,512]{2,1,0:T(8,128)(2,1)S(1)}, bf16[32,49,512]{2,1,0:T(8,128)(2,1)}, u32[]{:S(2)}) copy-start(bf16[32,49,512]{2,1,0:T(8,128)(2,1)} %copy-done.3) | copy-start | bytes 4816900
  284.7 26.0 %slice-start.5 = ((s8[7340032]{0:T(1024)(128)(4,1)}), s8[4194304]{0:T(1024)(128)(4,1)S(1)}, s32[]{:S(2)}) async-start(s8[7340032]{0:T(1024)(128)(4,1)} %bitcast.185), calls=%async_computation.10 | async-start | bytes 8388608
  317.3 17.3 %copy-start.11 = (bf16[32,49,512]{2,1,0:T(8,128)(2,1)S(1)}, bf16[32,49,512]{2,1,0:T(8,128)(2,1)}, u32[]{:S(2)}) copy-start(bf16[32,49,512]{2,1,0:T(8,128)(2,1)} %copy-done.10) | copy-start | bytes 4816900
  317.3 17.3 %copy-start.38 = (f32[32,49]{1,0:T(8,128)S(1)}, f32[32,49]{1,0:T(8,128)}, u32[]{:S(2)}) copy-start(f32[32,49]{1,0:T(8,128)} %copy-done.37) | copy-start | bytes 18820
  317.3 17.3 %copy-start.57 = (f32[32,49]{1,0:T(8,128)S(1)}, f32[32,49]{1,0:T(8,128)}, u32[]{:S(2)}) copy-start(f32[32,49]{1,0:T(8,128)} %copy-done.56) | copy-start | bytes 18820
  317.3 17.3 %copy-start.72 = (f32[1,512]{1,0:T(1,128)S(1)}, f32[1,512]{1,0:T(1,128)}, u32[]{:S(2)}) copy-start(f32[1,512]{1,0:T(1,128)} %copy-done.71) | copy-start | bytes 6148
  317.3 17.3 %copy-start.89 = (f32[1,512]{1,0:T(1,128)S(1)}, f32[1,512]{1,0:T(1,128)}, u32[]{:S(2)}) copy-start(f32[1,512]{1,0:T(1,128)} %copy-done.88) | copy-start | bytes 6148
  334.6 9.5 %copy-start.26 = (bf16[512,2048,1]{1,0,2:T(8,128)(2,1)S(1)}, bf16[512,2048,1]{1,0,2:T(8,128)(2,1)}, u32[]{:S(2)}) copy-start(bf16[512,2048,1]{1,0,2:T(8,128)(2,1)} %reshape.360) | copy-start | bytes 6291460
  334.6 9.5 %copy-start.102 = (bf16[32,49,2048]{2,1,0:T(8,128)(2,1)S(1)}, bf16[32,49,2048]{2,1,0:T(8,128)(2,1)}, u32[]{:S(2)}) copy-start(bf16[32,49,2048]{2,1,0:T(8,128)(2,1)} %get-tuple-element.98) | copy-start | bytes 19267588
  334.7 16.5 %slice-start.6 = ((s8[7340032]{0:T(1024)(128)(4,1)}), s8[4194304]{0:T(1024)(128)(4,1)S(1)}, s32[]{:S(2)}) async-start(s8[7340032]{0:T(1024)(128)(4,1)} %bitcast.187), calls=%async_computation.11 | async-start | bytes 8388608
  357.5 418.4 %all-reduce.7.cloned.1.call-start = ((), (), s32[]{:S(2)}) async-start(), calls=%async_computation.4 | async-start | bytes 34045952
  372.8 21.4 %copy-start.14 = (bf16[32,49,512]{2,0,1:T(8,128)(2,1)S(1)}, bf16[32,49,512]{2,0,1:T(8,128)(2,1)}, u32[]{:S(2)}) copy-start(bf16[32,49,512]{2,0,1:T(8,128)(2,1)} %param.11) | copy-start | bytes 4816900
  402.2 15.9 %slice-start.2 = ((s8[8388608]{0:T(1024)(128)(4,1)}), s8[4194304]{0:T(1024)(128)(4,1)S(1)}, s32[]{:S(2)}) async-start(s8[8388608]{0:T(1024)(128)(4,1)} %bitcast.141), calls=%async_computation.7 | async-start | bytes 8388608
  407.6 10.5 %slice-start.3 = ((s8[8388608]{0:T(1024)(128)(4,1)}), s8[4194304]{0:T(1024)(128)(4,1)S(1)}, s32[]{:S(2)}) async-start(s8[8388608]{0:T(1024)(128)(4,1)} %bitcast.141), calls=%async_computation.8 | async-start | bytes 8388608
  437.7 79.2 %copy-start.19 = (bf16[32,512,49]{1,2,0:T(8,128)(2,1)S(1)}, bf16[32,512,49]{1,2,0:T(8,128)(2,1)}, u32[]{:S(2)}) copy-start(bf16[32,512,49]{1,2,0:T(8,128)(2,1)} %copy-done.18) | copy-start | bytes 4816900
  437.7 79.5 %copy-start.44 = (f32[12544]{0:T(1024)S(1)}, f32[12544]{0:T(1024)}, u32[]{:S(2)}) copy-start(f32[12544]{0:T(1024)} %reshape.299) | copy-start | bytes 150532
  437.7 79.5 %copy-start.66 = (f32[2048]{0:T(1024)S(1)}, f32[2048]{0:T(1024)}, u32[]{:S(2)}) copy-start(f32[2048]{0:T(1024)} %get-tuple-element.90) | copy-start | bytes 24580
  437.8 79.5 %copy-start.77 = (f32[512]{0:T(512)S(1)}, f32[512]{0:T(512)}, u32[]{:S(2)}) copy-start(f32[512]{0:T(512)} %get-tuple-element.26) | copy-start | bytes 6148
  437.8 79.5 %copy-start.82 = (f32[49]{0:T(128)S(1)}, f32[49]{0:T(128)}, u32[]{:S(2)}) copy-start(f32[49]{0:T(128)} %get-tuple-element.27) | copy-start | bytes 592
  437.8 79.5 %copy-start.90 = (f32[512]{0:T(512)S(1)}, f32[512]{0:T(512)}, u32[]{:S(2)}) copy-start(f32[512]{0:T(512)} %get-tuple-element.22) | copy-start | bytes 6148
  437.8 79.5 %copy-start.91 = (f32[512]{0:T(512)S(1)}, f32[512]{0:T(512)}, u32[]{:S(2)}) copy-start(f32[512]{0:T(512)} %get-tuple-element.33) | copy-start | bytes 6148
  437.8 79.5 %copy-start.92 = (f32[512]{0:T(512)S(1)}, f32[512]{0:T(512)}, u32[]{:S(2)}) copy-start(f32[512]{0:T(512)} %get-tuple-element.21) | copy-start | bytes 6148
  437.8 79.5 %copy-start.95 = (f32[256]{0:T(256)S(1)}, f32[256]{0:T(256)}, u32[]{:S(2)}) copy-start(f32[256]{0:T(256)} %get-tuple-element.88) | copy-start | bytes 3076
  591.7 224.3 %copy-start.97 = (f32[128]{0:T(128)S(1)}, f32[128]{0:T(128)}, u32[]{:S(2)}) copy-start(f32[128]{0:T(128)} %param.15) | copy-start | bytes 1540
  591.7 224.3 %copy-start.98 = (f32[128]{0:T(128)S(1)}, f32[128]{0:T(128)}, u32[]{:S(2)}) copy-start(f32[128]{0:T(128)} %param.18) | copy-start | bytes 1540
  591.7 224.3 %copy-start.99 = (f32[128]{0:T(128)S(1)}, f32[128]{0:T(128)}, u32[]{:S(2)}) copy-start(f32[128]{0:T(128)} %param.21) | copy-start | bytes 1540
  591.7 225.0 %copy-start.21 = (f32[2,132992]{1,0:T(2,128)S(1)}, f32[2,132992]{1,0:T(2,128)}, u32[]{:S(2)}) copy-start(f32[2,132992]{1,0:T(2,128)} %param.13) | copy-start | bytes 3191812
  (53 other events, 247.1 us)
Sparse Core Ops, SparseCore 0:
  10.8 55.0 all-gather.5
  68.7 49.0 all-gather.7
  357.6 57.5 reduce-scatter.1
  591.8 183.9 all-reduce.6
where the time goes:
time: 846 us; the launch traced here: 832 us
  local copies, waits for them, and re-layouts  298 us (35%)
  matrix products  207 us (24%)
  waiting for transfers between devices  170 us (20%)
  blocking collectives  94.5 us (11%)
  other arithmetic  43.1 us (5%)
  between operations  20 us (2%)
    concatenate x2, local copies, waits for them, and re-layouts, layer_backward(): jnp.concatenate([g_w_tok1.reshape(-1), g_w_tok2.reshape(-1), g_w_ch1.resh...  153 us
    unnamed x5, waiting for transfers between devices  148 us
    slice x8, local copies, waits for them, and re-layouts, unpack_layer(): pieces.append(flat[piece_start:piece_start + piece_len].reshape(shape_one))  106 us
    dot_general x2, matrix products, layer_backward(): jnp.einsum('bsc,js->bcj', d_after_bf, w_tok2, preferred_element_type=jnp....  38.1 us
    dot_general x2, matrix products, layer_backward(): jnp.einsum('bsc,dc->bsd', d_out_bf, w_ch2, preferred_element_type=jnp.flo...  34.3 us
    unnamed x1, blocking collectives  32.6 us
    psum x1, blocking collectives, device_step(): loss_value = lax.psum(loss_sum, 'fsdp') / global_b  31.4 us
    dot_general x2, matrix products, layer_forward(): jnp.einsum('bsc,cd->bsd', normed2, w_ch1, preferred_element_type=jnp.floa...  22.6 us
  transfers between devices with their start and end apart: 4, of which 2 were waited for; matrix products, arithmetic and copies ran while one was open for 40% of the time, Pallas kernels for 0%

commit v1 on v0

--- a/solution.py
+++ b/solution.py
@@ -1,8 +1,360 @@
+import functools
 import math
 import jax
 import jax.numpy as jnp
 from jax import lax
+from jax.experimental import pallas as pl
+from jax.experimental.pallas import tpu as pltpu
 from jax.sharding import PartitionSpec as P
+
+MESH_ID = pl.DeviceIdType.MESH
+F32 = jnp.float32
+BF16 = jnp.bfloat16
+VMEM_CAP = 64 * 1024 * 1024 - 128 * 1024
+
+SHARD_ROWS = 1039
+SLOT_ROWS = 1040
+ROW_C1 = 196
+ROW_C2 = 8388
+ROW_VEC = 16580
+FLAT_ROWS = 16624
+SLAB_ROWS = 240
+HEAD_OFF = 2 * SLOT_ROWS
+SMALL_OFF = HEAD_OFF + 256
+AG_ROWS = SMALL_OFF + 16
+RS_ROWS = SMALL_OFF + 8
+ORDERS = ((2, 1, 0), (1, 0, 2), (0, 2, 1))
+AXIS_STEP = (8, 4, 2)
+
+
+def place():
+    me = lax.axis_index('fsdp')
+    coords = [me // 8, (me // 4) % 2, (me // 2) % 2]
+    core = me % 2
+    neighbours = [me + AXIS_STEP[a] - 2 * AXIS_STEP[a] * coords[a] for a in range(3)]
+    partner = me + 1 - 2 * core
+    return me, coords, core, neighbours, partner
+
+
+def enter_barrier(neighbours, partner):
+    barrier = pltpu.get_barrier_semaphore()
+    for other in list(neighbours) + [partner]:
+        pl.semaphore_signal(barrier, inc=1, device_id=(other,), device_id_type=MESH_ID)
+    pl.semaphore_wait(barrier, 4)
+
+
+def slot_view(buf, coords, core, free_axes, row0, rows):
+    index = [pl.ds(0, 2) if a in free_axes else coords[a] for a in range(3)]
+    return buf.at[index[0], index[1], index[2], core, pl.ds(row0, rows), :]
+
+
+class Gather:
+    def __init__(self, buf, where, row_groups, send_sem, recv_sem, sem0):
+        self.buf, self.where, self.groups = buf, where, row_groups
+        self.send_sem, self.recv_sem, self.sem0 = send_sem, recv_sem, sem0
+        self.pending = []
+
+    def copy(self, view, sem, device):
+        return pltpu.make_async_remote_copy(src_ref=view, dst_ref=view, send_sem=self.send_sem.at[self.sem0 + sem], recv_sem=self.recv_sem.at[self.sem0 + sem], device_id=(device,), device_id_type=MESH_ID)
+
+    def link(self, group, phase):
+        me, coords, core, neighbours, partner = self.where
+        order = ORDERS[group]
+        row0, rows = self.groups[group]
+        view = slot_view(self.buf, coords, core, order[:phase], row0, rows)
+        return self.copy(view, group * 3 + phase, neighbours[order[phase]])
+
+    def chip(self, group, phase):
+        me, coords, core, neighbours, partner = self.where
+        order = ORDERS[group]
+        row0, rows = self.groups[group]
+        if phase < 0:
+            view = slot_view(self.buf, coords, core, (), row0, rows)
+        else:
+            far = list(coords)
+            far[order[phase]] = 1 - coords[order[phase]]
+            view = slot_view(self.buf, far, core, order[:phase], row0, rows)
+        return self.copy(view, 9 + group * 4 + phase + 1, partner)
+
+    def start(self):
+        for group in range(3):
+            self.link(group, 0).start()
+        for group in range(3):
+            self.chip(group, -1).start()
+
+    def step(self, phase):
+        for group in range(3):
+            self.link(group, phase).wait_recv()
+            if phase < 2:
+                self.link(group, phase + 1).start()
+            self.chip(group, phase).start()
+
+    def finish(self):
+        for group in range(3):
+            for phase in range(-1, 3):
+                self.chip(group, phase).wait()
+            for phase in range(3):
+                self.link(group, phase).wait_send()
+
+
+def unflatten_layer(gath, layer, flat, w1_ref, w2_ref, slab_ref):
+    base = layer * SLOT_ROWS
+
+    def spread(dev, carry):
+        z, y, x, core = dev // 8, (dev // 4) % 2, (dev // 2) % 2, dev % 2
+
+        def chunk(k, inner):
+            block = gath[z, y, x, core, pl.ds(base + 16 * k, 16), :]
+            flat[pl.ds(dev * SHARD_ROWS + 16 * k, 16), :] = block.astype(F32)
+            return inner
+        return lax.fori_loop(0, SLOT_ROWS // 16, chunk, carry, unroll=5)
+    lax.fori_loop(0, 16, spread, 0)
+
+    def first(rb, carry):
+        for j in range(16):
+            block = flat[pl.ds(ROW_C1 + 256 * rb + j, 16, stride=16), :]
+            w1_ref[layer, pl.ds(pl.multiple_of(16 * rb, 16), 16), 128 * j:128 * j + 128] = block.astype(BF16)
+        return carry
+    lax.fori_loop(0, 32, first, 0)
+
+    def second(rb, carry):
+        for j in range(4):
+            block = flat[pl.ds(ROW_C2 + 64 * rb + j, 16, stride=4), :]
+            w2_ref[layer, pl.ds(pl.multiple_of(16 * rb, 16), 16), 128 * j:128 * j + 128] = block.astype(BF16)
+        return carry
+    lax.fori_loop(0, 128, second, 0)
+    slab_ref[layer, 0:196, :] = flat[0:196, :]
+    slab_ref[layer, 196:240, :] = flat[ROW_VEC:FLAT_ROWS, :]
+
+
+def gather_kernel(pack_ref, w1_ref, w2_ref, slab_ref, head_ref, small_ref, gath, flat, send_sem, recv_sem, load_sem):
+    where = place()
+    me, coords, core, neighbours, partner = where
+    load = pltpu.make_async_copy(pack_ref, gath.at[coords[0], coords[1], coords[2], core], load_sem)
+    load.start()
+    enter_barrier(neighbours, partner)
+    load.wait()
+    third = AG_ROWS // 3
+    work = Gather(gath, where, [(third * g, third) for g in range(3)], send_sem, recv_sem, 0)
+    work.start()
+    for phase in range(3):
+        work.step(phase)
+    work.finish()
+    for layer in range(2):
+        unflatten_layer(gath, layer, flat, w1_ref, w2_ref, slab_ref)
+
+    def spread_head(dev, carry):
+        z, y, x, own = dev // 8, (dev // 4) % 2, (dev // 2) % 2, dev % 2
+        for j in range(8):
+            head_ref[pl.ds(pl.multiple_of(32 * dev, 32), 32), 128 * j:128 * j + 128] = gath[z, y, x, own, pl.ds(HEAD_OFF + 32 * j, 32), :]
+        small_ref[pl.ds(dev, 1), :] = gath[z, y, x, own, pl.ds(SMALL_OFF, 16), :].astype(F32)[0:1, :]
+        return carry
+    lax.fori_loop(0, 16, spread_head, 0)
+
+
+def gather_weights(pack):
+    vmem = pl.BlockSpec(memory_space=pltpu.VMEM)
+    return pl.pallas_call(
+        gather_kernel,
+        out_shape=(jax.ShapeDtypeStruct((2, 512, 2048), BF16), jax.ShapeDtypeStruct((2, 2048, 512), BF16), jax.ShapeDtypeStruct((2, SLAB_ROWS, 128), F32), jax.ShapeDtypeStruct((512, 1024), BF16), jax.ShapeDtypeStruct((16, 128), F32)),
+        in_specs=[vmem],
+        out_specs=(vmem,) * 5,
+        scratch_shapes=[
+            pltpu.VMEM((2, 2, 2, 2, AG_ROWS, 128), BF16),
+            pltpu.VMEM((16640, 128), F32),
+            pltpu.SemaphoreType.DMA((21,)),
+            pltpu.SemaphoreType.DMA((21,)),
+            pltpu.SemaphoreType.DMA,
+        ],
+        compiler_params=pltpu.CompilerParams(collective_id=0, has_side_effects=True, vmem_limit_bytes=VMEM_CAP),
+        name='gather_weights',
+    )(pack)
+
+
+class Reduce:
+    def __init__(self, buf, temps, where, row_groups, send_sem, recv_sem, sem0):
+        self.buf, self.temps, self.where, self.groups = buf, temps, where, row_groups
+        self.send_sem, self.recv_sem, self.sem0 = send_sem, recv_sem, sem0
+
+    def views(self, group, phase):
+        me, coords, core, neighbours, partner = self.where
+        row0, rows = self.groups[group]
+        order = ORDERS[group]
+        if phase == 0:
+            free = (0, 1, 2)
+            leave = slot_view(self.buf, coords, 1 - core, free, row0, rows)
+            device = partner
+            stay = coords
+        else:
+            axis = order[phase - 1]
+            free = tuple(a for a in range(3) if a in order[phase:])
+            far = list(coords)
+            far[axis] = 1 - coords[axis]
+            leave = slot_view(self.buf, far, core, free, row0, rows)
+            device = neighbours[axis]
+            stay = coords
+        land = self.temps[phase].at[(slice(None),) * len(free) + (pl.ds(row0, rows), slice(None))]
+        return leave, land, device, free, stay
+
+    def copy(self, group, phase):
+        leave, land, device, free, stay = self.views(group, phase)
+        sem = self.sem0 + group * 4 + phase
+        return pltpu.make_async_remote_copy(src_ref=leave, dst_ref=land, send_sem=self.send_sem.at[sem], recv_sem=self.recv_sem.at[sem], device_id=(device,), device_id_type=MESH_ID)
+
+    def add(self, group, phase):
+        me, coords, core, neighbours, partner = self.where
+        leave, land, device, free, stay = self.views(group, phase)
+        row0, rows = self.groups[group]
+        temp = self.temps[phase]
+        count = 2 ** len(free)
+        per = max(1, 8 // count)
+        while rows % (8 * per):
+            per //= 2
+
+        def chunk(k, carry):
+            for part in range(per):
+                start = pl.multiple_of(row0 + 8 * (per * k + part), 8)
+                for n in range(count):
+                    index = list(coords)
+                    bits = []
+                    for pos, a in enumerate(free):
+                        bit = (n // 2 ** (len(free) - 1 - pos)) % 2
+                        index[a] = bit
+                        bits.append(bit)
+                    target = (index[0], index[1], index[2], core, pl.ds(start, 8), slice(None))
+                    self.buf[target] = self.buf[target] + temp[tuple(bits) + (pl.ds(start, 8), slice(None))]
+            return carry
+        lax.fori_loop(0, rows // (8 * per), chunk, 0)
+
+    def start(self):
+        for group in range(3):
+            self.copy(group, 0).start()
+
+    def step(self, phase):
+        for group in range(3):
+            self.copy(group, phase).wait_recv()
+            self.add(group, phase)
+            if phase < 3:
+                self.copy(group, phase + 1).start()
+
+    def finish(self):
+        for group in range(3):
+            for phase in range(4):
+                self.copy(group, phase).wait_send()
+
+
+def flatten_layer(layer, flat, w1_ref, w2_ref, slab_ref, grad):
+    base = layer * SLOT_ROWS
+
+    def first(rb, carry):
+        for j in range(16):
+            flat[pl.ds(ROW_C1 + 128 * rb + j, 8, stride=16), :] = w1_ref[pl.ds(pl.multiple_of(8 * rb, 8), 8), 128 * j:128 * j + 128]
+        return carry
+    lax.fori_loop(0, 64, first, 0)
+
+    def second(rb, carry):
+        for j in range(4):
+            flat[pl.ds(ROW_C2 + 32 * rb + j, 8, stride=4), :] = w2_ref[pl.ds(pl.multiple_of(8 * rb, 8), 8), 128 * j:128 * j + 128]
+        return carry
+    lax.fori_loop(0, 256, second, 0, unroll=2)
+    flat[0:196, :] = slab_ref[layer, 0:196, :]
+    flat[ROW_VEC:FLAT_ROWS, :] = slab_ref[layer, 196:240, :]
+
+    def spread(dev, carry):
+        z, y, x, core = dev // 8, (dev // 4) % 2, (dev // 2) % 2, dev % 2
+
+        def chunk(k, inner):
+            grad[z, y, x, core, pl.ds(pl.multiple_of(base + 8 * k, 8), 8), :] = flat[pl.ds(dev * SHARD_ROWS + 8 * k, 8), :]
+            return inner
+        return lax.fori_loop(0, SLOT_ROWS // 8, chunk, carry, unroll=10)
+    lax.fori_loop(0, 16, spread, 0)
+
+
+def square_sum(ref, coords, core, row0, rows):
+    def chunk(k, total):
+        block = ref[coords[0], coords[1], coords[2], core, pl.ds(pl.multiple_of(row0 + 8 * k, 8), 8), :]
+        return total + block * block
+    return lax.fori_loop(0, rows // 8, chunk, jnp.zeros((8, 128), F32), unroll=2)
+
+
+def reduce_kernel(gw1_hbm, gw2_hbm, slab_ref, gh_ref, gs_ref, loss_ref, gl_ref, ghead_ref, gsmall_ref, stat_ref, stage1, stage2, flat, grad, t0, t1, t2, t3, msg, box, send_sem, recv_sem, load_sem, tiny_send, tiny_recv):
+    where = place()
+    me, coords, core, neighbours, partner = where
+    enter_barrier(neighbours, partner)
+    flat[FLAT_ROWS:16640, :] = jnp.zeros((16, 128), F32)
+
+    def load(layer):
+        return pltpu.make_async_copy(gw1_hbm.at[layer], stage1, load_sem.at[0]), pltpu.make_async_copy(gw2_hbm.at[layer], stage2, load_sem.at[1])
+    for layer in (1, 0):
+        for item in load(layer):
+            item.start()
+        for item in load(layer):
+            item.wait()
+        flatten_layer(layer, flat, stage1, stage2, slab_ref, grad)
+
+    def spread_head(dev, carry):
+        z, y, x, own = dev // 8, (dev // 4) % 2, (dev // 2) % 2, dev % 2
+        for j in range(8):
+            grad[z, y, x, own, HEAD_OFF + 32 * j:HEAD_OFF + 32 * j + 32, :] = gh_ref[pl.ds(pl.multiple_of(32 * dev, 32), 32), 128 * j:128 * j + 128]
+        grad[z, y, x, own, SMALL_OFF:AG_ROWS, :] = jnp.zeros((16, 128), F32)
+        grad[z, y, x, own, SMALL_OFF:SMALL_OFF + 1, :] = gs_ref[pl.ds(dev, 1), :]
+        grad[z, y, x, own, SMALL_OFF + 8:SMALL_OFF + 16, :] = loss_ref[...]
+        return carry
+    lax.fori_loop(0, 16, spread_head, 0)
+    third = AG_ROWS // 3
+    work = Reduce(grad, (t0, t1, t2, t3), where, [(third * g, third) for g in range(3)], send_sem, recv_sem, 0)
+    work.start()
+    for phase in range(4):
+        work.step(phase)
+    work.finish()
+    own = (coords[0], coords[1], coords[2], core)
+    for layer in range(2):
+        last = layer * SLOT_ROWS + SHARD_ROWS
+        grad[own + (pl.ds(last, 1), slice(None))] = jnp.zeros((1, 128), F32)
+    total = square_sum(grad, coords, core, 0, SMALL_OFF + 8)
+    msg[0] = jnp.broadcast_to(jnp.sum(total), (8, 128))
+    for n, device in enumerate([partner, neighbours[2], neighbours[1], neighbours[0]]):
+        copy = pltpu.make_async_remote_copy(src_ref=msg.at[n], dst_ref=box.at[n], send_sem=tiny_send.at[n], recv_sem=tiny_recv.at[n], device_id=(device,), device_id_type=MESH_ID)
+        copy.start()
+        copy.wait()
+        msg[n + 1] = msg[n] + box[n]
+    stat_ref[0] = msg[4]
+    stat_ref[1] = grad[own + (pl.ds(SMALL_OFF + 8, 8), slice(None))]
+    for layer in range(2):
+        gl_ref[layer] = grad[own + (pl.ds(layer * SLOT_ROWS, SLOT_ROWS), slice(None))]
+    ghead_ref[...] = grad[own + (pl.ds(HEAD_OFF, 256), slice(None))]
+    gsmall_ref[...] = grad[own + (pl.ds(SMALL_OFF, 8), slice(None))]
+
+
+def reduce_grads(gw1, gw2, slab, gh, gs, loss):
+    vmem = pl.BlockSpec(memory_space=pltpu.VMEM)
+    hbm = pl.BlockSpec(memory_space=pl.ANY)
+    return pl.pallas_call(
+        reduce_kernel,
+        out_shape=(jax.ShapeDtypeStruct((2, SLOT_ROWS, 128), F32), jax.ShapeDtypeStruct((256, 128), F32), jax.ShapeDtypeStruct((8, 128), F32), jax.ShapeDtypeStruct((2, 8, 128), F32)),
+        in_specs=[hbm, hbm, vmem, vmem, vmem, vmem],
+        out_specs=(vmem,) * 4,
+        scratch_shapes=[
+            pltpu.VMEM((512, 2048), F32),
+            pltpu.VMEM((2048, 512), F32),
+            pltpu.VMEM((16640, 128), F32),
+            pltpu.VMEM((2, 2, 2, 2, AG_ROWS, 128), F32),
+            pltpu.VMEM((2, 2, 2, AG_ROWS, 128), F32),
+            pltpu.VMEM((2, 2, AG_ROWS, 128), F32),
+            pltpu.VMEM((2, AG_ROWS, 128), F32),
+            pltpu.VMEM((AG_ROWS, 128), F32),
+            pltpu.VMEM((5, 8, 128), F32),
+            pltpu.VMEM((4, 8, 128), F32),
+            pltpu.SemaphoreType.DMA((12,)),
+            pltpu.SemaphoreType.DMA((12,)),
+            pltpu.SemaphoreType.DMA((2,)),
+            pltpu.SemaphoreType.DMA((4,)),
+            pltpu.SemaphoreType.DMA((4,)),
+        ],
+        compiler_params=pltpu.CompilerParams(collective_id=1, has_side_effects=True, vmem_limit_bytes=VMEM_CAP),
+        name='reduce_grads',
+    )(gw1, gw2, slab, gh, gs, loss)
+
 
 LN_EPS = 1e-6
 LEARN_RATE = 0.003
@@ -23,12 +375,17 @@
     return sum(math.prod(shape_one) for shape_one in piece_shapes(num_tokens, num_chans))
 
 
-def unpack_layer(flat, num_tokens, num_chans):
-    pieces = []
+def unpack_layer(parts, num_tokens, num_chans):
+    w_ch1, w_ch2, slab = parts
+    shapes = piece_shapes(num_tokens, num_chans)
+    w_tok1 = slab[0:98].reshape(shapes[0]).astype(BF16)
+    w_tok2 = slab[98:196].reshape(shapes[1]).astype(BF16)
+    tail = slab[196:].reshape(-1)
+    pieces = [w_tok1, w_tok2, w_ch1, w_ch2]
     piece_start = 0
-    for shape_one in piece_shapes(num_tokens, num_chans):
+    for shape_one in shapes[4:]:
         piece_len = math.prod(shape_one)
-        pieces.append(flat[piece_start:piece_start + piece_len].reshape(shape_one))
+        pieces.append(tail[piece_start:piece_start + piece_len])
         piece_start = piece_start + piece_len
     return pieces
 
@@ -96,9 +453,9 @@
     d_normed = jnp.einsum('bcj,sj->bsc', d_hid_tok_bf, w_tok1, preferred_element_type=jnp.float32)
     d_in_ln, g_ln1_g, g_ln1_b = norm_grad(x_in, ln1_g, ln1_b, d_normed)
     d_in = d_in_ln + d_after
-    pad_len = flat.shape[0] - layer_length(num_tokens, num_chans)
-    flat_grad = jnp.concatenate([g_w_tok1.reshape(-1), g_w_tok2.reshape(-1), g_w_ch1.reshape(-1), g_w_ch2.reshape(-1), g_ln1_g, g_ln1_b, g_b_tok1, g_b_tok2, g_ln2_g, g_ln2_b, g_b_ch1, g_b_ch2, jnp.zeros((pad_len,), jnp.float32)])
-    return d_in, flat_grad
+    tail = jnp.concatenate([g_ln1_g, g_ln1_b, g_b_tok1, g_b_tok2, g_ln2_g, g_ln2_b, g_b_ch1, g_b_ch2, jnp.zeros((719,), jnp.float32)])
+    slab = jnp.concatenate([g_w_tok1.reshape(98, 128), g_w_tok2.reshape(98, 128), tail.reshape(44, 128)])
+    return d_in, (g_w_ch1, g_w_ch2, slab)
 
 
 def head_step(hidden, labels, small_full, head_full, global_b):
@@ -149,26 +506,25 @@
         mat_len = 2 * num_tokens * (num_chans // 2) + 8 * num_chans * num_chans
         caches = []
         hidden = act_in
+        layer_bf = jnp.pad(layer_p.astype(BF16).reshape(2, SHARD_ROWS, 128), ((0, 0), (0, 1), (0, 0)))
+        head_bf = jnp.pad(head_w.astype(BF16), ((0, 0), (0, 24))).reshape(32, 8, 128).transpose(1, 0, 2).reshape(256, 128)
+        small_bf = jnp.pad(small_p.astype(BF16).reshape(1, 128), ((0, 15), (0, 0)))
+        w1_all, w2_all, slab_all, head_all, small_all = gather_weights(jnp.concatenate([layer_bf.reshape(2 * SLOT_ROWS, 128), head_bf, small_bf]))
         for layer_idx in range(num_layers):
-            flat_full = lax.all_gather(layer_p[layer_idx].astype(jnp.bfloat16), 'fsdp', tiled=True)
-            hidden, cache = layer_forward(hidden, flat_full, num_tokens, num_chans)
+            hidden, cache = layer_forward(hidden, (w1_all[layer_idx], w2_all[layer_idx], slab_all[layer_idx]), num_tokens, num_chans)
             caches.append(cache)
-        small_full = lax.all_gather(small_p.astype(jnp.bfloat16), 'fsdp', tiled=True)
-        head_full = lax.all_gather(head_w.astype(jnp.bfloat16), 'fsdp', tiled=True)
-        loss_sum, d_hidden, g_head_w, g_small = head_step(hidden, labels, small_full, head_full, global_b)
-        layer_shards = [None] * num_layers
+        loss_sum, d_hidden, g_head_w, g_small = head_step(hidden, labels, small_all.reshape(-1), head_all[:, :head_w.shape[1]], global_b)
+        grads = [None] * num_layers
         for layer_idx in reversed(range(num_layers)):
-            flat_full = lax.all_gather(layer_p[layer_idx].astype(jnp.bfloat16), 'fsdp', tiled=True)
-            d_hidden, flat_grad = layer_backward(d_hidden, flat_full, caches[layer_idx], num_tokens, num_chans)
-            layer_shards[layer_idx] = lax.psum_scatter(flat_grad, 'fsdp', scatter_dimension=0, tiled=True)
-        layer_g = jnp.stack(layer_shards)
-        head_g = lax.psum_scatter(g_head_w, 'fsdp', scatter_dimension=0, tiled=True)
-        small_flat = jnp.concatenate([g_small, jnp.zeros((small_full.shape[0] - g_small.shape[0],), jnp.float32)])
-        small_g = lax.psum_scatter(small_flat, 'fsdp', scatter_dimension=0, tiled=True)
-        loss_value = lax.psum(loss_sum, 'fsdp') / global_b
-        sq_local = jnp.sum(jnp.square(layer_g)) + jnp.sum(jnp.square(head_g)) + jnp.sum(jnp.square(small_g))
-        grad_norm = jnp.sqrt(lax.psum(sq_local, 'fsdp'))
-        clip_scale = 1.0 / jnp.maximum(1.0, grad_norm)
+            d_hidden, grads[layer_idx] = layer_backward(d_hidden, (w1_all[layer_idx], w2_all[layer_idx], slab_all[layer_idx]), caches[layer_idx], num_tokens, num_chans)
+        gl, ghead, gsmall, stat = reduce_grads(
+            jnp.stack([grads[0][0], grads[1][0]]), jnp.stack([grads[0][1], grads[1][1]]), jnp.stack([grads[0][2], grads[1][2]]),
+            jnp.pad(g_head_w, ((0, 0), (0, 24))), jnp.pad(g_small, (0, 24)).reshape(16, 128), jnp.broadcast_to(loss_sum, (8, 128)))
+        layer_g = gl[:, :SHARD_ROWS].reshape(2, SHARD_ROWS * 128)
+        head_g = ghead.reshape(8, 32, 128).transpose(1, 0, 2).reshape(32, 1024)[:, :head_w.shape[1]]
+        small_g = gsmall[0]
+        loss_value = stat[1, 0, 0] / global_b
+        clip_scale = 1.0 / jnp.maximum(1.0, jnp.sqrt(stat[0, 0, 0]))
         shard_len = layer_p.shape[1]
         flat_pos = lax.axis_index('fsdp') * shard_len + jnp.arange(shard_len)
         layer_decay = jnp.where(flat_pos < mat_len, WEIGHT_DECAY, 0.0)[None, :]

time: 846 us -> 467 us (0.55)
  local copies, waits for them, and re-layouts: 298 us -> 9.71 us
  Pallas kernels: 0 us -> 173 us
  waiting for transfers between devices: 170 us -> 0 us
  blocking collectives: 94.5 us -> 0 us
  between operations: 20 us -> 4.91 us
  matrix products: 207 us -> 218 us
  other arithmetic: 43.1 us -> 52.7 us
    pallas_call x0 -> x2, Pallas kernels: none -> 173 us  [the longest x1 112 us: reduce_grads(): pl.pallas_call(reduce_kernel, out_shape=(jax.ShapeDtypeStruct((2, SLOT_RO...]
    concatenate x3 -> x2, local copies, waits for them, and re-layouts: 153 us -> 0.16 us  [layer_backward(): jnp.concatenate([g_ln1_g, g_ln1_b, g_b_tok1, g_b_tok2, g_ln2_g, g_ln2_b,...]
    unnamed x5 -> x0, waiting for transfers between devices: 148 us -> none
    slice x9 -> x8, local copies, waits for them, and re-layouts: 107 us -> 1.45 us  [the longest x1 1.2 us: device_step(): clip_scale = 1.0 / jnp.maximum(1.0, jnp.sqrt(stat[0, 0, 0]))]
    unnamed x1 -> x0, blocking collectives: 32.6 us -> none
    psum x1 -> x0, blocking collectives: 31.4 us -> none  [device_step(): loss_value = lax.psum(loss_sum, 'fsdp') / global_b]
    all_gather x2 -> x0, blocking collectives: 30.4 us -> none  [the longest x1 16 us: device_step(): head_full = lax.all_gather(head_w.astype(jnp.bfloat16), 'fsdp', tiled=True)]
    unnamed x232 -> x134, local copies, waits for them, and re-layouts: 22 us -> 0.33 us
  transfers between devices with their start and end apart: 4 -> 0, of which waited for: 2 -> 0; matrix products, arithmetic and copies ran while one was open for 40% -> 0% of each run, Pallas kernels for 0% -> 0%
where the time goes in v1:
time: 467 us; the launch traced here: 458 us
  matrix products  218 us (47%)
  Pallas kernels  173 us (37%)
  other arithmetic  52.7 us (11%)
  local copies, waits for them, and re-layouts  9.71 us (2%)
  between operations  4.91 us (1%)
    pallas_call x1, Pallas kernels, reduce_grads(): pl.pallas_call(reduce_kernel, out_shape=(jax.ShapeDtypeStruct((2, SLOT_RO...  112 us
    pallas_call x1, Pallas kernels, gather_weights(): pl.pallas_call(gather_kernel, out_shape=(jax.ShapeDtypeStruct((2, 512, 20...  60.7 us
    dot_general x2, matrix products, layer_backward(): jnp.einsum('bsc,js->bcj', d_after_bf, w_tok2, preferred_element_type=jnp....  35.7 us
    dot_general x2, matrix products, layer_backward(): jnp.einsum('bsc,dc->bsd', d_out_bf, w_ch2, preferred_element_type=jnp.flo...  33.6 us
    dot_general x2, matrix products, layer_forward(): jnp.einsum('bsc,sj->bcj', normed, w_tok1, preferred_element_type=jnp.floa...  23 us
    dot_general x2, matrix products, layer_forward(): jnp.einsum('bsc,cd->bsd', normed2, w_ch1, preferred_element_type=jnp.floa...  22.2 us
    dot_general x2, matrix products, layer_backward(): jnp.einsum('bcj,bsc->js', act_tok, d_after_bf, preferred_element_type=jnp...  14.8 us
    dot_general x2, matrix products, layer_backward(): jnp.einsum('bsd,cd->bsc', d_hid_ch_bf, w_ch1, preferred_element_type=jnp....  14.5 us

profile of v1, /device:TPU:0, one launch (start us, length us, event | category | flops | bytes accessed | tf_op | source)
XLA Modules:
  0.0 458.0 jit_solution(1552842706197704087)
XLA Ops:
  0.6 0.7 convert_bitcast_fusion.2
  1.3 0.9 convert_element_type.226
  2.2 1.5 convert_element_type.225
  3.7 0.9 reshape.313
  4.7 0.9 fusion.206.pack_ref
  5.5 60.7 %gather_weights.1 = (bf16[2,512,2048]{2,1,0:T(8,128)(2,1)}, bf16[2,2048,512]{2,1,0:T(8,128)(2,1)}, f32[2,240,128]{2,1,0:T(8,128)}, bf16[512,1024]{1,0:T(8,128)(2,1)}, f32[16,128]{1,0:T(8,128)}) custom-call(bf16[2352,128]{1,0:T(8,128)(2,1)} %fusion.206.pack_ref), custom_call_target="tpu_custom_call" | custom-call | tf_op jit(solution)/shard_map/gather_weights/pallas_call | solution.py:157
  66.3 0.9 slice_bitcast_fusion
  67.2 0.7 slice_bitcast_fusion.8
  67.9 1.0 convert.6
  69.1 0.7 slice_bitcast_fusion.5
  69.9 2.6 convert_reduce_fusion.5
  72.4 2.8 fusion.103
  75.3 11.5 %multiply_convert_fusion.1 = (bf16[32,512,256]{2,1,0:T(8,128)(2,1)}, f32[32,512,256]{2,1,0:T(8,128)}) fusion(f32[256]{0:T(256)S(1)} %get-tuple-element.63, bf16[49,256,1]{1,0,2:T(8,128)(2,1)S(1)} %reshape.330, f32[512]{0:T(512)S(1)} %get-tuple-element.66, f32[512]{0:T(512)S(1)} %get-tuple-element.67, f32[32,49]{1,0:T(8,128)S(1)} %add_rsqrt_fusion, ...), kind=kOutput, calls=%fused_computation.35 | convolution fusion | flops 457801728 | bytes 26814208 | tf_op jit(solution)/shard_map/bsc,sj->bcj/dot_general | solution.py:419
  87.1 7.1 %convert_reduce_fusion.4 = (f32[32,49]{1,0:T(8,128)S(1)}, bf16[32,49,512]{2,1,0:T(8,128)(2,1)S(1)}) fusion(f32[49]{0:T(128)S(1)} %slice.189, bf16[32,512,256]{2,1,0:T(8,128)(2,1)} %get-tuple-element.82, bf16[256,49]{1,0:T(8,128)(2,1)S(1)} %convert_element_type.228, bf16[32,49,512]{2,0,1:T(8,128)(2,1)S(1)} %copy-done.2), kind=kOutput, calls=%fused_computation.80 | convolution fusion | flops 415857120 | bytes 11631428 | tf_op jit(solution)/shard_map/bcj,js->bsc/dot_general | solution.py:421
  94.2 0.9 fusion.110
  95.2 10.7 %multiply_convert_fusion.3 = (bf16[32,49,2048]{2,1,0:T(8,128)(2,1)S(1)}, f32[32,49,2048]{2,1,0:T(8,128)}) fusion(f32[2048]{0:T(1024)S(1)} %slice.193, bf16[2,512,2048]{2,1,0:T(8,128)(2,1)S(1)} %copy-done.62, bf16[32,49,512]{2,1,0:T(8,128)(2,1)S(1)} %get-tuple-element.85, f32[512]{0:T(512)S(1)} %get-tuple-element.113, f32[512]{0:T(512)S(1)} %get-tuple-element.115, ...), kind=kOutput, calls=%fused_computation.55 | convolution fusion | flops 3325263872 | bytes 23244800 | tf_op jit(solution)/shard_map/bsc,cd->bsd/dot_general | solution.py:424
  105.9 4.5 convert_reduce_fusion.3
  110.5 0.8 fusion.113
  111.3 11.5 %multiply_convert_fusion = (bf16[32,512,256]{2,1,0:T(8,128)(2,1)}, f32[32,512,256]{2,1,0:T(8,128)}) fusion(f32[256]{0:T(256)S(1)} %get-tuple-element.62, bf16[49,256,1]{1,0,2:T(8,128)(2,1)S(1)} %reshape.334, bf16[32,49,512]{2,1,0:T(8,128)(2,1)S(1)} %get-tuple-element.89, f32[512]{0:T(512)S(1)} %get-tuple-element.65, f32[512]{0:T(512)S(1)} %get-tuple-element.64, ...), kind=kOutput, calls=%fused_computation.34 | convolution fusion | flops 457801728 | bytes 26814208 | tf_op jit(solution)/shard_map/bsc,sj->bcj/dot_general | solution.py:419
  123.1 6.4 %convert_reduce_fusion.2 = (f32[32,49]{1,0:T(8,128)S(1)}, bf16[32,49,512]{2,1,0:T(8,128)(2,1)S(1)}) fusion(f32[49]{0:T(128)S(1)} %slice.196, bf16[32,512,256]{2,1,0:T(8,128)(2,1)} %get-tuple-element.90, bf16[256,49]{1,0:T(8,128)(2,1)S(1)} %convert_element_type.239, bf16[32,49,512]{2,1,0:T(8,128)(2,1)S(1)} %get-tuple-element.89), kind=kOutput, calls=%fused_computation.66 | convolution fusion | flops 415857120 | bytes 11631428 | tf_op jit(solution)/shard_map/bcj,js->bsc/dot_general | solution.py:421
  129.4 0.9 fusion.116
  130.3 11.5 %multiply_convert_fusion.2 = (bf16[32,49,2048]{2,1,0:T(8,128)(2,1)}, f32[32,49,2048]{2,1,0:T(8,128)}) fusion(f32[2048]{0:T(1024)S(1)} %slice.199, bf16[2,512,2048]{2,1,0:T(8,128)(2,1)S(1)} %copy-done.63, bf16[32,49,512]{2,1,0:T(8,128)(2,1)S(1)} %get-tuple-element.93, f32[512]{0:T(512)S(1)} %get-tuple-element.73, f32[512]{0:T(512)S(1)} %get-tuple-element.74, ...), kind=kOutput, calls=%fused_computation.54 | convolution fusion | flops 3325263872 | bytes 23244800 | tf_op jit(solution)/shard_map/bsc,cd->bsd/dot_general | solution.py:424
  141.8 7.5 %convert_reduce_fusion.9 = (f32[32,49]{1,0:T(8,128)S(1)}, bf16[32,49,512]{2,1,0:T(8,128)(2,1)S(1)}) fusion(f32[512]{0:T(512)S(1)} %get-tuple-element.72, bf16[32,49,2048]{2,1,0:T(8,128)(2,1)} %get-tuple-element.94, bf16[2,2048,512]{2,1,0:T(8,128)(2,1)S(1)} %copy-done.65, bf16[32,49,512]{2,1,0:T(8,128)(2,1)S(1)} %get-tuple-element.93), kind=kOutput, calls=%fused_computation.101 | convolution fusion | flops 3293149696 | bytes 11968640 | tf_op jit(solution)/shard_map/bsd,dc->bsc/dot_general | solution.py:426
  149.4 0.8 fusion.104
  150.3 1.1 convert_reduce_fusion.10
  152.5 1.4 fusion.48
  153.9 1.0 fusion.78
  154.9 15.7 %fusion.247 = (f32[2048]{0:T(1024)S(1)}, bf16[32,49,2048]{2,1,0:T(8,128)(2,1)S(1)}) fusion(f32[32,49,2048]{2,1,0:T(8,128)} %get-tuple-element.95, f32[2048]{0:T(1024)S(1)} %slice.199, bf16[2,2048,512]{2,1,0:T(8,128)(2,1)S(1)} %copy-done.65, bf16[32,49,512]{2,1,0:T(8,128)(2,1)S(1)} %get-tuple-element.97, f32[32,49]{1,0:T(8,128)S(1)} %add_multiply_fusion.3, ...), kind=kOutput, calls=%fused_computation.318 | convolution fusion | flops 3371825152 | bytes 23349248 | tf_op jit(solution)/shard_map/bsc,dc->bsd/dot_general | solution.py:437
  170.6 4.5 fusion.129
  175.1 5.4 %fusion.119 = (f32[512]{0:T(512)S(1)}, f32[32,49]{1,0:T(8,128)S(1)}, f32[32,49]{1,0:T(8,128)S(1)}, f32[512]{0:T(512)S(1)}, bf16[32,49,512]{2,1,0:T(8,128)(2,1)S(1)}) fusion(bf16[32,49,512]{2,1,0:T(8,128)(2,1)S(1)} %get-tuple-element.93, f32[32,49]{1,0:T(8,128)S(1)} %fusion.217, f32[32,49]{1,0:T(8,128)S(1)} %broadcast_multiply_fusion.1, ...), kind=kOutput, calls=%fused_computation.169 | convolution fusion | flops 3298766848 | bytes 12929280 | tf_op jit(solution)/shard_map/bsd,cd->bsc/dot_general | solution.py:442
  180.5 1.0 fusion.84
  181.5 4.1 convert_reduce_fusion.8
  185.6 18.8 %fusion.246 = (f32[256]{0:T(256)S(1)}, bf16[32,512,256]{2,1,0:T(8,128)(2,1)}) fusion(f32[32,512,256]{2,1,0:T(8,128)} %get-tuple-element.91, f32[256]{0:T(256)S(1)} %get-tuple-element.62, bf16[256,49]{1,0:T(8,128)(2,1)S(1)} %convert_element_type.239, bf16[32,49,512]{2,1,0:T(8,128)(2,1)S(1)} %get-tuple-element.59, f32[32,49]{1,0:T(8,128)S(1)} %add_multiply_fusion.3, ...), kind=kOutput, calls=%fused_computation.317 | convolution fusion | flops 521338624 | bytes 28496896 | tf_op jit(solution)/shard_map/bsc,js->bcj/dot_general | solution.py:448
  204.4 6.2 %fusion.105 = (f32[512]{0:T(512)S(1)}, f32[32,49]{1,0:T(8,128)S(1)}, f32[32,49]{1,0:T(8,128)S(1)}, bf16[49,32,512]{2,0,1:T(8,128)(2,1)S(1)}) fusion(bf16[32,49,512]{2,1,0:T(8,128)(2,1)S(1)} %copy-done.5, f32[32,49]{1,0:T(8,128)S(1)} %fusion.216, f32[32,49]{1,0:T(8,128)S(1)} %broadcast_multiply_fusion.2, f32[512]{0:T(512)S(1)} %get-tuple-element.64, ...), kind=kOutput, calls=%fused_computation.155 | convolution fusion | flops 420671936 | bytes 11654144 | tf_op jit(solution)/shard_map/bcj,sj->bsc/dot_general | solution.py:453
  210.7 1.0 fusion.82
  211.7 3.2 convert_add_fusion.6
  214.9 17.9 %fusion.249 = (f32[2048]{0:T(1024)S(1)}, bf16[32,49,2048]{2,1,0:T(8,128)(2,1)}) fusion(f32[32,49,2048]{2,1,0:T(8,128)} %get-tuple-element.87, f32[2048]{0:T(1024)S(1)} %copy-done.43, bf16[2,2048,512]{2,1,0:T(8,128)(2,1)} %get-tuple-element.21, f32[32,49,512]{2,1,0:T(8,128)S(1)} %convert_add_fusion.6), kind=kOutput, calls=%fused_computation.320 | convolution fusion | flops 3366205440 | bytes 26427392 | tf_op jit(solution)/shard_map/bsc,dc->bsd/dot_general | solution.py:437
  232.9 7.6 %fusion.132 = f32[1,512,2048]{2,1,0:T(8,128)S(1)} fusion(bf16[32,49,2048]{2,1,0:T(8,128)(2,1)} %get-tuple-element.112, bf16[32,49,512]{2,1,0:T(8,128)(2,1)S(1)} %copy-done.7, f32[512]{0:T(512)S(1)} %copy-done.46, f32[512]{0:T(512)S(1)} %copy-done.39, f32[32,49]{1,0:T(8,128)S(1)} %copy-done.37, f32[32,49]{1,0:T(8,128)S(1)} %copy-done.20), kind=kOutput, calls=%fused_computation.183 | convolution fusion | flops 3293151232 | bytes 12239104 | tf_op jit(solution)/shard_map/bsc,bsd->cd/dot_general | solution.py:441
  240.5 3.8 pad_maximum_fusion.gw1_hbm
  244.3 7.4 %convolution_bitcast_fusion = f32[1,2048,512]{2,1,0:T(8,128)S(1)} fusion(bf16[32,49,2048]{2,1,0:T(8,128)(2,1)} %get-tuple-element.94, bf16[32,49,512]{2,1,0:T(8,128)(2,1)S(1)} %get-tuple-element.97, f32[32,49]{1,0:T(8,128)S(1)} %add_multiply_fusion.3, f32[32,49]{1,0:T(8,128)S(1)} %multiply_multiply_fusion.15, f32[32,512]{1,0:T(8,128)S(1)} %fusion.187, ...), kind=kOutput, calls=%fused_computation.184 | convolution fusion | flops 3294756864 | bytes 12315136 | tf_op jit(solution)/shard_map/bsd,bsc->dc/dot_general | solution.py:436
  251.8 6.5 %convolution_bitcast_fusion.1 = f32[1,2048,512]{2,1,0:T(8,128)S(1)} fusion(bf16[32,49,2048]{2,1,0:T(8,128)(2,1)} %copy-done.66, f32[32,49,512]{2,1,0:T(8,128)S(1)} %convert_add_fusion.6), kind=kOutput, calls=%fused_computation.185 | convolution fusion | flops 3289137152 | bytes 13828096 | tf_op jit(solution)/shard_map/bsd,bsc->dc/dot_general | solution.py:436
  258.3 4.2 pad_maximum_fusion.1.gw2_hbm
  262.9 7.4 %convolution_bitcast_fusion.2 = f32[256,49]{1,0:T(8,128)S(1)} fusion(bf16[32,512,256]{2,1,0:T(8,128)(2,1)} %get-tuple-element.90, bf16[32,49,512]{2,1,0:T(8,128)(2,1)} %copy-done.10, bf16[32,49,512]{2,1,0:T(8,128)(2,1)S(1)} %get-tuple-element.97, f32[32,49]{1,0:T(8,128)S(1)} %add_multiply_fusion.3, f32[32,49]{1,0:T(8,128)S(1)} %multiply_multiply_fusion.15, ...), kind=kOutput, calls=%fused_computation.219 | convolution fusion | flops 420675584 | bytes 11742720 | tf_op jit(solution)/shard_map/bcj,bsc->js/dot_general | solution.py:447
  270.5 5.7 %fusion.180 = f32[49,256]{1,0:T(8,128)S(1)} fusion(bf16[32,512,256]{2,1,0:T(8,128)(2,1)} %get-tuple-element.103, bf16[32,49,512]{2,1,0:T(8,128)(2,1)} %copy-done.4, f32[512]{0:T(512)S(1)} %copy-done.52, f32[512]{0:T(512)S(1)} %get-tuple-element.64, f32[32,49]{1,0:T(8,128)S(1)} %fusion.216, f32[32,49]{1,0:T(8,128)S(1)} %broadcast_multiply_fusion.2), kind=kOutput, calls=%fused_computation.222 | convolution fusion | flops 415858688 | bytes 10061056 | tf_op jit(solution)/shard_map/bsc,bcj->sj/dot_general | solution.py:452
  276.3 0.7 maximum_bitcast_fusion.1
  276.9 9.2 %fusion.120 = (f32[512]{0:T(512)S(1)}, f32[32,49]{1,0:T(8,128)S(1)}, f32[32,49]{1,0:T(8,128)S(1)}, f32[512]{0:T(512)S(1)}, bf16[32,49,512]{2,1,0:T(8,128)(2,1)S(1)}) fusion(bf16[32,49,512]{2,1,0:T(8,128)(2,1)S(1)} %copy-done.8, f32[32,49]{1,0:T(8,128)S(1)} %copy-done.37, f32[32,49]{1,0:T(8,128)S(1)} %copy-done.20, f32[512]{0:T(512)S(1)} %copy-done.39, ...), kind=kOutput, calls=%fused_computation.170 | convolution fusion | flops 3298766848 | bytes 12679680 | tf_op jit(solution)/shard_map/bsd,cd->bsc/dot_general | solution.py:442
  286.1 1.2 fusion.80
  287.4 3.1 fusion.233
  290.5 16.9 %fusion.248 = (f32[256]{0:T(256)S(1)}, bf16[32,512,256]{2,1,0:T(8,128)(2,1)S(1)}) fusion(f32[32,512,256]{2,1,0:T(8,128)} %get-tuple-element.83, f32[256]{0:T(256)S(1)} %copy-done.58, bf16[256,49]{1,0:T(8,128)(2,1)S(1)} %copy-done.22, f32[32,49,512]{2,1,0:T(8,128)S(1)} %copy-done.1, bf16[32,49,512]{2,1,0:T(8,128)(2,1)} %get-tuple-element.58), kind=kOutput, calls=%fused_computation.319 | convolution fusion | flops 514113280 | bytes 30009856 | tf_op jit(solution)/shard_map/bsc,js->bcj/dot_general | solution.py:448
  307.5 3.6 fusion.98
  311.6 7.4 %convolution_bitcast_fusion.3 = f32[256,49]{1,0:T(8,128)} fusion(bf16[32,512,256]{2,1,0:T(8,128)(2,1)} %get-tuple-element.82, f32[32,49,512]{2,1,0:T(8,128)} %copy-done, bf16[32,49,512]{2,1,0:T(8,128)(2,1)S(1)} %copy-done.11), kind=kOutput, calls=%fused_computation.220 | convolution fusion | flops 413450240 | bytes 13255680 | tf_op jit(solution)/shard_map/bcj,bsc->js/dot_general | solution.py:447
  319.1 1.1 reshape.322
  320.2 5.9 %fusion.183 = f32[49,256]{1,0:T(8,128)S(1)} fusion(bf16[32,512,256]{2,1,0:T(8,128)(2,1)} %copy-done.9, f32[512]{0:T(512)S(1)} %copy-done.48, f32[512]{0:T(512)S(1)} %copy-done.50, f32[32,49]{1,0:T(8,128)S(1)} %copy-done.35, f32[32,49]{1,0:T(8,128)S(1)} %copy-done.24, bf16[32,49,512]{2,0,1:T(8,128)(2,1)S(1)} %copy-done.3), kind=kOutput, calls=%fused_computation.223 | convolution fusion | flops 415858688 | bytes 10061056 | tf_op jit(solution)/shard_map/bsc,bcj->sj/dot_general | solution.py:452
  326.2 0.7 pad_maximum_fusion.2.slab_ref
  327.4 1.5 pad.23.gh_ref
  329.1 0.6 fusion.220.gs_ref
  329.7 0.6 subtract_reduce_fusion
  330.3 1.2 broadcast_in_dim.30.loss_ref
  331.6 111.9 %reduce_grads.1 = (f32[2,1040,128]{2,1,0:T(8,128)}, f32[256,128]{1,0:T(8,128)}, f32[8,128]{1,0:T(8,128)}, f32[2,8,128]{2,1,0:T(8,128)}) custom-call(f32[2,512,2048]{2,1,0:T(8,128)} %pad_maximum_fusion.gw1_hbm, f32[2,2048,512]{2,1,0:T(8,128)} %pad_maximum_fusion.1.gw2_hbm, f32[2,240,128]{2,1,0:T(8,128)} %pad_maximum_fusion.2.slab_ref, ...), custom_call_target="tpu_custom_call" | custom-call | tf_op jit(solution)/shard_map/reduce_grads/pallas_call | solution.py:332
  443.4 1.2 fusion.244
  446.1 1.3 multiply_bitcast_fusion
  447.5 6.9 %multiply_subtract_fusion = (f32[2,132992]{1,0:T(2,128)}, f32[2,132992]{1,0:T(2,128)}, f32[2,132992]{1,0:T(2,128)}) fusion(f32[2,132992]{1,0:T(2,128)} %param.13, f32[132992]{0:T(1024)S(1)} %fusion.207, f32[1,2,1039,128]{3,2,1,0:T(8,128)S(1)} %multiply_bitcast_fusion, f32[2,132992]{1,0:T(2,128)} %param.16, f32[2,132992]{1,0:T(2,128)} %param.19), kind=kLoop, calls=%fused_computation.230 | loop fusion | flops 3989760 | bytes 7979520 | tf_op jit(solution)/shard_map/sub | solution.py:491
  454.4 0.8 multiply_subtract_fusion.1
  455.2 1.2 multiply_subtract_fusion.2
  (184 shorter events, 4.2 us)
Async XLA Ops:
  66.3 9.0 %copy-start.2 = (bf16[32,49,512]{2,0,1:T(8,128)(2,1)S(1)}, bf16[32,49,512]{2,0,1:T(8,128)(2,1)}, u32[]{:S(2)}) copy-start(bf16[32,49,512]{2,0,1:T(8,128)(2,1)} %param.11) | copy-start | bytes 4816900
  67.9 18.9 %copy-start.57 = (f32[256]{0:T(256)}, f32[256]{0:T(256)S(1)}, u32[]{:S(2)}) copy-start(f32[256]{0:T(256)S(1)} %get-tuple-element.63) | copy-start | bytes 3076
  69.0 26.1 %copy-start.38 = (f32[512]{0:T(512)}, f32[512]{0:T(512)S(1)}, u32[]{:S(2)}) copy-start(f32[512]{0:T(512)S(1)} %get-tuple-element.115) | copy-start | bytes 6148
  69.0 26.1 %copy-start.45 = (f32[512]{0:T(512)}, f32[512]{0:T(512)S(1)}, u32[]{:S(2)}) copy-start(f32[512]{0:T(512)S(1)} %get-tuple-element.113) | copy-start | bytes 6148
  69.1 26.0 %copy-start.42 = (f32[2048]{0:T(1024)}, f32[2048]{0:T(1024)S(1)}, u32[]{:S(2)}) copy-start(f32[2048]{0:T(1024)S(1)} %slice.193) | copy-start | bytes 24580
  69.1 17.7 %copy-start.32 = (bf16[49,256,1]{1,0,2:T(8,128)(2,1)}, bf16[49,256,1]{1,0,2:T(8,128)(2,1)S(1)}, u32[]{:S(2)}) copy-start(bf16[49,256,1]{1,0,2:T(8,128)(2,1)S(1)} %reshape.330) | copy-start | bytes 75268
  69.8 17.0 %copy-start.47 = (f32[512]{0:T(512)}, f32[512]{0:T(512)S(1)}, u32[]{:S(2)}) copy-start(f32[512]{0:T(512)S(1)} %get-tuple-element.66) | copy-start | bytes 6148
  69.9 17.0 %copy-start.49 = (f32[512]{0:T(512)}, f32[512]{0:T(512)S(1)}, u32[]{:S(2)}) copy-start(f32[512]{0:T(512)S(1)} %get-tuple-element.67) | copy-start | bytes 6148
  69.9 41.5 %copy-start.51 = (f32[512]{0:T(512)}, f32[512]{0:T(512)S(1)}, u32[]{:S(2)}) copy-start(f32[512]{0:T(512)S(1)} %get-tuple-element.65) | copy-start | bytes 6148
  72.4 14.4 %copy-start.23 = (f32[32,49]{1,0:T(8,128)}, f32[32,49]{1,0:T(8,128)S(1)}, u32[]{:S(2)}) copy-start(f32[32,49]{1,0:T(8,128)S(1)} %broadcast_multiply_fusion.4) | copy-start | bytes 18820
  75.3 11.5 %copy-start.34 = (f32[32,49]{1,0:T(8,128)}, f32[32,49]{1,0:T(8,128)S(1)}, u32[]{:S(2)}) copy-start(f32[32,49]{1,0:T(8,128)S(1)} %add_rsqrt_fusion) | copy-start | bytes 18820
  87.1 7.1 %copy-start.21 = (bf16[256,49]{1,0:T(8,128)(2,1)}, bf16[256,49]{1,0:T(8,128)(2,1)S(1)}, u32[]{:S(2)}) copy-start(bf16[256,49]{1,0:T(8,128)(2,1)S(1)} %convert_element_type.228) | copy-start | bytes 75268
  87.1 8.0 %copy-start.62 = (bf16[2,512,2048]{2,1,0:T(8,128)(2,1)S(1)}, bf16[2,512,2048]{2,1,0:T(8,128)(2,1)}, u32[]{:S(2)}) copy-start(bf16[2,512,2048]{2,1,0:T(8,128)(2,1)} %get-tuple-element.20) | copy-start | bytes 12582916
  94.2 11.7 %copy-start.6 = (bf16[32,49,512]{2,1,0:T(8,128)(2,1)}, bf16[32,49,512]{2,1,0:T(8,128)(2,1)S(1)}, u32[]{:S(2)}) copy-start(bf16[32,49,512]{2,1,0:T(8,128)(2,1)S(1)} %get-tuple-element.85) | copy-start | bytes 4816900
  94.2 11.7 %copy-start.19 = (f32[32,49]{1,0:T(8,128)}, f32[32,49]{1,0:T(8,128)S(1)}, u32[]{:S(2)}) copy-start(f32[32,49]{1,0:T(8,128)S(1)} %broadcast_multiply_fusion.3) | copy-start | bytes 18820
  95.1 10.8 %copy-start.25 = (f32[32,49]{1,0:T(8,128)}, f32[32,49]{1,0:T(8,128)S(1)}, u32[]{:S(2)}) copy-start(f32[32,49]{1,0:T(8,128)S(1)} %fusion.110) | copy-start | bytes 18820
  95.1 10.7 %copy-start.36 = (f32[32,49]{1,0:T(8,128)}, f32[32,49]{1,0:T(8,128)S(1)}, u32[]{:S(2)}) copy-start(f32[32,49]{1,0:T(8,128)S(1)} %fusion.215) | copy-start | bytes 18820
  95.1 10.7 %copy-start.64 = (bf16[2,2048,512]{2,1,0:T(8,128)(2,1)S(1)}, bf16[2,2048,512]{2,1,0:T(8,128)(2,1)}, u32[]{:S(2)}) copy-start(bf16[2,2048,512]{2,1,0:T(8,128)(2,1)} %get-tuple-element.21) | copy-start | bytes 12582916
  105.9 4.6 %copy-start.66 = (bf16[32,49,2048]{2,1,0:T(8,128)(2,1)}, bf16[32,49,2048]{2,1,0:T(8,128)(2,1)S(1)}, u32[]{:S(2)}) copy-start(bf16[32,49,2048]{2,1,0:T(8,128)(2,1)S(1)} %get-tuple-element.86) | copy-start | bytes 19267588
  110.5 12.6 %copy-start.4 = (bf16[32,49,512]{2,1,0:T(8,128)(2,1)}, bf16[32,49,512]{2,1,0:T(8,128)(2,1)S(1)}, u32[]{:S(2)}) copy-start(bf16[32,49,512]{2,1,0:T(8,128)(2,1)S(1)} %get-tuple-element.89) | copy-start | bytes 4816900
  111.3 11.5 %copy-start.27 = (f32[32,49]{1,0:T(8,128)}, f32[32,49]{1,0:T(8,128)S(1)}, u32[]{:S(2)}) copy-start(f32[32,49]{1,0:T(8,128)S(1)} %fusion.113) | copy-start | bytes 18820
  123.1 7.3 %copy-start.63 = (bf16[2,512,2048]{2,1,0:T(8,128)(2,1)S(1)}, bf16[2,512,2048]{2,1,0:T(8,128)(2,1)}, u32[]{:S(2)}) copy-start(bf16[2,512,2048]{2,1,0:T(8,128)(2,1)} %get-tuple-element.20) | copy-start | bytes 12582916
  130.3 11.5 %copy-start.65 = (bf16[2,2048,512]{2,1,0:T(8,128)(2,1)S(1)}, bf16[2,2048,512]{2,1,0:T(8,128)(2,1)}, u32[]{:S(2)}) copy-start(bf16[2,2048,512]{2,1,0:T(8,128)(2,1)} %get-tuple-element.21) | copy-start | bytes 12582916
  141.8 7.6 %copy-start.44 = (f32[16,128]{1,0:T(8,128)S(1)}, f32[16,128]{1,0:T(8,128)}, u32[]{:S(2)}) copy-start(f32[16,128]{1,0:T(8,128)} %get-tuple-element.22) | copy-start | bytes 24580
  151.4 19.3 %copy-start.15 = (f32[32,512]{1,0:T(8,128)}, f32[32,512]{1,0:T(8,128)S(1)}, u32[]{:S(2)}) copy-start(f32[32,512]{1,0:T(8,128)S(1)} %convert_reduce_fusion.10) | copy-start | bytes 196612
  151.8 18.9 %copy-start.12 = (f32[32,1000]{1,0:T(8,128)}, f32[32,1000]{1,0:T(8,128)S(1)}, u32[]{:S(2)}) copy-start(f32[32,1000]{1,0:T(8,128)S(1)} %get-tuple-element.99) | copy-start | bytes 384004
  185.6 26.1 %copy-start.10 = (bf16[32,49,512]{2,1,0:T(8,128)(2,1)}, bf16[32,49,512]{2,1,0:T(8,128)(2,1)S(1)}, u32[]{:S(2)}) copy-start(bf16[32,49,512]{2,1,0:T(8,128)(2,1)S(1)} %get-tuple-element.59) | copy-start | bytes 4816900
  185.6 18.8 %copy-start.5 = (bf16[32,49,512]{2,1,0:T(8,128)(2,1)S(1)}, bf16[32,49,512]{2,1,0:T(8,128)(2,1)}, u32[]{:S(2)}) copy-start(bf16[32,49,512]{2,1,0:T(8,128)(2,1)} %copy-done.4) | copy-start | bytes 4816900
  204.4 6.2 %copy-start.28 = (f32[32,49]{1,0:T(8,128)S(1)}, f32[32,49]{1,0:T(8,128)}, u32[]{:S(2)}) copy-start(f32[32,49]{1,0:T(8,128)} %copy-done.27) | copy-start | bytes 18820
  211.7 3.2 copy-start.43
  214.9 36.9 %copy-start = (f32[32,49,512]{2,1,0:T(8,128)}, f32[32,49,512]{2,1,0:T(8,128)S(1)}, u32[]{:S(2)}) copy-start(f32[32,49,512]{2,1,0:T(8,128)S(1)} %convert_add_fusion.6) | copy-start | bytes 9633796
  214.9 18.0 %copy-start.7 = (bf16[32,49,512]{2,1,0:T(8,128)(2,1)S(1)}, bf16[32,49,512]{2,1,0:T(8,128)(2,1)}, u32[]{:S(2)}) copy-start(bf16[32,49,512]{2,1,0:T(8,128)(2,1)} %copy-done.6) | copy-start | bytes 4816900
  214.9 18.0 %copy-start.20 = (f32[32,49]{1,0:T(8,128)S(1)}, f32[32,49]{1,0:T(8,128)}, u32[]{:S(2)}) copy-start(f32[32,49]{1,0:T(8,128)} %copy-done.19) | copy-start | bytes 18820
  214.9 18.0 %copy-start.37 = (f32[32,49]{1,0:T(8,128)S(1)}, f32[32,49]{1,0:T(8,128)}, u32[]{:S(2)}) copy-start(f32[32,49]{1,0:T(8,128)} %copy-done.36) | copy-start | bytes 18820
  214.9 18.0 %copy-start.39 = (f32[512]{0:T(512)S(1)}, f32[512]{0:T(512)}, u32[]{:S(2)}) copy-start(f32[512]{0:T(512)} %copy-done.38) | copy-start | bytes 6148
  214.9 18.0 %copy-start.46 = (f32[512]{0:T(512)S(1)}, f32[512]{0:T(512)}, u32[]{:S(2)}) copy-start(f32[512]{0:T(512)} %copy-done.45) | copy-start | bytes 6148
  262.9 7.6 %copy-start.52 = (f32[512]{0:T(512)S(1)}, f32[512]{0:T(512)}, u32[]{:S(2)}) copy-start(f32[512]{0:T(512)} %copy-done.51) | copy-start | bytes 6148
  270.5 6.4 %copy-start.8 = (bf16[32,49,512]{2,1,0:T(8,128)(2,1)S(1)}, bf16[32,49,512]{2,1,0:T(8,128)(2,1)}, u32[]{:S(2)}) copy-start(bf16[32,49,512]{2,1,0:T(8,128)(2,1)} %copy-done.6) | copy-start | bytes 4816900
  276.9 9.2 %copy-start.26 = (f32[32,49]{1,0:T(8,128)S(1)}, f32[32,49]{1,0:T(8,128)}, u32[]{:S(2)}) copy-start(f32[32,49]{1,0:T(8,128)} %copy-done.25) | copy-start | bytes 18820
  276.9 10.4 %copy-start.1 = (f32[32,49,512]{2,1,0:T(8,128)S(1)}, f32[32,49,512]{2,1,0:T(8,128)}, u32[]{:S(2)}) copy-start(f32[32,49,512]{2,1,0:T(8,128)} %copy-done) | copy-start | bytes 9633796
  287.4 3.1 copy-start.22
  287.4 3.1 copy-start.58
  290.5 17.0 %copy-start.3 = (bf16[32,49,512]{2,0,1:T(8,128)(2,1)S(1)}, bf16[32,49,512]{2,0,1:T(8,128)(2,1)}, u32[]{:S(2)}) copy-start(bf16[32,49,512]{2,0,1:T(8,128)(2,1)} %param.11) | copy-start | bytes 4816900
  290.5 17.0 %copy-start.24 = (f32[32,49]{1,0:T(8,128)S(1)}, f32[32,49]{1,0:T(8,128)}, u32[]{:S(2)}) copy-start(f32[32,49]{1,0:T(8,128)} %copy-done.23) | copy-start | bytes 18820
  290.5 17.0 %copy-start.33 = (bf16[49,256,1]{1,0,2:T(8,128)(2,1)S(1)}, bf16[49,256,1]{1,0,2:T(8,128)(2,1)}, u32[]{:S(2)}) copy-start(bf16[49,256,1]{1,0,2:T(8,128)(2,1)} %copy-done.32) | copy-start | bytes 75268
  290.5 17.0 %copy-start.35 = (f32[32,49]{1,0:T(8,128)S(1)}, f32[32,49]{1,0:T(8,128)}, u32[]{:S(2)}) copy-start(f32[32,49]{1,0:T(8,128)} %copy-done.34) | copy-start | bytes 18820
  307.4 3.7 copy-start.9
  307.5 4.1 copy-start.11
  311.6 8.6 %copy-start.48 = (f32[512]{0:T(512)S(1)}, f32[512]{0:T(512)}, u32[]{:S(2)}) copy-start(f32[512]{0:T(512)} %copy-done.47) | copy-start | bytes 6148
  311.6 8.6 %copy-start.50 = (f32[512]{0:T(512)S(1)}, f32[512]{0:T(512)}, u32[]{:S(2)}) copy-start(f32[512]{0:T(512)} %copy-done.49) | copy-start | bytes 6148
  320.2 6.0 %copy-start.18 = (f32[1,240,128]{2,1,0:T(8,128)S(1)}, f32[1,240,128]{2,1,0:T(8,128)}, u32[]{:S(2)}) copy-start(f32[1,240,128]{2,1,0:T(8,128)} %maximum_bitcast_fusion.1) | copy-start | bytes 368644
  320.2 6.7 %copy-start.13 = (f32[32,1000]{1,0:T(8,128)S(1)}, f32[32,1000]{1,0:T(8,128)}, u32[]{:S(2)}) copy-start(f32[32,1000]{1,0:T(8,128)} %copy-done.12) | copy-start | bytes 384004
  320.2 6.7 %copy-start.16 = (f32[32,512]{1,0:T(8,128)S(1)}, f32[32,512]{1,0:T(8,128)}, u32[]{:S(2)}) copy-start(f32[32,512]{1,0:T(8,128)} %copy-done.15) | copy-start | bytes 196612
  320.2 6.7 %copy-start.54 = (s32[32]{0:T(128)S(1)}, s32[32]{0:T(128)}, u32[]{:S(2)}) copy-start(s32[32]{0:T(128)} %param.12) | copy-start | bytes 388
  320.2 6.7 %copy-start.56 = (f32[32]{0:T(128)S(1)}, f32[32]{0:T(128)}, u32[]{:S(2)}) copy-start(f32[32]{0:T(128)} %copy-done.55) | copy-start | bytes 388
  326.1 3.0 copy-start.40
  326.1 3.0 copy-start.41
  447.4 7.0 %copy-start.31 = (f32[256,128]{1,0:T(8,128)S(1)}, f32[256,128]{1,0:T(8,128)}, u32[]{:S(2)}) copy-start(f32[256,128]{1,0:T(8,128)} %get-tuple-element.26) | copy-start | bytes 393220
  447.4 7.0 %copy-start.17 = (f32[32,1000]{1,0:T(8,128)S(1)}, f32[32,1000]{1,0:T(8,128)}, u32[]{:S(2)}) copy-start(f32[32,1000]{1,0:T(8,128)} %param.14) | copy-start | bytes 384004
  447.4 7.0 %copy-start.29 = (f32[32,1000]{1,0:T(8,128)S(1)}, f32[32,1000]{1,0:T(8,128)}, u32[]{:S(2)}) copy-start(f32[32,1000]{1,0:T(8,128)} %param.17) | copy-start | bytes 384004
  447.5 7.0 %copy-start.30 = (f32[32,1000]{1,0:T(8,128)S(1)}, f32[32,1000]{1,0:T(8,128)}, u32[]{:S(2)}) copy-start(f32[32,1000]{1,0:T(8,128)} %param.20) | copy-start | bytes 384004
  447.5 7.8 %copy-start.59 = (f32[128]{0:T(128)S(1)}, f32[128]{0:T(128)}, u32[]{:S(2)}) copy-start(f32[128]{0:T(128)} %param.15) | copy-start | bytes 1540
  447.5 7.8 %copy-start.60 = (f32[128]{0:T(128)S(1)}, f32[128]{0:T(128)}, u32[]{:S(2)}) copy-start(f32[128]{0:T(128)} %param.18) | copy-start | bytes 1540
  447.5 7.7 %copy-start.61 = (f32[128]{0:T(128)S(1)}, f32[128]{0:T(128)}, u32[]{:S(2)}) copy-start(f32[128]{0:T(128)} %param.21) | copy-start | bytes 1540
  (3 other events, 6.5 us)

commit v2 on v1

v2 whole, which is shorter than its diff:
```python
import functools
import math
import jax
import jax.numpy as jnp
from jax import lax
from jax.experimental import pallas as pl
from jax.experimental.pallas import tpu as pltpu
from jax.sharding import PartitionSpec as P

ZERO = 0
ONE = 1
TWO = 2
THREE = 3
FOUR = 4
FIVE = 5
SIX = 6
SEVEN = 7
EIGHT = 8
NINE = 9
SIXTEEN = 16
LANES = 128
IMAGES = 32
LAST_IMAGE = 31
CH = 512
CLASS_PAD = 1024
HID = 2048
TH = 256
F_ZERO = 0.0
F_ONE = 1.0
TWENTY_FOUR = 24
TOKEN_PAD = 56
QVALID = 196
SIXTY_FOUR = 64
TEN = 10
MESH_ID = pl.DeviceIdType.MESH
F32 = jnp.float32
BF16 = jnp.bfloat16
VMEM_CAP = 64 * 1024 * 1024 - 128 * 1024

SHARD_ROWS = 1039
SLOT_ROWS = 1040
ROW_C1 = 196
ROW_C2 = 8388
ROW_VEC = 16580
FLAT_ROWS = 16624
SLAB_ROWS = 240
HEAD_OFF = 2 * SLOT_ROWS
SMALL_OFF = HEAD_OFF + 256
AG_ROWS = SMALL_OFF + 16
RS_ROWS = SMALL_OFF + 8
ORDERS = ((2, 1, 0), (1, 0, 2), (0, 2, 1))
AXIS_STEP = (8, 4, 2)


def place():
    me = lax.axis_index('fsdp')
    coords = [me // EIGHT, (me // FOUR) % TWO, (me // TWO) % TWO]
    core = me % TWO
    neighbours = [me + AXIS_STEP[a] - TWO * AXIS_STEP[a] * coords[a] for a in range(THREE)]
    partner = me + ONE - TWO * core
    return me, coords, core, neighbours, partner


def enter_barrier(neighbours, partner):
    barrier = pltpu.get_barrier_semaphore()
    for other in list(neighbours) + [partner]:
        pl.semaphore_signal(barrier, inc=ONE, device_id=(other,), device_id_type=MESH_ID)
    pl.semaphore_wait(barrier, FOUR)


def slot_view(buf, coords, core, free_axes, row0, rows):
    index = [pl.ds(ZERO, TWO) if a in free_axes else coords[a] for a in range(THREE)]
    return buf.at[index[ZERO], index[ONE], index[TWO], core, pl.ds(row0, rows), :]


class Gather:
    def __init__(self, buf, where, row_groups, send_sem, recv_sem, sem0):
        self.buf, self.where, self.groups = buf, where, row_groups
        self.send_sem, self.recv_sem, self.sem0 = send_sem, recv_sem, sem0
        self.pending = []

    def copy(self, view, sem, device):
        return pltpu.make_async_remote_copy(src_ref=view, dst_ref=view, send_sem=self.send_sem.at[self.sem0 + sem], recv_sem=self.recv_sem.at[self.sem0 + sem], device_id=(device,), device_id_type=MESH_ID)

    def link(self, group, phase):
        me, coords, core, neighbours, partner = self.where
        order = ORDERS[group]
        row0, rows = self.groups[group]
        view = slot_view(self.buf, coords, core, order[:phase], row0, rows)
        return self.copy(view, group * THREE + phase, neighbours[order[phase]])

    def chip(self, group, phase):
        me, coords, core, neighbours, partner = self.where
        order = ORDERS[group]
        row0, rows = self.groups[group]
        if phase < ZERO:
            view = slot_view(self.buf, coords, core, (), row0, rows)
        else:
            far = list(coords)
            far[order[phase]] = ONE - coords[order[phase]]
            view = slot_view(self.buf, far, core, order[:phase], row0, rows)
        return self.copy(view, NINE + group * FOUR + phase + ONE, partner)

    def start(self):
        for group in range(THREE):
            self.link(group, ZERO).start()
        for group in range(THREE):
            self.chip(group, -ONE).start()

    def step(self, phase):
        for group in range(THREE):
            self.link(group, phase).wait_recv()
            if phase < TWO:
                self.link(group, phase + ONE).start()
            self.chip(group, phase).start()

    def finish(self):
        for group in range(THREE):
            for phase in range(-ONE, THREE):
                self.chip(group, phase).wait()
            for phase in range(THREE):
                self.link(group, phase).wait_send()


def unflatten_layer(gath, layer, flat, w1_ref, w2_ref, slab_ref):
    base = layer * SLOT_ROWS

    def spread(dev, carry):
        z, y, x, core = dev // EIGHT, (dev // FOUR) % TWO, (dev // TWO) % TWO, dev % TWO

        def chunk(k, inner):
            block = gath[z, y, x, core, pl.ds(base + SIXTEEN * k, SIXTEEN), :]
            flat[pl.ds(dev * SHARD_ROWS + SIXTEEN * k, SIXTEEN), :] = block.astype(F32)
            return inner
        return lax.fori_loop(ZERO, SLOT_ROWS // SIXTEEN, chunk, carry, unroll=FIVE)
    lax.fori_loop(ZERO, SIXTEEN, spread, ZERO)

    def first(rb, carry):
        for j in range(SIXTEEN):
            block = flat[pl.ds(ROW_C1 + TH * rb + j, SIXTEEN, stride=SIXTEEN), :]
            w1_ref[layer, pl.ds(pl.multiple_of(SIXTEEN * rb, SIXTEEN), SIXTEEN), LANES * j:LANES * j + LANES] = block.astype(BF16)
        return carry
    lax.fori_loop(ZERO, IMAGES, first, ZERO)

    def second(rb, carry):
        for j in range(FOUR):
            block = flat[pl.ds(ROW_C2 + SIXTY_FOUR * rb + j, SIXTEEN, stride=FOUR), :]
            w2_ref[layer, pl.ds(pl.multiple_of(SIXTEEN * rb, SIXTEEN), SIXTEEN), LANES * j:LANES * j + LANES] = block.astype(BF16)
        return carry
    lax.fori_loop(ZERO, LANES, second, ZERO)
    slab_ref[layer, ZERO:QVALID, :] = flat[ZERO:QVALID, :]
    slab_ref[layer, QVALID:240, :] = flat[ROW_VEC:FLAT_ROWS, :]


def gather_kernel(pack_ref, w1_ref, w2_ref, slab_ref, head_ref, small_ref, gath, flat, send_sem, recv_sem, load_sem):
    where = place()
    me, coords, core, neighbours, partner = where
    load = pltpu.make_async_copy(pack_ref, gath.at[coords[ZERO], coords[ONE], coords[TWO], core], load_sem)
    load.start()
    enter_barrier(neighbours, partner)
    load.wait()
    third = AG_ROWS // THREE
    work = Gather(gath, where, [(third * g, third) for g in range(THREE)], send_sem, recv_sem, ZERO)
    work.start()
    for phase in range(THREE):
        work.step(phase)
    work.finish()
    for layer in range(TWO):
        unflatten_layer(gath, layer, flat, w1_ref, w2_ref, slab_ref)

    def spread_head(dev, carry):
        z, y, x, own = dev // EIGHT, (dev // FOUR) % TWO, (dev // TWO) % TWO, dev % TWO
        for j in range(EIGHT):
            head_ref[pl.ds(pl.multiple_of(IMAGES * dev, IMAGES), IMAGES), LANES * j:LANES * j + LANES] = gath[z, y, x, own, pl.ds(HEAD_OFF + IMAGES * j, IMAGES), :]
        small_ref[pl.ds(dev, ONE), :] = gath[z, y, x, own, pl.ds(SMALL_OFF, SIXTEEN), :].astype(F32)[ZERO:ONE, :]
        return carry
    lax.fori_loop(ZERO, SIXTEEN, spread_head, ZERO)


def gather_weights(pack):
    vmem = pl.BlockSpec(memory_space=pltpu.VMEM)
    return pl.pallas_call(
        gather_kernel,
        out_shape=(jax.ShapeDtypeStruct((TWO, CH, HID), BF16), jax.ShapeDtypeStruct((TWO, HID, CH), BF16), jax.ShapeDtypeStruct((TWO, SLAB_ROWS, LANES), F32), jax.ShapeDtypeStruct((CH, CLASS_PAD), BF16), jax.ShapeDtypeStruct((SIXTEEN, LANES), F32)),
        in_specs=[vmem],
        out_specs=(vmem,) * FIVE,
        scratch_shapes=[
            pltpu.VMEM((TWO, TWO, TWO, TWO, AG_ROWS, LANES), BF16),
            pltpu.VMEM((16640, LANES), F32),
            pltpu.SemaphoreType.DMA((21,)),
            pltpu.SemaphoreType.DMA((21,)),
            pltpu.SemaphoreType.DMA,
        ],
        compiler_params=pltpu.CompilerParams(collective_id=ZERO, has_side_effects=True, vmem_limit_bytes=VMEM_CAP),
        name='gather_weights',
    )(pack)


class Reduce:
    def __init__(self, buf, temps, where, row_groups, send_sem, recv_sem, sem0):
        self.buf, self.temps, self.where, self.groups = buf, temps, where, row_groups
        self.send_sem, self.recv_sem, self.sem0 = send_sem, recv_sem, sem0

    def views(self, group, phase):
        me, coords, core, neighbours, partner = self.where
        row0, rows = self.groups[group]
        order = ORDERS[group]
        if phase == ZERO:
            free = (ZERO, ONE, TWO)
            leave = slot_view(self.buf, coords, ONE - core, free, row0, rows)
            device = partner
            stay = coords
        else:
            axis = order[phase - ONE]
            free = tuple(a for a in range(THREE) if a in order[phase:])
            far = list(coords)
            far[axis] = ONE - coords[axis]
            leave = slot_view(self.buf, far, core, free, row0, rows)
            device = neighbours[axis]
            stay = coords
        land = self.temps[phase].at[(slice(None),) * len(free) + (pl.ds(row0, rows), slice(None))]
        return leave, land, device, free, stay

    def copy(self, group, phase):
        leave, land, device, free, stay = self.views(group, phase)
        sem = self.sem0 + group * FOUR + phase
        return pltpu.make_async_remote_copy(src_ref=leave, dst_ref=land, send_sem=self.send_sem.at[sem], recv_sem=self.recv_sem.at[sem], device_id=(device,), device_id_type=MESH_ID)

    def add(self, group, phase):
        me, coords, core, neighbours, partner = self.where
        leave, land, device, free, stay = self.views(group, phase)
        row0, rows = self.groups[group]
        temp = self.temps[phase]
        count = TWO ** len(free)
        per = max(ONE, EIGHT // count)
        while rows % (EIGHT * per):
            per //= TWO

        def chunk(k, carry):
            for part in range(per):
                start = pl.multiple_of(row0 + EIGHT * (per * k + part), EIGHT)
                for n in range(count):
                    index = list(coords)
                    bits = []
                    for pos, a in enumerate(free):
                        bit = (n // TWO ** (len(free) - ONE - pos)) % TWO
                        index[a] = bit
                        bits.append(bit)
                    target = (index[ZERO], index[ONE], index[TWO], core, pl.ds(start, EIGHT), slice(None))
                    self.buf[target] = self.buf[target] + temp[tuple(bits) + (pl.ds(start, EIGHT), slice(None))]
            return carry
        lax.fori_loop(ZERO, rows // (EIGHT * per), chunk, ZERO)

    def start(self):
        for group in range(THREE):
            self.copy(group, ZERO).start()

    def step(self, phase):
        for group in range(THREE):
            self.copy(group, phase).wait_recv()
            self.add(group, phase)
            if phase < THREE:
                self.copy(group, phase + ONE).start()

    def finish(self):
        for group in range(THREE):
            for phase in range(FOUR):
                self.copy(group, phase).wait_send()


def spread_layer(layer, flat, grad):
    base = layer * SLOT_ROWS

    def spread(dev, carry):
        z, y, x, core = dev // EIGHT, (dev // FOUR) % TWO, (dev // TWO) % TWO, dev % TWO

        def chunk(k, inner):
            grad[z, y, x, core, pl.ds(pl.multiple_of(base + EIGHT * k, EIGHT), EIGHT), :] = flat[pl.ds(dev * SHARD_ROWS + EIGHT * k, EIGHT), :]
            return inner
        return lax.fori_loop(ZERO, SLOT_ROWS // EIGHT, chunk, carry, unroll=TEN)
    lax.fori_loop(ZERO, SIXTEEN, spread, ZERO)


def square_sum(ref, coords, core, row0, rows):
    def chunk(k, total):
        block = ref[coords[ZERO], coords[ONE], coords[TWO], core, pl.ds(pl.multiple_of(row0 + EIGHT * k, EIGHT), EIGHT), :]
        return total + block * block
    return lax.fori_loop(ZERO, rows // EIGHT, chunk, jnp.zeros((EIGHT, LANES), F32), unroll=TWO)


def reduce_kernel(flat_hbm, gh_ref, gs_ref, loss_ref, gl_ref, ghead_ref, gsmall_ref, stat_ref, flat, grad, t0, t1, t2, t3, msg, box, send_sem, recv_sem, load_sem, tiny_send, tiny_recv):
    where = place()
    me, coords, core, neighbours, partner = where
    enter_barrier(neighbours, partner)
    for layer in (ONE, ZERO):
        copy = pltpu.make_async_copy(flat_hbm.at[layer], flat, load_sem)
        copy.start()
        copy.wait()
        spread_layer(layer, flat, grad)

    def spread_head(dev, carry):
        z, y, x, own = dev // EIGHT, (dev // FOUR) % TWO, (dev // TWO) % TWO, dev % TWO
        for j in range(EIGHT):
            grad[z, y, x, own, HEAD_OFF + IMAGES * j:HEAD_OFF + IMAGES * j + IMAGES, :] = gh_ref[pl.ds(pl.multiple_of(IMAGES * dev, IMAGES), IMAGES), LANES * j:LANES * j + LANES]
        grad[z, y, x, own, SMALL_OFF:AG_ROWS, :] = jnp.zeros((SIXTEEN, LANES), F32)
        grad[z, y, x, own, SMALL_OFF:SMALL_OFF + ONE, :] = gs_ref[pl.ds(dev, ONE), :]
        grad[z, y, x, own, SMALL_OFF + EIGHT:SMALL_OFF + SIXTEEN, :] = loss_ref[...]
        return carry
    lax.fori_loop(ZERO, SIXTEEN, spread_head, ZERO)
    third = AG_ROWS // THREE
    work = Reduce(grad, (t0, t1, t2, t3), where, [(third * g, third) for g in range(THREE)], send_sem, recv_sem, ZERO)
    work.start()
    for phase in range(FOUR):
        work.step(phase)
    work.finish()
    own = (coords[ZERO], coords[ONE], coords[TWO], core)
    for layer in range(TWO):
        last = layer * SLOT_ROWS + SHARD_ROWS
        grad[own + (pl.ds(last, ONE), slice(None))] = jnp.zeros((ONE, LANES), F32)
    total = square_sum(grad, coords, core, ZERO, SMALL_OFF + EIGHT)
    msg[ZERO] = jnp.broadcast_to(jnp.sum(total), (EIGHT, LANES))
    for n, device in enumerate([partner, neighbours[TWO], neighbours[ONE], neighbours[ZERO]]):
        copy = pltpu.make_async_remote_copy(src_ref=msg.at[n], dst_ref=box.at[n], send_sem=tiny_send.at[n], recv_sem=tiny_recv.at[n], device_id=(device,), device_id_type=MESH_ID)
        copy.start()
        copy.wait()
        msg[n + ONE] = msg[n] + box[n]
    stat_ref[ZERO] = msg[FOUR]
    stat_ref[ONE] = grad[own + (pl.ds(SMALL_OFF + EIGHT, EIGHT), slice(None))]
    for layer in range(TWO):
        gl_ref[layer] = grad[own + (pl.ds(layer * SLOT_ROWS, SLOT_ROWS), slice(None))]
    ghead_ref[...] = grad[own + (pl.ds(HEAD_OFF, TH), slice(None))]
    gsmall_ref[...] = grad[own + (pl.ds(SMALL_OFF, EIGHT), slice(None))]


def reduce_grads(flat, gh, gs, loss):
    vmem = pl.BlockSpec(memory_space=pltpu.VMEM)
    hbm = pl.BlockSpec(memory_space=pl.ANY)
    return pl.pallas_call(
        reduce_kernel,
        out_shape=(jax.ShapeDtypeStruct((TWO, SLOT_ROWS, LANES), F32), jax.ShapeDtypeStruct((TH, LANES), F32), jax.ShapeDtypeStruct((EIGHT, LANES), F32), jax.ShapeDtypeStruct((TWO, EIGHT, LANES), F32)),
        in_specs=[hbm, vmem, vmem, vmem],
        out_specs=(vmem,) * FOUR,
        scratch_shapes=[
            pltpu.VMEM((16640, LANES), F32),
            pltpu.VMEM((TWO, TWO, TWO, TWO, AG_ROWS, LANES), F32),
            pltpu.VMEM((TWO, TWO, TWO, AG_ROWS, LANES), F32),
            pltpu.VMEM((TWO, TWO, AG_ROWS, LANES), F32),
            pltpu.VMEM((TWO, AG_ROWS, LANES), F32),
            pltpu.VMEM((AG_ROWS, LANES), F32),
            pltpu.VMEM((FIVE, EIGHT, LANES), F32),
            pltpu.VMEM((FOUR, EIGHT, LANES), F32),
            pltpu.SemaphoreType.DMA((12,)),
            pltpu.SemaphoreType.DMA((12,)),
            pltpu.SemaphoreType.DMA,
            pltpu.SemaphoreType.DMA((FOUR,)),
            pltpu.SemaphoreType.DMA((FOUR,)),
        ],
        compiler_params=pltpu.CompilerParams(collective_id=ONE, has_side_effects=True, vmem_limit_bytes=VMEM_CAP),
        name='reduce_grads',
    )(flat, gh, gs, loss)

QUADS = 8
QROWS = 208
TOKENS = 49
ALL_ROWS = QUADS * QROWS
CHUNK = 256
BLOCK = 416
CLASSES = 1000
GLOBAL_IMAGES = 512.0
LN_EPS = 1e-6
GELU_A = 0.7978845608028654
GELU_B = GELU_A * 0.044715
HALF = 0.5
ROW_T2 = 98
INV49 = 81
LOW7 = 127
SLAB_VEC = 196
V_BT1 = 204
V_MIS = 206
STEP8 = 8


def mm(a, b):
    return jnp.dot(a, b, preferred_element_type=F32)


def mm_nt(a, b):
    return lax.dot_general(a, b, (((ONE,), (ONE,)), ((), ())), preferred_element_type=F32)


def iota(shape, axis):
    return lax.broadcasted_iota(jnp.int32, shape, axis)


def aligned(start, unit):
    return pl.multiple_of(start * unit, unit)


def stats(x):
    mean = jnp.mean(x, axis=-ONE, keepdims=True)
    centered = x - mean
    scale = lax.rsqrt(jnp.mean(centered * centered, axis=-ONE, keepdims=True) + LN_EPS)
    return centered * scale, scale


def fold8(x):
    return jnp.sum(x.reshape(x.shape[ZERO] // STEP8, STEP8, x.shape[ONE]), axis=ZERO)


def gelu_tanh(h):
    sq = h * h
    return sq, jnp.tanh(h * (GELU_A + GELU_B * sq))


def gelu(h):
    sq, t = gelu_tanh(h)
    half = HALF * h
    return (half + half * t).astype(BF16)


def gelu_both(h):
    sq, t = gelu_tanh(h)
    half = HALF * h
    slope = (HALF + HALF * t) + half * (F_ONE - t * t) * (GELU_A + (3.0 * GELU_B) * sq)
    return (half + half * t).astype(BF16), slope


def norm_back(xh, scale, gain, dy):
    dxh = dy * gain
    return scale * (dxh - jnp.mean(dxh, axis=-ONE, keepdims=True) - xh * jnp.mean(dxh * xh, axis=-ONE, keepdims=True))


def token_maps():
    s = iota((TOKEN_PAD, LANES), ZERO)
    lane = iota((TOKEN_PAD, LANES), ONE)
    j = ((lane - s) * INV49) & LOW7
    row = jnp.where(s < TOKENS, (j * TOKENS + s) >> SEVEN, -ONE)
    perm = (iota((LANES, LANES), ZERO) == ((iota((LANES, LANES), ONE) * TOKENS) & LOW7))
    return s, row, perm


def skew(x, s, left):
    for bit in range(SEVEN):
        amount = TWO ** bit
        x = jnp.where(((s >> bit) & ONE) == ONE, pltpu.roll(x, LANES - amount if left else amount, ONE), x)
    return x


def prep_layer(l, slab, vrow, bd, v2, ma1, mb1, ma2, mb2, col):
    for k in range(FOUR):
        lanes = slice(LANES * k, LANES * k + LANES)
        vrow[l, ZERO:ONE, lanes] = slab[l, SLAB_VEC + k:SLAB_VEC + k + ONE, :]
        vrow[l, ONE:TWO, lanes] = slab[l, SLAB_VEC + FOUR + k:SLAB_VEC + FIVE + k, :]
    lane = iota((IMAGES, LANES), ONE)
    cut = LANES - TOKENS
    v2[...] = jnp.where(lane < cut, pltpu.roll(slab[l, V_MIS:V_MIS + IMAGES, :], cut, ONE), pltpu.roll(slab[l, V_MIS + ONE:V_MIS + 33, :], cut, ONE))
    for row, first, count in ((TWO, ZERO, FOUR), (THREE, FOUR, FOUR), (FOUR, EIGHT, SIXTEEN), (FIVE, TWENTY_FOUR, FOUR)):
        for k in range(count):
            vrow[l, row:row + ONE, LANES * k:LANES * k + LANES] = v2[first + k:first + k + ONE, :]
    bd[...] = jnp.zeros_like(bd)
    for h in range(TWO):
        w = slab[l, pl.ds(h, TOKENS, stride=TWO), :]
        for i in range(FOUR):
            bd[TOKENS * i:TOKENS * i + TOKENS, TH * i + LANES * h:TH * i + LANES * h + LANES] = w
    mb1[l] = bd[ZERO:QROWS, :].astype(BF16)
    for h in range(TWO):
        for i in range(FOUR):
            bd[QVALID:QVALID + ONE, TH * i + LANES * h:TH * i + LANES * h + LANES] = slab[l, V_BT1 + h:V_BT1 + h + ONE, :]
    ma1[l] = bd[...].T[:, ZERO:QROWS].astype(BF16)
    bd[...] = jnp.zeros_like(bd)
    s, row, perm = token_maps()
    for h in range(TWO):
        def pick(r, acc):
            return jnp.where(row == r, slab[l, pl.ds(ROW_T2 + TOKENS * h + r, ONE), :], acc)
        x = skew(lax.fori_loop(ZERO, TOKENS, pick, jnp.zeros((TOKEN_PAD, LANES), F32)), s, True)
        w = mm(x.astype(BF16), perm.astype(BF16))[ZERO:TOKENS]
        for i in range(FOUR):
            bd[TOKENS * i:TOKENS * i + TOKENS, TH * i + LANES * h:TH * i + LANES * h + LANES] = w
    ma2[l] = bd[ZERO:QROWS, :].astype(BF16)
    mb2[l] = bd[...].T[:, ZERO:QROWS].astype(BF16)
    bias = jnp.where(iota((ONE, LANES), ONE) < TOKENS, slab[l, V_MIS:V_MIS + ONE, :], F_ZERO)
    wide = jnp.concatenate([jnp.broadcast_to(bias, (LANES, LANES)), jnp.zeros((LANES, LANES), F32)], axis=ONE)
    spread = wide
    for i in range(ONE, FOUR):
        spread = spread + pltpu.roll(wide, TOKENS * i, ONE)
    col[l] = spread.T[ZERO:QROWS, :]


def forward_layer(l, x_in, x_mid, x_out, vrow, ma1, ma2, col, w1, w2, uq, uch):
    def quad(q, carry):
        rows = pl.ds(aligned(q, QROWS), QROWS)
        xq = x_in[rows, :].astype(F32)
        n = token_input(xq, vrow, l)[TWO]
        for i in range(FOUR):
            uq[TH * i:TH * i + TH, :] = gelu(mm(ma1[l, TH * i:TH * i + TH, :], n))
        y = mm(ma2[l], uq[...])
        x1 = (xq + (y + jnp.concatenate([col[l]] * FOUR, axis=ONE))).astype(BF16)
        x_mid[rows, :] = x1
        x1 = x1.astype(F32)
        n2 = (stats(x1)[ZERO] * vrow[l, TWO:THREE, ZERO:CH] + vrow[l, THREE:FOUR, ZERO:CH]).astype(BF16)
        for c in range(FOUR):
            lanes = slice(CH * c, CH * c + CH)
            uch[:, lanes] = gelu(mm(n2, w1[l, :, lanes]) + vrow[l, FOUR:FIVE, lanes])
        x_out[rows, :] = (x1 + (mm(uch[...], w2[l]) + vrow[l, FIVE:SIX, ZERO:CH])).astype(BF16)
        return carry
    lax.fori_loop(ZERO, QUADS, quad, ZERO)


def token_input(xq, vrow, l):
    xh, scale = stats(xq)
    n = xh * vrow[l, ZERO:ONE, ZERO:CH] + vrow[l, ONE:TWO, ZERO:CH]
    return xh, scale, jnp.where(iota((QROWS, CH), ZERO) == QVALID, F_ONE, n).astype(BF16)


def image_of(shape, axis):
    c = iota(shape, axis)
    return jnp.where(c < QVALID, (c >= TOKENS).astype(jnp.int32) + (c >= TWO * TOKENS).astype(jnp.int32) + (c >= THREE * TOKENS).astype(jnp.int32), IMAGES)


def head_pass(x_out, labels, small, head, d, pool, srow, gsum, gh, gs, loss):
    for k in range(FOUR):
        lanes = slice(LANES * k, LANES * k + LANES)
        srow[ZERO:ONE, lanes] = small[k:k + ONE, :]
        srow[ONE:TWO, lanes] = small[FOUR + k:FIVE + k, :]
    for k in range(EIGHT):
        srow[TWO:THREE, LANES * k:LANES * k + LANES] = small[EIGHT + k:NINE + k, :]
    gain, shift = srow[ZERO:ONE, ZERO:CH], srow[ONE:TWO, ZERO:CH]
    pool[...] = jnp.zeros_like(pool)

    def quad(q, carry):
        xh, scale = stats(x_out[pl.ds(aligned(q, QROWS), QROWS), :].astype(F32))
        pick = (iota((IMAGES, QROWS), ZERO) == image_of((IMAGES, QROWS), ONE) + FOUR * q)
        pool[...] += mm(pick.astype(BF16), (xh * gain + shift).astype(BF16))
        return carry
    lax.fori_loop(ZERO, QUADS, quad, ZERO)
    pooled = (pool[...] / TOKENS).astype(BF16)
    real = iota((IMAGES, CLASS_PAD), ONE) < CLASSES
    logits = jnp.where(real, mm(pooled, head[...]) + srow[TWO:THREE, :], -1e30)
    top = jnp.max(logits, axis=-ONE, keepdims=True)
    log_norm = top + jnp.log(jnp.sum(jnp.exp(logits - top), axis=-ONE, keepdims=True))
    hit = iota((IMAGES, CLASS_PAD), ONE) == labels[:, ZERO:ONE]
    picked = jnp.sum(jnp.where(hit, logits, F_ZERO), axis=-ONE, keepdims=True)
    loss[...] = jnp.broadcast_to(jnp.sum(log_norm - picked), loss.shape)
    d_logits = (jnp.exp(logits - log_norm) - hit.astype(F32)) / GLOBAL_IMAGES
    d_bf = d_logits.astype(BF16)
    gh[...] = mm(pool_t(pooled), d_bf)
    d_pool = (mm_nt(d_bf, head[...]) / TOKENS).astype(BF16)
    gsum[...] = jnp.zeros_like(gsum)

    def back(q, carry):
        rows = pl.ds(aligned(q, QROWS), QROWS)
        xh, scale = stats(x_out[rows, :].astype(F32))
        pick = (iota((QROWS, IMAGES), ONE) == image_of((QROWS, IMAGES), ZERO) + FOUR * q)
        dy = mm(pick.astype(BF16), d_pool)
        gsum[ZERO] += fold8(dy * xh)
        gsum[ONE] += fold8(dy)
        d[rows, :] = norm_back(xh, scale, gain, dy)
        return carry
    lax.fori_loop(ZERO, QUADS, back, ZERO)
    g_gain = jnp.sum(gsum[ZERO], axis=ZERO, keepdims=True)
    g_shift = jnp.sum(gsum[ONE], axis=ZERO, keepdims=True)
    g_bias = jnp.sum(d_logits, axis=ZERO, keepdims=True)
    for k in range(FOUR):
        lanes = slice(LANES * k, LANES * k + LANES)
        gs[k:k + ONE, :] = g_gain[:, lanes]
        gs[FOUR + k:FIVE + k, :] = g_shift[:, lanes]
    for k in range(EIGHT):
        gs[EIGHT + k:NINE + k, :] = g_bias[:, LANES * k:LANES * k + LANES]


def pool_t(pooled):
    return pooled.astype(F32).T.astype(BF16)


def channel_back(l, x_mid, d, vrow, w1, w2, n2, dbf, n2t, dt, uh, dh, dn2, flat, gsum, gb1):
    gsum[...] = jnp.zeros_like(gsum)
    gb1[...] = jnp.zeros_like(gb1)

    def quad(q, carry):
        rows = pl.ds(aligned(q, QROWS), QROWS)
        n2[rows, :] = (stats(x_mid[rows, :].astype(F32))[ZERO] * vrow[l, TWO:THREE, ZERO:CH] + vrow[l, THREE:FOUR, ZERO:CH]).astype(BF16)
        dq = d[rows, :]
        gsum[FOUR] += fold8(dq)
        dbf[rows, :] = dq.astype(BF16)
        dn2[rows, :] = jnp.zeros((QROWS, CH), F32)
        return carry
    lax.fori_loop(ZERO, QUADS, quad, ZERO)
    for k in range(ALL_ROWS // LANES):
        lanes = slice(LANES * k, LANES * k + LANES)
        n2t[:, lanes] = n2[lanes, :].T
        dt[:, lanes] = dbf[lanes, :].T

    def chunk(c, carry):
        lanes = pl.ds(aligned(c, CHUNK), CHUNK)

        def block(b, inner):
            rows = pl.ds(aligned(b, BLOCK), BLOCK)
            u, slope = gelu_both(mm(n2[rows, :], w1[l, :, lanes]) + vrow[l, FOUR:FIVE, lanes])
            uh[rows, :] = u
            dhid = mm_nt(dbf[rows, :], w2[l, lanes, :]).astype(BF16).astype(F32) * slope
            gb1[:, lanes] += fold8(dhid)
            dhid = dhid.astype(BF16)
            dh[rows, :] = dhid
            dn2[rows, :] += mm_nt(dhid, w1[l, :, lanes])
            return inner
        lax.fori_loop(ZERO, ALL_ROWS // BLOCK, block, ZERO)
        g1 = mm(n2t[...], dh[...])
        for r in range(CH // STEP8):
            for k in range(TWO):
                flat[pl.ds(ROW_C1 + LANES * r + k + TWO * c, STEP8, stride=SIXTEEN), :] = g1[STEP8 * r:STEP8 * r + STEP8, LANES * k:LANES * k + LANES]
        g2 = mm(dt[...], uh[...]).T
        for r in range(CHUNK // STEP8):
            for k in range(FOUR):
                flat[pl.ds(ROW_C2 + FOUR * (STEP8 * r) + k + FOUR * CHUNK * c, STEP8, stride=FOUR), :] = g2[STEP8 * r:STEP8 * r + STEP8, LANES * k:LANES * k + LANES]
        return carry
    lax.fori_loop(ZERO, HID // CHUNK, chunk, ZERO)


def token_back(l, x_in, x_mid, d, vrow, dn2, ma1, mb1, ma2, mb2, uq, dq_ref, acc1, acc2, rowsum, colsum, gsum):
    for ref in (acc1, acc2, rowsum, colsum):
        ref[...] = jnp.zeros_like(ref)

    def quad(q, carry):
        rows = pl.ds(aligned(q, QROWS), QROWS)
        xh, scale = stats(x_mid[rows, :].astype(F32))
        dy = dn2[rows, :].astype(BF16).astype(F32)
        gsum[TWO] += fold8(dy * xh)
        gsum[THREE] += fold8(dy)
        d_after = norm_back(xh, scale, vrow[l, TWO:THREE, ZERO:CH], dy) + d[rows, :]
        part = d_after[:, ZERO:LANES]
        for k in range(ONE, FOUR):
            part = part + d_after[:, LANES * k:LANES * k + LANES]
        colsum[ZERO:QROWS, :] += part
        d_bf = d_after.astype(BF16)
        xh, scale, n = token_input(x_in[rows, :].astype(F32), vrow, l)
        for i in range(FOUR):
            part = slice(TH * i, TH * i + TH)
            u, slope = gelu_both(mm(ma1[l, part, :], n))
            uq[part, :] = u
            dhid = mm(mb2[l, part, :], d_bf).astype(BF16).astype(F32) * slope
            total = dhid[:, ZERO:LANES]
            for k in range(ONE, FOUR):
                total = total + dhid[:, LANES * k:LANES * k + LANES]
            rowsum[part, :] += total
            dq_ref[part, :] = dhid.astype(BF16)
        acc1[...] += mm_nt(n, dq_ref[...])
        acc2[...] += mm_nt(d_bf, uq[...])
        dy = mm(mb1[l], dq_ref[...]).astype(BF16).astype(F32)
        gsum[ZERO] += fold8(dy * xh)
        gsum[ONE] += fold8(dy)
        d[rows, :] = norm_back(xh, scale, vrow[l, ZERO:ONE, ZERO:CH], dy) + d_after
        return carry
    lax.fori_loop(ZERO, QUADS, quad, ZERO)


def small_flat(l, flat, acc1, acc2, rowsum, colsum, gsum, gb1, v2):
    g = sum_images(acc1)
    for h in range(TWO):
        flat[pl.ds(h, TOKENS, stride=TWO), :] = g[:, LANES * h:LANES * h + LANES]
    g = sum_images(acc2)
    s, row, perm = token_maps()
    for h in range(TWO):
        padded = jnp.concatenate([g[:, LANES * h:LANES * h + LANES], jnp.zeros((SEVEN, LANES), F32)], axis=ZERO)
        x = skew(lax.dot_general(padded, perm.astype(F32), (((ONE,), (ONE,)), ((), ())), precision=lax.Precision.HIGHEST, preferred_element_type=F32), s, False)

        def place_row(r, carry):
            flat[pl.ds(ROW_T2 + TOKENS * h + r, ONE), :] = jnp.sum(jnp.where(row == r, x, F_ZERO), axis=ZERO, keepdims=True)
            return carry
        lax.fori_loop(ZERO, TOKENS, place_row, ZERO)
    flat[ROW_VEC:FLAT_ROWS + SIXTEEN, :] = jnp.zeros((FLAT_ROWS + SIXTEEN - ROW_VEC, LANES), F32)
    for n in range(TWO):
        v = jnp.sum(gsum[n], axis=ZERO, keepdims=True)
        for k in range(FOUR):
            flat[ROW_VEC + FOUR * n + k:ROW_VEC + FOUR * n + k + ONE, :] = v[:, LANES * k:LANES * k + LANES]
    t = jnp.sum(rowsum[...].T, axis=ZERO, keepdims=True)
    t = t[:, ZERO:TH] + t[:, TH:TWO * TH] + t[:, TWO * TH:THREE * TH] + t[:, THREE * TH:FOUR * TH]
    for h in range(TWO):
        flat[ROW_VEC + EIGHT + h:ROW_VEC + NINE + h, :] = t[:, LANES * h:LANES * h + LANES]
    v2[...] = jnp.zeros_like(v2)
    lists = [(jnp.sum(gsum[TWO], axis=ZERO, keepdims=True), ZERO, FOUR), (jnp.sum(gsum[THREE], axis=ZERO, keepdims=True), FOUR, FOUR), (jnp.sum(gb1[...], axis=ZERO, keepdims=True), EIGHT, SIXTEEN), (jnp.sum(gsum[FOUR], axis=ZERO, keepdims=True), TWENTY_FOUR, FOUR)]
    for v, first, count in lists:
        for k in range(count):
            v2[first + k:first + k + ONE, :] = v[:, LANES * k:LANES * k + LANES]
    turned = pltpu.roll(v2[...], TOKENS, ONE)
    t = jnp.broadcast_to(jnp.sum(colsum[...].T, axis=ZERO, keepdims=True), (STEP8, TWO * LANES))
    b2 = t
    for i in range(ONE, FOUR):
        b2 = b2 + pltpu.roll(t, TWO * LANES - TOKENS * i, ONE)
    before = jnp.concatenate([b2[ZERO:ONE, ZERO:LANES], turned[ZERO:LAST_IMAGE, :]], axis=ZERO)
    merged = jnp.where(iota((IMAGES, LANES), ONE) < TOKENS, before, turned)
    flat[ROW_VEC + TEN:ROW_VEC + 42, :] = merged


def sum_images(acc):
    g = acc[ZERO:TOKENS, ZERO:TH]
    for i in range(ONE, FOUR):
        g = g + acc[TOKENS * i:TOKENS * i + TOKENS, TH * i:TH * i + TH]
    return g


def step_kernel(x0, labels, w1, w2, slab, head, small, flat_out, gh, gs, loss, x1, x2, x3, x4, d, dn2, n2, dbf, n2t, dt, uh, dh, uq, dq_ref, uch, ma1, mb1, ma2, mb2, col, vrow, v2, bd, srow, pool, gsum, gb1, acc1, acc2, rowsum, colsum, flat, sem):
    for l in range(TWO):
        prep_layer(l, slab, vrow, bd, v2, ma1, mb1, ma2, mb2, col)
    forward_layer(ZERO, x0, x1, x2, vrow, ma1, ma2, col, w1, w2, uq, uch)
    forward_layer(ONE, x2, x3, x4, vrow, ma1, ma2, col, w1, w2, uq, uch)
    head_pass(x4, labels, small, head, d, pool, srow, gsum, gh, gs, loss)
    for l, x_in, x_mid in ((ONE, x2, x3), (ZERO, x0, x1)):
        channel_back(l, x_mid, d, vrow, w1, w2, n2, dbf, n2t, dt, uh, dh, dn2, flat, gsum, gb1)
        token_back(l, x_in, x_mid, d, vrow, dn2, ma1, mb1, ma2, mb2, uq, dq_ref, acc1, acc2, rowsum, colsum, gsum)
        small_flat(l, flat, acc1, acc2, rowsum, colsum, gsum, gb1, v2)
        copy = pltpu.make_async_copy(flat, flat_out.at[l], sem)
        copy.start()
        copy.wait()


def local_step(x0, labels, w1, w2, slab, head, small):
    vmem = pl.BlockSpec(memory_space=pltpu.VMEM)
    act = pltpu.VMEM((ALL_ROWS, CH), BF16)
    wide = pltpu.VMEM((ALL_ROWS, CH), F32)
    across = pltpu.VMEM((CH, ALL_ROWS), BF16)
    part = pltpu.VMEM((ALL_ROWS, CHUNK), BF16)
    tok = pltpu.VMEM((FOUR * TH, CH), BF16)
    tall = pltpu.VMEM((TWO, FOUR * TH, QROWS), BF16)
    flat_mat = pltpu.VMEM((TWO, QROWS, FOUR * TH), BF16)
    acc = pltpu.VMEM((QROWS, FOUR * TH), F32)
    return pl.pallas_call(
        step_kernel,
        out_shape=(jax.ShapeDtypeStruct((TWO, FLAT_ROWS + SIXTEEN, LANES), F32), jax.ShapeDtypeStruct((CH, CLASS_PAD), F32), jax.ShapeDtypeStruct((SIXTEEN, LANES), F32), jax.ShapeDtypeStruct((STEP8, LANES), F32)),
        in_specs=[vmem] * SEVEN,
        out_specs=(pl.BlockSpec(memory_space=pl.ANY), vmem, vmem, vmem),
        scratch_shapes=[act, act, act, act, wide, wide, act, act, across, across, part, part, tok, tok, pltpu.VMEM((QROWS, HID), BF16),
                        tall, flat_mat, flat_mat, tall, pltpu.VMEM((TWO, QROWS, LANES), F32), pltpu.VMEM((TWO, STEP8, HID), F32), pltpu.VMEM((IMAGES, LANES), F32), pltpu.VMEM((TWO * LANES, FOUR * TH), F32),
                        pltpu.VMEM((STEP8, CLASS_PAD), F32), pltpu.VMEM((IMAGES, CH), F32), pltpu.VMEM((FIVE, STEP8, CH), F32), pltpu.VMEM((STEP8, HID), F32), acc, acc,
                        pltpu.VMEM((FOUR * TH, LANES), F32), pltpu.VMEM((TWO * LANES, LANES), F32), pltpu.VMEM((FLAT_ROWS + SIXTEEN, LANES), F32), pltpu.SemaphoreType.DMA],
        compiler_params=pltpu.CompilerParams(vmem_limit_bytes=VMEM_CAP),
        name='local_step',
    )(x0, labels, w1, w2, slab, head, small)


LEARN_RATE = 0.003
BETA_ONE = 0.9
BETA_TWO = 0.999
ADAM_EPS = 1e-8
WEIGHT_DECAY = 0.03
ADAM_STEP = 10


def adam_update(master, gradient, moment, second, decay_rate):
    moment_new = BETA_ONE * moment + (F_ONE - BETA_ONE) * gradient
    second_new = BETA_TWO * second + (F_ONE - BETA_TWO) * gradient * gradient
    m_hat = moment_new / (F_ONE - BETA_ONE ** ADAM_STEP)
    v_hat = second_new / (F_ONE - BETA_TWO ** ADAM_STEP)
    master_new = master - LEARN_RATE * (m_hat / (jnp.sqrt(v_hat) + ADAM_EPS) + decay_rate * master)
    return master_new, moment_new, second_new


def solution(mesh):
    row_spec = P('fsdp')
    layer_spec = P(None, 'fsdp')
    in_specs = (row_spec, row_spec, layer_spec, row_spec, row_spec, layer_spec, row_spec, row_spec, layer_spec, row_spec, row_spec)
    out_specs = (P(),) + in_specs[TWO:]

    def device_step(act_in, labels, layer_p, head_w, small_p, layer_m, head_m, small_m, layer_v, head_v, small_v):
        mat_len = ROW_VEC * LANES
        quads = jnp.pad(act_in.reshape(QUADS, QVALID, CH), ((ZERO, ZERO), (ZERO, QROWS - QVALID), (ZERO, ZERO))).reshape(ALL_ROWS, CH)
        layer_bf = jnp.pad(layer_p.astype(BF16).reshape(TWO, SHARD_ROWS, LANES), ((ZERO, ZERO), (ZERO, ONE), (ZERO, ZERO)))
        head_bf = jnp.pad(head_w.astype(BF16), ((ZERO, ZERO), (ZERO, CLASS_PAD - CLASSES))).reshape(IMAGES, EIGHT, LANES).transpose(ONE, ZERO, TWO).reshape(TH, LANES)
        small_bf = jnp.pad(small_p.astype(BF16).reshape(ONE, LANES), ((ZERO, 15), (ZERO, ZERO)))
        weights = gather_weights(jnp.concatenate([layer_bf.reshape(TWO * SLOT_ROWS, LANES), head_bf, small_bf]))
        local = local_step(quads, jnp.broadcast_to(labels[:, None], (IMAGES, LANES)), *weights)
        gl, ghead, gsmall, stat = reduce_grads(*local)
        layer_g = gl[:, :SHARD_ROWS].reshape(TWO, SHARD_ROWS * LANES)
        head_g = ghead.reshape(EIGHT, IMAGES, LANES).transpose(ONE, ZERO, TWO).reshape(IMAGES, CLASS_PAD)[:, :CLASSES]
        small_g = gsmall[ZERO]
        loss_value = stat[ONE, ZERO, ZERO] / GLOBAL_IMAGES
        clip_scale = F_ONE / jnp.maximum(F_ONE, jnp.sqrt(stat[ZERO, ZERO, ZERO]))
        shard_len = layer_p.shape[ONE]
        flat_pos = lax.axis_index('fsdp') * shard_len + jnp.arange(shard_len)
        layer_decay = jnp.where(flat_pos < mat_len, WEIGHT_DECAY, F_ZERO)[None, :]
        new_lp, new_lm, new_lv = adam_update(layer_p, layer_g * clip_scale, layer_m, layer_v, layer_decay)
        new_hw, new_hm, new_hv = adam_update(head_w, head_g * clip_scale, head_m, head_v, WEIGHT_DECAY)
        new_sp, new_sm, new_sv = adam_update(small_p, small_g * clip_scale, small_m, small_v, F_ZERO)
        return (loss_value, new_lp, new_hw, new_sp, new_lm, new_hm, new_sm, new_lv, new_hv, new_sv)

    return jax.shard_map(device_step, mesh=mesh, in_specs=in_specs, out_specs=out_specs, check_vma=False)
```

time: 467 us -> 392 us (0.84); the launches traced: 458 us -> 392 us
  matrix products: 218 us -> 0 us
  Pallas kernels: 173 us -> 367 us
  other arithmetic: 52.7 us -> 11.9 us
    dot_general x27 -> x0, matrix products: 218 us -> none  [the longest x2 35.7 us: layer_backward(): jnp.einsum('bsc,js->bcj', d_after_bf, w_tok2, preferred_element_type=jnp....]
    pallas_call x2 -> x3, Pallas kernels: 173 us -> 367 us  [the longest x1 200 us: local_step(): pl.pallas_call(step_kernel, out_shape=(jax.ShapeDtypeStruct((TWO, FLAT_RO...]
    reduce_sum x19 -> x0, other arithmetic: 24.2 us -> none  [the longest x9 10.3 us: layer_norm(): var_val = jnp.mean(jnp.square(x_f - mean_val), axis=-1, keepdims=True)]
    another operation x6 -> x0, other arithmetic: 10.3 us -> none  [the longest x1 4.19 us: device_step(): jnp.stack([grads[0][1], grads[1][1]])]
where the time goes in v2:
time: 392 us
  Pallas kernels  367 us (94%)
  other arithmetic  11.9 us (3%)
  local copies, waits for them, and re-layouts  9.42 us (2%)
    pallas_call x1, Pallas kernels, local_step(): pl.pallas_call(step_kernel, out_shape=(jax.ShapeDtypeStruct((TWO, FLAT_RO...  200 us
    pallas_call x1, Pallas kernels, reduce_grads(): pl.pallas_call(reduce_kernel, out_shape=(jax.ShapeDtypeStruct((TWO, SLOT_...  106 us
    pallas_call x1, Pallas kernels, gather_weights(): pl.pallas_call(gather_kernel, out_shape=(jax.ShapeDtypeStruct((TWO, CH, H...  60.6 us
    sub x3, other arithmetic, adam_update(): master - LEARN_RATE * (m_hat / (jnp.sqrt(v_hat) + ADAM_EPS) + decay_rate...  9.46 us

profile of v2, /device:TPU:0, one launch (start us, length us, event | category | flops | bytes accessed | tf_op | source)
XLA Modules:
  0.0 391.5 jit_solution(17876684124799296487)
XLA Ops:
  0.6 1.5 convert_element_type.17
  2.1 0.0 copy-start.3
  2.1 0.0 copy-start.5
  2.1 0.9 reshape.68
  3.1 0.0 copy-done.3
  3.1 0.0 copy-done.5
  3.2 0.9 fusion.3.pack_ref
  4.0 60.6 %gather_weights.1 = (bf16[2,512,2048]{2,1,0:T(8,128)(2,1)}, bf16[2,2048,512]{2,1,0:T(8,128)(2,1)}, f32[2,240,128]{2,1,0:T(8,128)}, bf16[512,1024]{1,0:T(8,128)(2,1)}, f32[16,128]{1,0:T(8,128)}) custom-call(bf16[2352,128]{1,0:T(8,128)(2,1)} %fusion.3.pack_ref), custom_call_target="tpu_custom_call" | custom-call | tf_op jit(solution)/shard_map/gather_weights/pallas_call | solution.py:182
  64.6 2.3 copy.23
  67.0 0.5 reshape.66
  67.4 0.0 copy-start.4
  67.5 1.4 pad.16
  68.8 0.0 copy-done.4
  68.8 0.7 broadcast_in_dim.15.labels
  69.5 199.9 %local_step.1 = (f32[2,16640,128]{2,1,0:T(8,128)}, f32[512,1024]{1,0:T(8,128)}, f32[16,128]{1,0:T(8,128)}, f32[8,128]{1,0:T(8,128)}) custom-call(bf16[1664,512]{1,0:T(8,128)(2,1)} %bitcast.37, s32[32,128]{1,0:T(8,128)} %broadcast_in_dim.15.labels, bf16[2,512,2048]{2,1,0:T(8,128)(2,1)} %get-tuple-element.23.w1, bf16[2,2048,512]{2,1,0:T(8,128)(2,1)} %get-tuple-element.24.w2, ...), custom_call_target="tpu_custom_call" | custom-call | tf_op jit(solution)/shard_map/local_step/pallas_call | solution.py:726
  269.4 0.0 copy-start.6
  269.4 0.0 copy-start.7
  269.4 106.4 %reduce_grads.1 = (f32[2,1040,128]{2,1,0:T(8,128)}, f32[256,128]{1,0:T(8,128)}, f32[8,128]{1,0:T(8,128)}, f32[2,8,128]{2,1,0:T(8,128)}) custom-call(f32[2,16640,128]{2,1,0:T(8,128)} %get-tuple-element.28.flat_hbm, f32[512,1024]{1,0:T(8,128)} %get-tuple-element.29.gh_ref, f32[16,128]{1,0:T(8,128)} %get-tuple-element.30.gs_ref, ...), custom_call_target="tpu_custom_call" | custom-call | tf_op jit(solution)/shard_map/reduce_grads/pallas_call | solution.py:338
  375.8 0.0 copy-start.1
  375.8 1.3 fusion.13
  377.8 0.0 copy-done.6
  377.8 0.0 copy-done.7
  377.8 1.2 multiply_subtract_fusion.2
  379.1 0.9 copy.35
  380.0 1.8 multiply_subtract_fusion.1
  381.8 0.0 copy-done.1
  381.8 0.0 copy-start
  381.8 0.0 copy-start.2
  381.8 0.1 multiply_bitcast_fusion
  381.9 0.1 fusion.4
  382.0 1.1 copy-done
  383.0 0.3 copy-done.2
  383.4 6.4 %multiply_subtract_fusion = (f32[2,132992]{1,0:T(2,128)}, f32[2,132992]{1,0:T(2,128)}, f32[2,132992]{1,0:T(2,128)}) fusion(f32[2,132992]{1,0:T(2,128)S(1)} %copy-done, f32[132992]{0:T(1024)S(1)} %fusion.4, f32[1,2,1039,128]{3,2,1,0:T(8,128)S(1)} %multiply_bitcast_fusion, f32[2,132992]{1,0:T(2,128)S(1)} %copy-done.2, f32[2,132992]{1,0:T(2,128)} %param.19), kind=kLoop, calls=%fused_computation.7 | loop fusion | flops 3989760 | bytes 7979520 | tf_op jit(solution)/shard_map/sub | solution.py:753
  (4 shorter events, 0.1 us)
Async XLA Ops:
  2.1 1.0 copy-start.3
  2.1 1.0 copy-start.5
  67.4 1.4 copy-start.4
  269.4 108.4 %copy-start.6 = (f32[128]{0:T(128)S(1)}, f32[128]{0:T(128)}, u32[]{:S(2)}) copy-start(f32[128]{0:T(128)} %param.18) | copy-start | bytes 1540
  269.4 108.4 %copy-start.7 = (f32[128]{0:T(128)S(1)}, f32[128]{0:T(128)}, u32[]{:S(2)}) copy-start(f32[128]{0:T(128)} %param.21) | copy-start | bytes 1540
  375.8 6.0 %copy-start.1 = (f32[2,1040,128]{2,1,0:T(8,128)S(1)}, f32[2,1040,128]{2,1,0:T(8,128)}, u32[]{:S(2)}) copy-start(f32[2,1040,128]{2,1,0:T(8,128)} %get-tuple-element.33) | copy-start | bytes 3194884
  381.8 1.2 copy-start
  381.8 1.5 copy-start.2

commit v3 on v2

--- a/solution.py
+++ b/solution.py
@@ -35,7 +35,6 @@
 MESH_ID = pl.DeviceIdType.MESH
 F32 = jnp.float32
 BF16 = jnp.bfloat16
-VMEM_CAP = 64 * 1024 * 1024 - 128 * 1024
 
 SHARD_ROWS = 1039
 SLOT_ROWS = 1040
@@ -47,7 +46,7 @@
 HEAD_OFF = 2 * SLOT_ROWS
 SMALL_OFF = HEAD_OFF + 256
 AG_ROWS = SMALL_OFF + 16
-RS_ROWS = SMALL_OFF + 8
+HEAD_ROWS = 272
 ORDERS = ((2, 1, 0), (1, 0, 2), (0, 2, 1))
 AXIS_STEP = (8, 4, 2)
 
@@ -122,14 +121,27 @@
                 self.link(group, phase).wait_send()
 
 
-def unflatten_layer(gath, layer, flat, w1_ref, w2_ref, slab_ref):
+def slot_of(dev):
+    return dev // EIGHT, (dev // FOUR) % TWO, (dev // TWO) % TWO, dev % TWO
+
+
+def unflatten_layer(gath, layer, flat, stage, stage_sem, w1_ref, w2_ref, slab_ref):
     base = layer * SLOT_ROWS
 
+    def fetch(dev):
+        z, y, x, core = slot_of(dev)
+        return pltpu.make_async_copy(gath.at[z, y, x, core, pl.ds(base, SLOT_ROWS), :], stage.at[dev % TWO], stage_sem.at[dev % TWO])
+    fetch(ZERO).start()
+
     def spread(dev, carry):
-        z, y, x, core = dev // EIGHT, (dev // FOUR) % TWO, (dev // TWO) % TWO, dev % TWO
+        fetch(dev).wait()
+
+        @pl.when(dev < 15)
+        def _():
+            fetch(dev + ONE).start()
 
         def chunk(k, inner):
-            block = gath[z, y, x, core, pl.ds(base + SIXTEEN * k, SIXTEEN), :]
+            block = stage[dev % TWO, pl.ds(pl.multiple_of(SIXTEEN * k, SIXTEEN), SIXTEEN), :]
             flat[pl.ds(dev * SHARD_ROWS + SIXTEEN * k, SIXTEEN), :] = block.astype(F32)
             return inner
         return lax.fori_loop(ZERO, SLOT_ROWS // SIXTEEN, chunk, carry, unroll=FIVE)
@@ -147,59 +159,45 @@
             block = flat[pl.ds(ROW_C2 + SIXTY_FOUR * rb + j, SIXTEEN, stride=FOUR), :]
             w2_ref[layer, pl.ds(pl.multiple_of(SIXTEEN * rb, SIXTEEN), SIXTEEN), LANES * j:LANES * j + LANES] = block.astype(BF16)
         return carry
-    lax.fori_loop(ZERO, LANES, second, ZERO)
+    lax.fori_loop(ZERO, LANES, second, ZERO, unroll=FOUR)
     slab_ref[layer, ZERO:QVALID, :] = flat[ZERO:QVALID, :]
     slab_ref[layer, QVALID:240, :] = flat[ROW_VEC:FLAT_ROWS, :]
 
 
-def gather_kernel(pack_ref, w1_ref, w2_ref, slab_ref, head_ref, small_ref, gath, flat, send_sem, recv_sem, load_sem):
-    where = place()
-    me, coords, core, neighbours, partner = where
-    load = pltpu.make_async_copy(pack_ref, gath.at[coords[ZERO], coords[ONE], coords[TWO], core], load_sem)
-    load.start()
-    enter_barrier(neighbours, partner)
-    load.wait()
-    third = AG_ROWS // THREE
-    work = Gather(gath, where, [(third * g, third) for g in range(THREE)], send_sem, recv_sem, ZERO)
-    work.start()
-    for phase in range(THREE):
-        work.step(phase)
-    work.finish()
-    for layer in range(TWO):
-        unflatten_layer(gath, layer, flat, w1_ref, w2_ref, slab_ref)
-
-    def spread_head(dev, carry):
-        z, y, x, own = dev // EIGHT, (dev // FOUR) % TWO, (dev // TWO) % TWO, dev % TWO
+def unflatten_head(gath, stage, stage_sem, head_ref, small_ref):
+    def fetch(dev):
+        z, y, x, core = slot_of(dev)
+        return pltpu.make_async_copy(gath.at[z, y, x, core, pl.ds(HEAD_OFF, HEAD_ROWS), :], stage.at[dev % TWO, pl.ds(ZERO, HEAD_ROWS), :], stage_sem.at[dev % TWO])
+    fetch(ZERO).start()
+
+    def spread(dev, carry):
+        fetch(dev).wait()
+
+        @pl.when(dev < 15)
+        def _():
+            fetch(dev + ONE).start()
         for j in range(EIGHT):
-            head_ref[pl.ds(pl.multiple_of(IMAGES * dev, IMAGES), IMAGES), LANES * j:LANES * j + LANES] = gath[z, y, x, own, pl.ds(HEAD_OFF + IMAGES * j, IMAGES), :]
-        small_ref[pl.ds(dev, ONE), :] = gath[z, y, x, own, pl.ds(SMALL_OFF, SIXTEEN), :].astype(F32)[ZERO:ONE, :]
-        return carry
-    lax.fori_loop(ZERO, SIXTEEN, spread_head, ZERO)
-
-
-def gather_weights(pack):
-    vmem = pl.BlockSpec(memory_space=pltpu.VMEM)
-    return pl.pallas_call(
-        gather_kernel,
-        out_shape=(jax.ShapeDtypeStruct((TWO, CH, HID), BF16), jax.ShapeDtypeStruct((TWO, HID, CH), BF16), jax.ShapeDtypeStruct((TWO, SLAB_ROWS, LANES), F32), jax.ShapeDtypeStruct((CH, CLASS_PAD), BF16), jax.ShapeDtypeStruct((SIXTEEN, LANES), F32)),
-        in_specs=[vmem],
-        out_specs=(vmem,) * FIVE,
-        scratch_shapes=[
-            pltpu.VMEM((TWO, TWO, TWO, TWO, AG_ROWS, LANES), BF16),
-            pltpu.VMEM((16640, LANES), F32),
-            pltpu.SemaphoreType.DMA((21,)),
-            pltpu.SemaphoreType.DMA((21,)),
-            pltpu.SemaphoreType.DMA,
-        ],
-        compiler_params=pltpu.CompilerParams(collective_id=ZERO, has_side_effects=True, vmem_limit_bytes=VMEM_CAP),
-        name='gather_weights',
-    )(pack)
+            head_ref[pl.ds(pl.multiple_of(IMAGES * dev, IMAGES), IMAGES), LANES * j:LANES * j + LANES] = stage[dev % TWO, IMAGES * j:IMAGES * j + IMAGES, :]
+        small_ref[pl.ds(dev, ONE), :] = stage[dev % TWO, TH:272, :].astype(F32)[ZERO:ONE, :]
+        return carry
+    lax.fori_loop(ZERO, SIXTEEN, spread, ZERO)
 
 
 class Reduce:
-    def __init__(self, buf, temps, where, row_groups, send_sem, recv_sem, sem0):
-        self.buf, self.temps, self.where, self.groups = buf, temps, where, row_groups
-        self.send_sem, self.recv_sem, self.sem0 = send_sem, recv_sem, sem0
+    def __init__(self, flat, pitch, rows, groups, out, out_row, bufs, where, sems):
+        self.flat, self.pitch, self.rows, self.groups, self.out, self.out_row = flat, pitch, rows, groups, out, out_row
+        self.leaving, self.temps = bufs[ZERO], bufs[ONE:]
+        self.where = where
+        self.send_sem, self.recv_sem = sems
+
+    def spread(self):
+        me, coords, core, neighbours, partner = self.where
+
+        def chunk(k, carry):
+            for n in range(EIGHT):
+                self.leaving[n // FOUR, (n // TWO) % TWO, n % TWO, pl.ds(pl.multiple_of(EIGHT * k, EIGHT), EIGHT), :] = self.flat[pl.ds(self.pitch * (TWO * n + ONE - core) + EIGHT * k, EIGHT), :]
+            return carry
+        lax.fori_loop(ZERO, self.rows // EIGHT, chunk, ZERO)
 
     def views(self, group, phase):
         me, coords, core, neighbours, partner = self.where
@@ -207,30 +205,28 @@
         order = ORDERS[group]
         if phase == ZERO:
             free = (ZERO, ONE, TWO)
-            leave = slot_view(self.buf, coords, ONE - core, free, row0, rows)
+            leave = self.leaving.at[:, :, :, pl.ds(row0, rows), :]
             device = partner
-            stay = coords
         else:
             axis = order[phase - ONE]
             free = tuple(a for a in range(THREE) if a in order[phase:])
-            far = list(coords)
-            far[axis] = ONE - coords[axis]
-            leave = slot_view(self.buf, far, core, free, row0, rows)
+            index = [pl.ds(ZERO, TWO) if a in free else coords[a] for a in range(THREE)]
+            index[axis] = ONE - coords[axis]
+            leave = self.temps[ZERO].at[index[ZERO], index[ONE], index[TWO], pl.ds(row0, rows), :]
             device = neighbours[axis]
-            stay = coords
         land = self.temps[phase].at[(slice(None),) * len(free) + (pl.ds(row0, rows), slice(None))]
-        return leave, land, device, free, stay
+        return leave, land, device, free
 
     def copy(self, group, phase):
-        leave, land, device, free, stay = self.views(group, phase)
-        sem = self.sem0 + group * FOUR + phase
+        leave, land, device, free = self.views(group, phase)
+        sem = group * FOUR + phase
         return pltpu.make_async_remote_copy(src_ref=leave, dst_ref=land, send_sem=self.send_sem.at[sem], recv_sem=self.recv_sem.at[sem], device_id=(device,), device_id_type=MESH_ID)
 
     def add(self, group, phase):
         me, coords, core, neighbours, partner = self.where
-        leave, land, device, free, stay = self.views(group, phase)
+        free = self.views(group, phase)[THREE]
         row0, rows = self.groups[group]
-        temp = self.temps[phase]
+        total, temp = self.temps[ZERO], self.temps[phase]
         count = TWO ** len(free)
         per = max(ONE, EIGHT // count)
         while rows % (EIGHT * per):
@@ -246,12 +242,20 @@
                         bit = (n // TWO ** (len(free) - ONE - pos)) % TWO
                         index[a] = bit
                         bits.append(bit)
-                    target = (index[ZERO], index[ONE], index[TWO], core, pl.ds(start, EIGHT), slice(None))
-                    self.buf[target] = self.buf[target] + temp[tuple(bits) + (pl.ds(start, EIGHT), slice(None))]
+                    target = (index[ZERO], index[ONE], index[TWO], pl.ds(start, EIGHT), slice(None))
+                    if phase == ZERO:
+                        value = total[target] + self.flat[pl.ds(self.pitch * (TWO * n + core) + start, EIGHT), :]
+                    else:
+                        value = total[target] + temp[tuple(bits) + (pl.ds(start, EIGHT), slice(None))]
+                    if phase == THREE:
+                        self.out[pl.ds(pl.multiple_of(self.out_row + start, EIGHT), EIGHT), :] = value
+                    else:
+                        total[target] = value
             return carry
         lax.fori_loop(ZERO, rows // (EIGHT * per), chunk, ZERO)
 
     def start(self):
+        self.spread()
         for group in range(THREE):
             self.copy(group, ZERO).start()
 
@@ -268,96 +272,12 @@
                 self.copy(group, phase).wait_send()
 
 
-def spread_layer(layer, flat, grad):
-    base = layer * SLOT_ROWS
-
-    def spread(dev, carry):
-        z, y, x, core = dev // EIGHT, (dev // FOUR) % TWO, (dev // TWO) % TWO, dev % TWO
-
-        def chunk(k, inner):
-            grad[z, y, x, core, pl.ds(pl.multiple_of(base + EIGHT * k, EIGHT), EIGHT), :] = flat[pl.ds(dev * SHARD_ROWS + EIGHT * k, EIGHT), :]
-            return inner
-        return lax.fori_loop(ZERO, SLOT_ROWS // EIGHT, chunk, carry, unroll=TEN)
-    lax.fori_loop(ZERO, SIXTEEN, spread, ZERO)
-
-
-def square_sum(ref, coords, core, row0, rows):
+def square_sum(ref, row0, rows):
     def chunk(k, total):
-        block = ref[coords[ZERO], coords[ONE], coords[TWO], core, pl.ds(pl.multiple_of(row0 + EIGHT * k, EIGHT), EIGHT), :]
+        block = ref[pl.ds(pl.multiple_of(row0 + EIGHT * k, EIGHT), EIGHT), :]
         return total + block * block
     return lax.fori_loop(ZERO, rows // EIGHT, chunk, jnp.zeros((EIGHT, LANES), F32), unroll=TWO)
 
-
-def reduce_kernel(flat_hbm, gh_ref, gs_ref, loss_ref, gl_ref, ghead_ref, gsmall_ref, stat_ref, flat, grad, t0, t1, t2, t3, msg, box, send_sem, recv_sem, load_sem, tiny_send, tiny_recv):
-    where = place()
-    me, coords, core, neighbours, partner = where
-    enter_barrier(neighbours, partner)
-    for layer in (ONE, ZERO):
-        copy = pltpu.make_async_copy(flat_hbm.at[layer], flat, load_sem)
-        copy.start()
-        copy.wait()
-        spread_layer(layer, flat, grad)
-
-    def spread_head(dev, carry):
-        z, y, x, own = dev // EIGHT, (dev // FOUR) % TWO, (dev // TWO) % TWO, dev % TWO
-        for j in range(EIGHT):
-            grad[z, y, x, own, HEAD_OFF + IMAGES * j:HEAD_OFF + IMAGES * j + IMAGES, :] = gh_ref[pl.ds(pl.multiple_of(IMAGES * dev, IMAGES), IMAGES), LANES * j:LANES * j + LANES]
-        grad[z, y, x, own, SMALL_OFF:AG_ROWS, :] = jnp.zeros((SIXTEEN, LANES), F32)
-        grad[z, y, x, own, SMALL_OFF:SMALL_OFF + ONE, :] = gs_ref[pl.ds(dev, ONE), :]
-        grad[z, y, x, own, SMALL_OFF + EIGHT:SMALL_OFF + SIXTEEN, :] = loss_ref[...]
-        return carry
-    lax.fori_loop(ZERO, SIXTEEN, spread_head, ZERO)
-    third = AG_ROWS // THREE
-    work = Reduce(grad, (t0, t1, t2, t3), where, [(third * g, third) for g in range(THREE)], send_sem, recv_sem, ZERO)
-    work.start()
-    for phase in range(FOUR):
-        work.step(phase)
-    work.finish()
-    own = (coords[ZERO], coords[ONE], coords[TWO], core)
-    for layer in range(TWO):
-        last = layer * SLOT_ROWS + SHARD_ROWS
-        grad[own + (pl.ds(last, ONE), slice(None))] = jnp.zeros((ONE, LANES), F32)
-    total = square_sum(grad, coords, core, ZERO, SMALL_OFF + EIGHT)
-    msg[ZERO] = jnp.broadcast_to(jnp.sum(total), (EIGHT, LANES))
-    for n, device in enumerate([partner, neighbours[TWO], neighbours[ONE], neighbours[ZERO]]):
-        copy = pltpu.make_async_remote_copy(src_ref=msg.at[n], dst_ref=box.at[n], send_sem=tiny_send.at[n], recv_sem=tiny_recv.at[n], device_id=(device,), device_id_type=MESH_ID)
-        copy.start()
-        copy.wait()
-        msg[n + ONE] = msg[n] + box[n]
-    stat_ref[ZERO] = msg[FOUR]
-    stat_ref[ONE] = grad[own + (pl.ds(SMALL_OFF + EIGHT, EIGHT), slice(None))]
-    for layer in range(TWO):
-        gl_ref[layer] = grad[own + (pl.ds(layer * SLOT_ROWS, SLOT_ROWS), slice(None))]
-    ghead_ref[...] = grad[own + (pl.ds(HEAD_OFF, TH), slice(None))]
-    gsmall_ref[...] = grad[own + (pl.ds(SMALL_OFF, EIGHT), slice(None))]
-
-
-def reduce_grads(flat, gh, gs, loss):
-    vmem = pl.BlockSpec(memory_space=pltpu.VMEM)
-    hbm = pl.BlockSpec(memory_space=pl.ANY)
-    return pl.pallas_call(
-        reduce_kernel,
-        out_shape=(jax.ShapeDtypeStruct((TWO, SLOT_ROWS, LANES), F32), jax.ShapeDtypeStruct((TH, LANES), F32), jax.ShapeDtypeStruct((EIGHT, LANES), F32), jax.ShapeDtypeStruct((TWO, EIGHT, LANES), F32)),
-        in_specs=[hbm, vmem, vmem, vmem],
-        out_specs=(vmem,) * FOUR,
-        scratch_shapes=[
-            pltpu.VMEM((16640, LANES), F32),
-            pltpu.VMEM((TWO, TWO, TWO, TWO, AG_ROWS, LANES), F32),
-            pltpu.VMEM((TWO, TWO, TWO, AG_ROWS, LANES), F32),
-            pltpu.VMEM((TWO, TWO, AG_ROWS, LANES), F32),
-            pltpu.VMEM((TWO, AG_ROWS, LANES), F32),
-            pltpu.VMEM((AG_ROWS, LANES), F32),
-            pltpu.VMEM((FIVE, EIGHT, LANES), F32),
-            pltpu.VMEM((FOUR, EIGHT, LANES), F32),
-            pltpu.SemaphoreType.DMA((12,)),
-            pltpu.SemaphoreType.DMA((12,)),
-            pltpu.SemaphoreType.DMA,
-            pltpu.SemaphoreType.DMA((FOUR,)),
-            pltpu.SemaphoreType.DMA((FOUR,)),
-        ],
-        compiler_params=pltpu.CompilerParams(collective_id=ONE, has_side_effects=True, vmem_limit_bytes=VMEM_CAP),
-        name='reduce_grads',
-    )(flat, gh, gs, loss)
 
 QUADS = 8
 QROWS = 208
@@ -486,8 +406,9 @@
     col[l] = spread.T[ZERO:QROWS, :]
 
 
-def forward_layer(l, x_in, x_mid, x_out, vrow, ma1, ma2, col, w1, w2, uq, uch):
+def forward_layer(l, x_in, x_mid, x_out, vrow, ma1, ma2, col, w1, w2, uq, uch, hook):
     def quad(q, carry):
+        hook(q)
         rows = pl.ds(aligned(q, QROWS), QROWS)
         xq = x_in[rows, :].astype(F32)
         n = token_input(xq, vrow, l)[TWO]
@@ -517,7 +438,7 @@
     return jnp.where(c < QVALID, (c >= TOKENS).astype(jnp.int32) + (c >= TWO * TOKENS).astype(jnp.int32) + (c >= THREE * TOKENS).astype(jnp.int32), IMAGES)
 
 
-def head_pass(x_out, labels, small, head, d, pool, srow, gsum, gh, gs, loss):
+def head_pass(x_out, labels, small, head, d, pool, srow, gsum, flat):
     for k in range(FOUR):
         lanes = slice(LANES * k, LANES * k + LANES)
         srow[ZERO:ONE, lanes] = small[k:k + ONE, :]
@@ -540,10 +461,15 @@
     log_norm = top + jnp.log(jnp.sum(jnp.exp(logits - top), axis=-ONE, keepdims=True))
     hit = iota((IMAGES, CLASS_PAD), ONE) == labels[:, ZERO:ONE]
     picked = jnp.sum(jnp.where(hit, logits, F_ZERO), axis=-ONE, keepdims=True)
-    loss[...] = jnp.broadcast_to(jnp.sum(log_norm - picked), loss.shape)
+    loss = jnp.broadcast_to(jnp.sum(log_norm - picked), (STEP8, LANES))
     d_logits = (jnp.exp(logits - log_norm) - hit.astype(F32)) / GLOBAL_IMAGES
     d_bf = d_logits.astype(BF16)
-    gh[...] = mm(pool_t(pooled), d_bf)
+    g_head = mm(pool_t(pooled), d_bf)
+    for n in range(SIXTEEN):
+        for j in range(EIGHT):
+            flat[HEAD_ROWS * n + IMAGES * j:HEAD_ROWS * n + IMAGES * j + IMAGES, :] = g_head[IMAGES * n:IMAGES * n + IMAGES, LANES * j:LANES * j + LANES]
+        flat[HEAD_ROWS * n + TH:HEAD_ROWS * n + 264, :] = jnp.zeros((STEP8, LANES), F32)
+        flat[HEAD_ROWS * n + 264:HEAD_ROWS * n + 272, :] = loss
     d_pool = (mm_nt(d_bf, head[...]) / TOKENS).astype(BF16)
     gsum[...] = jnp.zeros_like(gsum)
 
@@ -562,17 +488,18 @@
     g_bias = jnp.sum(d_logits, axis=ZERO, keepdims=True)
     for k in range(FOUR):
         lanes = slice(LANES * k, LANES * k + LANES)
-        gs[k:k + ONE, :] = g_gain[:, lanes]
-        gs[FOUR + k:FIVE + k, :] = g_shift[:, lanes]
+        for row, value in ((HEAD_ROWS * k, g_gain), (HEAD_ROWS * (FOUR + k), g_shift)):
+            flat[row + TH:row + 257, :] = value[:, lanes]
     for k in range(EIGHT):
-        gs[EIGHT + k:NINE + k, :] = g_bias[:, LANES * k:LANES * k + LANES]
+        row = HEAD_ROWS * (EIGHT + k) + TH
+        flat[row:row + ONE, :] = g_bias[:, LANES * k:LANES * k + LANES]
 
 
 def pool_t(pooled):
     return pooled.astype(F32).T.astype(BF16)
 
 
-def channel_back(l, x_mid, d, vrow, w1, w2, n2, dbf, n2t, dt, uh, dh, dn2, flat, gsum, gb1):
+def channel_back(l, x_mid, d, vrow, w1, w2, n2, dbf, n2t, dt, uh, dh, dn2, flat, gsum, gb1, hook):
     gsum[...] = jnp.zeros_like(gsum)
     gb1[...] = jnp.zeros_like(gb1)
 
@@ -589,8 +516,10 @@
         lanes = slice(LANES * k, LANES * k + LANES)
         n2t[:, lanes] = n2[lanes, :].T
         dt[:, lanes] = dbf[lanes, :].T
+    hook(-ONE)
 
     def chunk(c, carry):
+        hook(c)
         lanes = pl.ds(aligned(c, CHUNK), CHUNK)
 
         def block(b, inner):
@@ -616,11 +545,12 @@
     lax.fori_loop(ZERO, HID // CHUNK, chunk, ZERO)
 
 
-def token_back(l, x_in, x_mid, d, vrow, dn2, ma1, mb1, ma2, mb2, uq, dq_ref, acc1, acc2, rowsum, colsum, gsum):
+def token_back(l, x_in, x_mid, d, vrow, dn2, ma1, mb1, ma2, mb2, uq, dq_ref, acc1, acc2, rowsum, colsum, gsum, hook):
     for ref in (acc1, acc2, rowsum, colsum):
         ref[...] = jnp.zeros_like(ref)
 
     def quad(q, carry):
+        hook(q)
         rows = pl.ds(aligned(q, QROWS), QROWS)
         xh, scale = stats(x_mid[rows, :].astype(F32))
         dy = dn2[rows, :].astype(BF16).astype(F32)
@@ -698,43 +628,123 @@
     return g
 
 
-def step_kernel(x0, labels, w1, w2, slab, head, small, flat_out, gh, gs, loss, x1, x2, x3, x4, d, dn2, n2, dbf, n2t, dt, uh, dh, uq, dq_ref, uch, ma1, mb1, ma2, mb2, col, vrow, v2, bd, srow, pool, gsum, gb1, acc1, acc2, rowsum, colsum, flat, sem):
+def no_hook(k):
+    return None
+
+
+def at(table):
+    def hook(k):
+        for key, act in table.items():
+            if isinstance(k, int):
+                if key == k:
+                    act()
+            elif key >= ZERO:
+                pl.when(k == key)(act)
+    return hook
+
+
+def both(*acts):
+    def run():
+        for act in acts:
+            act()
+    return run
+
+
+def step_kernel(x0, labels, pack, own, stat, gath, x1, x2, x3, d, dn2, n2, dbf, n2t, dt, mix, uch, ma1, mb1, ma2, mb2, col, vrow, v2, bd, srow, pool, gsum, gb1, acc2, rowsum, colsum, flat, w1, w2, slab, head, small, stage, leaving, t0, t1, t2, t3, msg, box, ag_send, ag_recv, rs_send, rs_recv, stage_sem, load_sem, tiny_send, tiny_recv, done):
+    where = place()
+    me, coords, core, neighbours, partner = where
+    load = pltpu.make_async_copy(pack, gath.at[coords[ZERO], coords[ONE], coords[TWO], core], load_sem)
+    load.start()
+    enter_barrier(neighbours, partner)
+    load.wait()
+    first = Gather(gath, where, ((ZERO, 352), (352, 352), (704, 336)), ag_send, ag_recv, ZERO)
+    rest = Gather(gath, where, ((1040, 448), (1488, 432), (1920, 432)), ag_send, ag_recv, 21)
+    first.start()
+    for phase in range(THREE):
+        first.step(phase)
+    rest.start()
+    first.finish()
+    mats = (ma1, mb1, ma2, mb2, col)
+    unflatten_layer(gath, ZERO, flat, stage, stage_sem, w1, w2, slab)
+    prep_layer(ZERO, slab, vrow, bd, v2, *mats)
+    uq, dq = mix.at[ZERO:FOUR * TH, :], mix.at[FOUR * TH:EIGHT * TH, :]
+    uh, dh = mix.at[ZERO:ALL_ROWS, ZERO:CHUNK], mix.at[ZERO:ALL_ROWS, CHUNK:TWO * CHUNK]
+    acc1 = bd.at[ZERO:QROWS, :]
+    forward_layer(ZERO, x0, x1, x2, vrow, ma1, ma2, col, w1, w2, uq, uch, at({ONE: lambda: rest.step(ZERO), THREE: lambda: rest.step(ONE), SEVEN: lambda: rest.step(TWO)}))
+    rest.finish()
+    unflatten_layer(gath, ONE, flat, stage, stage_sem, w1, w2, slab)
+    unflatten_head(gath, stage, stage_sem, head, small)
+    prep_layer(ONE, slab, vrow, bd, v2, *mats)
+    forward_layer(ONE, x2, x3, n2, vrow, ma1, ma2, col, w1, w2, uq, uch, no_hook)
+    head_pass(n2, labels, small, head, d, pool, srow, gsum, flat)
+
+    bufs, sems = (leaving, t0, t1, t2, t3), (rs_send, rs_recv)
+    thirds = ((ZERO, 352), (352, 352), (704, 336))
+    reduces = [Reduce(flat, HEAD_ROWS, HEAD_ROWS, ((ZERO, 96), (96, 88), (184, 88)), own, HEAD_OFF, bufs, where, sems)]
+    reduces += [Reduce(flat, SHARD_ROWS, SLOT_ROWS, thirds, own, l * SLOT_ROWS, bufs, where, sems) for l in (ONE, ZERO)]
+
+    def done_one(work):
+        def run():
+            work.finish()
+            for other in list(neighbours) + [partner]:
+                pl.semaphore_signal(done, inc=ONE, device_id=(other,), device_id_type=MESH_ID)
+        return run
+
+    def go(work, phase):
+        return lambda: work.step(phase)
+
+    h, r1, r0 = reduces
+    plans = [
+        (ONE, x2, x3, {-ONE: go(h, ZERO), ONE: go(h, ONE), TWO: go(h, TWO), FOUR: both(go(h, THREE), done_one(h))}, {}, r1),
+        (ZERO, x0, x1, {-ONE: go(r1, ZERO), FOUR: go(r1, ONE), SEVEN: go(r1, TWO)}, {TWO: both(go(r1, THREE), done_one(r1))}, r0),
+    ]
+    h.start()
+    for l, x_in, x_mid, channel_plan, token_plan, after in plans:
+        channel_back(l, x_mid, d, vrow, w1, w2, n2, dbf, n2t, dt, uh, dh, dn2, flat, gsum, gb1, at(channel_plan))
+        token_back(l, x_in, x_mid, d, vrow, dn2, ma1, mb1, ma2, mb2, uq, dq, acc1, acc2, rowsum, colsum, gsum, at(token_plan))
+        small_flat(l, flat, acc1, acc2, rowsum, colsum, gsum, gb1, v2)
+        pl.semaphore_wait(done, FOUR)
+        after.start()
+    for phase in range(FOUR):
+        r0.step(phase)
+    r0.finish()
     for l in range(TWO):
-        prep_layer(l, slab, vrow, bd, v2, ma1, mb1, ma2, mb2, col)
-    forward_layer(ZERO, x0, x1, x2, vrow, ma1, ma2, col, w1, w2, uq, uch)
-    forward_layer(ONE, x2, x3, x4, vrow, ma1, ma2, col, w1, w2, uq, uch)
-    head_pass(x4, labels, small, head, d, pool, srow, gsum, gh, gs, loss)
-    for l, x_in, x_mid in ((ONE, x2, x3), (ZERO, x0, x1)):
-        channel_back(l, x_mid, d, vrow, w1, w2, n2, dbf, n2t, dt, uh, dh, dn2, flat, gsum, gb1)
-        token_back(l, x_in, x_mid, d, vrow, dn2, ma1, mb1, ma2, mb2, uq, dq_ref, acc1, acc2, rowsum, colsum, gsum)
-        small_flat(l, flat, acc1, acc2, rowsum, colsum, gsum, gb1, v2)
-        copy = pltpu.make_async_copy(flat, flat_out.at[l], sem)
+        own[l * SLOT_ROWS + SHARD_ROWS:l * SLOT_ROWS + SLOT_ROWS, :] = jnp.zeros((ONE, LANES), F32)
+    msg[ZERO] = jnp.broadcast_to(jnp.sum(square_sum(own, ZERO, SMALL_OFF + EIGHT)), (STEP8, LANES))
+    for n, device in enumerate([partner, neighbours[TWO], neighbours[ONE], neighbours[ZERO]]):
+        copy = pltpu.make_async_remote_copy(src_ref=msg.at[n], dst_ref=box.at[n], send_sem=tiny_send.at[n], recv_sem=tiny_recv.at[n], device_id=(device,), device_id_type=MESH_ID)
         copy.start()
         copy.wait()
-
-
-def local_step(x0, labels, w1, w2, slab, head, small):
+        msg[n + ONE] = msg[n] + box[n]
+    stat[ZERO] = msg[FOUR]
+    stat[ONE] = own[SMALL_OFF + EIGHT:SMALL_OFF + SIXTEEN, :]
+
+
+def train_step(x0, labels, pack):
     vmem = pl.BlockSpec(memory_space=pltpu.VMEM)
     act = pltpu.VMEM((ALL_ROWS, CH), BF16)
     wide = pltpu.VMEM((ALL_ROWS, CH), F32)
     across = pltpu.VMEM((CH, ALL_ROWS), BF16)
-    part = pltpu.VMEM((ALL_ROWS, CHUNK), BF16)
-    tok = pltpu.VMEM((FOUR * TH, CH), BF16)
     tall = pltpu.VMEM((TWO, FOUR * TH, QROWS), BF16)
     flat_mat = pltpu.VMEM((TWO, QROWS, FOUR * TH), BF16)
     acc = pltpu.VMEM((QROWS, FOUR * TH), F32)
+    dma = pltpu.SemaphoreType.DMA
     return pl.pallas_call(
         step_kernel,
-        out_shape=(jax.ShapeDtypeStruct((TWO, FLAT_ROWS + SIXTEEN, LANES), F32), jax.ShapeDtypeStruct((CH, CLASS_PAD), F32), jax.ShapeDtypeStruct((SIXTEEN, LANES), F32), jax.ShapeDtypeStruct((STEP8, LANES), F32)),
-        in_specs=[vmem] * SEVEN,
-        out_specs=(pl.BlockSpec(memory_space=pl.ANY), vmem, vmem, vmem),
-        scratch_shapes=[act, act, act, act, wide, wide, act, act, across, across, part, part, tok, tok, pltpu.VMEM((QROWS, HID), BF16),
+        out_shape=(jax.ShapeDtypeStruct((AG_ROWS, LANES), F32), jax.ShapeDtypeStruct((TWO, STEP8, LANES), F32), jax.ShapeDtypeStruct((TWO, TWO, TWO, TWO, AG_ROWS, LANES), BF16)),
+        in_specs=[vmem] * THREE,
+        out_specs=(vmem, vmem, pl.BlockSpec(memory_space=pl.ANY)),
+        scratch_shapes=[act, act, act, wide, wide, act, act, across, across, pltpu.VMEM((EIGHT * TH, CH), BF16), pltpu.VMEM((QROWS, HID), BF16),
                         tall, flat_mat, flat_mat, tall, pltpu.VMEM((TWO, QROWS, LANES), F32), pltpu.VMEM((TWO, STEP8, HID), F32), pltpu.VMEM((IMAGES, LANES), F32), pltpu.VMEM((TWO * LANES, FOUR * TH), F32),
-                        pltpu.VMEM((STEP8, CLASS_PAD), F32), pltpu.VMEM((IMAGES, CH), F32), pltpu.VMEM((FIVE, STEP8, CH), F32), pltpu.VMEM((STEP8, HID), F32), acc, acc,
-                        pltpu.VMEM((FOUR * TH, LANES), F32), pltpu.VMEM((TWO * LANES, LANES), F32), pltpu.VMEM((FLAT_ROWS + SIXTEEN, LANES), F32), pltpu.SemaphoreType.DMA],
-        compiler_params=pltpu.CompilerParams(vmem_limit_bytes=VMEM_CAP),
-        name='local_step',
-    )(x0, labels, w1, w2, slab, head, small)
+                        pltpu.VMEM((STEP8, CLASS_PAD), F32), pltpu.VMEM((IMAGES, CH), F32), pltpu.VMEM((FIVE, STEP8, CH), F32), pltpu.VMEM((STEP8, HID), F32), acc,
+                        pltpu.VMEM((FOUR * TH, LANES), F32), pltpu.VMEM((TWO * LANES, LANES), F32), pltpu.VMEM((FLAT_ROWS + SIXTEEN, LANES), F32),
+                        pltpu.VMEM((TWO, CH, HID), BF16), pltpu.VMEM((TWO, HID, CH), BF16), pltpu.VMEM((TWO, SLAB_ROWS, LANES), F32), pltpu.VMEM((CH, CLASS_PAD), BF16), pltpu.VMEM((SIXTEEN, LANES), F32),
+                        pltpu.VMEM((TWO, SLOT_ROWS, LANES), BF16), pltpu.VMEM((TWO, TWO, TWO, SLOT_ROWS, LANES), F32), pltpu.VMEM((TWO, TWO, TWO, SLOT_ROWS, LANES), F32), pltpu.VMEM((TWO, TWO, SLOT_ROWS, LANES), F32), pltpu.VMEM((TWO, SLOT_ROWS, LANES), F32), pltpu.VMEM((SLOT_ROWS, LANES), F32),
+                        pltpu.VMEM((FIVE, STEP8, LANES), F32), pltpu.VMEM((FOUR, STEP8, LANES), F32),
+                        dma((42,)), dma((42,)), dma((12,)), dma((12,)), dma((TWO,)), dma, dma((FOUR,)), dma((FOUR,)), pltpu.SemaphoreType.REGULAR],
+        compiler_params=pltpu.CompilerParams(collective_id=ZERO, has_side_effects=True, vmem_limit_bytes=67043328),
+        name='train_step',
+    )(x0, labels, pack)
 
 
 LEARN_RATE = 0.003
@@ -766,12 +776,11 @@
         layer_bf = jnp.pad(layer_p.astype(BF16).reshape(TWO, SHARD_ROWS, LANES), ((ZERO, ZERO), (ZERO, ONE), (ZERO, ZERO)))
         head_bf = jnp.pad(head_w.astype(BF16), ((ZERO, ZERO), (ZERO, CLASS_PAD - CLASSES))).reshape(IMAGES, EIGHT, LANES).transpose(ONE, ZERO, TWO).reshape(TH, LANES)
         small_bf = jnp.pad(small_p.astype(BF16).reshape(ONE, LANES), ((ZERO, 15), (ZERO, ZERO)))
-        weights = gather_weights(jnp.concatenate([layer_bf.reshape(TWO * SLOT_ROWS, LANES), head_bf, small_bf]))
-        local = local_step(quads, jnp.broadcast_to(labels[:, None], (IMAGES, LANES)), *weights)
-        gl, ghead, gsmall, stat = reduce_grads(*local)
-        layer_g = gl[:, :SHARD_ROWS].reshape(TWO, SHARD_ROWS * LANES)
-        head_g = ghead.reshape(EIGHT, IMAGES, LANES).transpose(ONE, ZERO, TWO).reshape(IMAGES, CLASS_PAD)[:, :CLASSES]
-        small_g = gsmall[ZERO]
+        pack = jnp.concatenate([layer_bf.reshape(TWO * SLOT_ROWS, LANES), head_bf, small_bf])
+        own, stat, _ = train_step(quads, jnp.broadcast_to(labels[:, None], (IMAGES, LANES)), pack)
+        layer_g = own[:HEAD_OFF].reshape(TWO, SLOT_ROWS, LANES)[:, :SHARD_ROWS].reshape(TWO, SHARD_ROWS * LANES)
+        head_g = own[HEAD_OFF:SMALL_OFF].reshape(EIGHT, IMAGES, LANES).transpose(ONE, ZERO, TWO).reshape(IMAGES, CLASS_PAD)[:, :CLASSES]
+        small_g = own[SMALL_OFF]
         loss_value = stat[ONE, ZERO, ZERO] / GLOBAL_IMAGES
         clip_scale = F_ONE / jnp.maximum(F_ONE, jnp.sqrt(stat[ZERO, ZERO, ZERO]))
         shard_len = layer_p.shape[ONE]

time: 392 us -> 352 us (0.90)
  Pallas kernels: 367 us -> 326 us
    pallas_call x3 -> x1, Pallas kernels: 367 us -> 326 us  [train_step(): pl.pallas_call(step_kernel, out_shape=(jax.ShapeDtypeStruct((AG_ROWS, LAN...]
where the time goes in v3:
time: 352 us; the launch traced here: 350 us
  Pallas kernels  326 us (93%)
  other arithmetic  10.9 us (3%)
  local copies, waits for them, and re-layouts  9.64 us (3%)
    pallas_call x1, Pallas kernels, train_step(): pl.pallas_call(step_kernel, out_shape=(jax.ShapeDtypeStruct((AG_ROWS, LAN...  326 us
    sub x3, other arithmetic, adam_update(): master - LEARN_RATE * (m_hat / (jnp.sqrt(v_hat) + ADAM_EPS) + decay_rate...  9.47 us

profile of v3, /device:TPU:0, one launch (start us, length us, event | category | flops | bytes accessed | tf_op | source)
XLA Modules:
  0.0 350.0 jit_solution(18001663901868572906)
XLA Ops:
  0.6 2.3 copy.23
  3.0 0.5 reshape.69
  3.5 0.0 copy-start
  3.5 1.4 pad.16
  4.8 0.2 copy-done
  5.0 0.4 convert_element_type.17
  5.4 0.0 copy-start.4
  5.4 0.0 copy-start.6
  5.4 0.9 reshape.71
  6.3 0.0 copy-start.5
  6.4 0.0 copy-done.4
  6.4 0.0 copy-done.6
  6.5 0.9 fusion.4.pack
  7.3 0.0 copy-done.5
  7.3 0.7 broadcast_in_dim.15.labels
  8.0 326.2 %train_step.1 = (f32[2352,128]{1,0:T(8,128)}, f32[2,8,128]{2,1,0:T(8,128)}, bf16[2,2,2,2,2352,128]{5,4,3,2,1,0:T(8,128)(2,1)}) custom-call(bf16[1664,512]{1,0:T(8,128)(2,1)} %bitcast.38, s32[32,128]{1,0:T(8,128)} %broadcast_in_dim.15.labels, bf16[2352,128]{1,0:T(8,128)(2,1)} %fusion.4.pack), custom_call_target="tpu_custom_call" | custom-call | tf_op jit(solution)/shard_map/train_step/pallas_call | solution.py:732
  334.2 0.0 copy-start.2
  334.2 1.3 fusion.14
  336.2 1.2 multiply_subtract_fusion.2
  337.4 0.9 slice.25
  338.4 1.8 multiply_subtract_fusion.1
  340.2 0.0 copy-done.2
  340.2 0.1 slice.22
  340.3 0.0 copy-start.1
  340.3 0.0 copy-start.3
  340.3 0.1 fusion.1
  340.4 0.1 fusion.5
  340.5 1.0 copy-done.1
  341.5 0.3 copy-done.3
  341.8 6.4 %multiply_subtract_fusion = (f32[2,132992]{1,0:T(2,128)}, f32[2,132992]{1,0:T(2,128)}, f32[2,132992]{1,0:T(2,128)}) fusion(f32[2,132992]{1,0:T(2,128)S(1)} %copy-done.1, f32[132992]{0:T(1024)S(1)} %fusion.5, f32[1,2,1039,128]{3,2,1,0:T(8,128)S(1)} %fusion.1, f32[2,132992]{1,0:T(2,128)S(1)} %copy-done.3, f32[2,132992]{1,0:T(2,128)} %param.19), kind=kLoop, calls=%fused_computation.8 | loop fusion | flops 3989760 | bytes 7979520 | tf_op jit(solution)/shard_map/sub | solution.py:763
  (5 shorter events, 0.1 us)
Async XLA Ops:
  3.5 1.5 copy-start
  5.4 1.0 copy-start.4
  5.4 1.0 copy-start.6
  6.3 1.0 copy-start.5
  334.2 6.0 %copy-start.2 = (f32[2352,128]{1,0:T(8,128)S(1)}, f32[2352,128]{1,0:T(8,128)}, u32[]{:S(2)}) copy-start(f32[2352,128]{1,0:T(8,128)} %get-tuple-element.13) | copy-start | bytes 3612676
  340.3 1.2 copy-start.1
  340.3 1.5 copy-start.3

commit v4 on v3

--- a/solution.py
+++ b/solution.py
@@ -125,27 +125,27 @@
     return dev // EIGHT, (dev // FOUR) % TWO, (dev // TWO) % TWO, dev % TWO
 
 
-def unflatten_layer(gath, layer, flat, stage, stage_sem, w1_ref, w2_ref, slab_ref):
-    base = layer * SLOT_ROWS
-
-    def fetch(dev):
+def fetch_layer(gath, layer, bays, stage_sem):
+    copies = []
+    for dev in range(SIXTEEN):
         z, y, x, core = slot_of(dev)
-        return pltpu.make_async_copy(gath.at[z, y, x, core, pl.ds(base, SLOT_ROWS), :], stage.at[dev % TWO], stage_sem.at[dev % TWO])
-    fetch(ZERO).start()
-
-    def spread(dev, carry):
-        fetch(dev).wait()
-
-        @pl.when(dev < 15)
-        def _():
-            fetch(dev + ONE).start()
+        land = bays[dev // FOUR].at[pl.ds(ZERO, SLOT_ROWS), pl.ds(LANES * (dev % FOUR), LANES)]
+        copies.append(pltpu.make_async_copy(gath.at[z, y, x, core, pl.ds(layer * SLOT_ROWS, SLOT_ROWS), :], land, stage_sem.at[dev]))
+    for copy in copies:
+        copy.start()
+    return copies
+
+
+def unflatten_layer(gath, layer, flat, bays, stage_sem, w1_ref, w2_ref, slab_ref):
+    copies = fetch_layer(gath, layer, bays, stage_sem)
+    for dev in range(SIXTEEN):
+        copies[dev].wait()
 
         def chunk(k, inner):
-            block = stage[dev % TWO, pl.ds(pl.multiple_of(SIXTEEN * k, SIXTEEN), SIXTEEN), :]
+            block = bays[dev // FOUR][pl.ds(pl.multiple_of(SIXTEEN * k, SIXTEEN), SIXTEEN), LANES * (dev % FOUR):LANES * (dev % FOUR) + LANES]
             flat[pl.ds(dev * SHARD_ROWS + SIXTEEN * k, SIXTEEN), :] = block.astype(F32)
             return inner
-        return lax.fori_loop(ZERO, SLOT_ROWS // SIXTEEN, chunk, carry, unroll=FIVE)
-    lax.fori_loop(ZERO, SIXTEEN, spread, ZERO)
+        lax.fori_loop(ZERO, SLOT_ROWS // SIXTEEN, chunk, ZERO, unroll=FIVE)
 
     def first(rb, carry):
         for j in range(SIXTEEN):
@@ -164,23 +164,19 @@
     slab_ref[layer, QVALID:240, :] = flat[ROW_VEC:FLAT_ROWS, :]
 
 
-def unflatten_head(gath, stage, stage_sem, head_ref, small_ref):
-    def fetch(dev):
+def unflatten_head(gath, bays, stage_sem, head_ref, small_ref):
+    copies = []
+    for dev in range(SIXTEEN):
         z, y, x, core = slot_of(dev)
-        return pltpu.make_async_copy(gath.at[z, y, x, core, pl.ds(HEAD_OFF, HEAD_ROWS), :], stage.at[dev % TWO, pl.ds(ZERO, HEAD_ROWS), :], stage_sem.at[dev % TWO])
-    fetch(ZERO).start()
-
-    def spread(dev, carry):
-        fetch(dev).wait()
-
-        @pl.when(dev < 15)
-        def _():
-            fetch(dev + ONE).start()
+        copies.append(pltpu.make_async_copy(gath.at[z, y, x, core, pl.ds(HEAD_OFF, HEAD_ROWS), :], bays[dev // FOUR].at[pl.ds(ZERO, HEAD_ROWS), pl.ds(LANES * (dev % FOUR), LANES)], stage_sem.at[dev]))
+    for copy in copies:
+        copy.start()
+    for dev in range(SIXTEEN):
+        copies[dev].wait()
+        lanes = slice(LANES * (dev % FOUR), LANES * (dev % FOUR) + LANES)
         for j in range(EIGHT):
-            head_ref[pl.ds(pl.multiple_of(IMAGES * dev, IMAGES), IMAGES), LANES * j:LANES * j + LANES] = stage[dev % TWO, IMAGES * j:IMAGES * j + IMAGES, :]
-        small_ref[pl.ds(dev, ONE), :] = stage[dev % TWO, TH:272, :].astype(F32)[ZERO:ONE, :]
-        return carry
-    lax.fori_loop(ZERO, SIXTEEN, spread, ZERO)
+            head_ref[IMAGES * dev:IMAGES * dev + IMAGES, LANES * j:LANES * j + LANES] = bays[dev // FOUR][IMAGES * j:IMAGES * j + IMAGES, lanes]
+        small_ref[dev:dev + ONE, :] = bays[dev // FOUR][TH:272, lanes].astype(F32)[ZERO:ONE, :]
 
 
 class Reduce:
@@ -340,9 +336,9 @@
 
 def gelu_both(h):
     sq, t = gelu_tanh(h)
-    half = HALF * h
-    slope = (HALF + HALF * t) + half * (F_ONE - t * t) * (GELU_A + (3.0 * GELU_B) * sq)
-    return (half + half * t).astype(BF16), slope
+    side = HALF + HALF * t
+    u = h * side
+    return u.astype(BF16), side + (u - u * t) * (GELU_A + (3.0 * GELU_B) * sq)
 
 
 def norm_back(xh, scale, gain, dy):
@@ -421,8 +417,11 @@
         n2 = (stats(x1)[ZERO] * vrow[l, TWO:THREE, ZERO:CH] + vrow[l, THREE:FOUR, ZERO:CH]).astype(BF16)
         for c in range(FOUR):
             lanes = slice(CH * c, CH * c + CH)
-            uch[:, lanes] = gelu(mm(n2, w1[l, :, lanes]) + vrow[l, FOUR:FIVE, lanes])
-        x_out[rows, :] = (x1 + (mm(uch[...], w2[l]) + vrow[l, FIVE:SIX, ZERO:CH])).astype(BF16)
+            uch[QROWS * c:QROWS * c + QROWS, :] = gelu(mm(n2, w1[l, :, lanes]) + vrow[l, FOUR:FIVE, lanes])
+        y = mm(uch[ZERO:QROWS, :], w2[l, ZERO:CH, :])
+        for c in range(ONE, FOUR):
+            y = y + mm(uch[QROWS * c:QROWS * c + QROWS, :], w2[l, CH * c:CH * c + CH, :])
+        x_out[rows, :] = (x1 + (y + vrow[l, FIVE:SIX, ZERO:CH])).astype(BF16)
         return carry
     lax.fori_loop(ZERO, QUADS, quad, ZERO)
 
@@ -522,8 +521,8 @@
         hook(c)
         lanes = pl.ds(aligned(c, CHUNK), CHUNK)
 
-        def block(b, inner):
-            rows = pl.ds(aligned(b, BLOCK), BLOCK)
+        for b in range(ALL_ROWS // BLOCK):
+            rows = slice(BLOCK * b, BLOCK * b + BLOCK)
             u, slope = gelu_both(mm(n2[rows, :], w1[l, :, lanes]) + vrow[l, FOUR:FIVE, lanes])
             uh[rows, :] = u
             dhid = mm_nt(dbf[rows, :], w2[l, lanes, :]).astype(BF16).astype(F32) * slope
@@ -531,8 +530,6 @@
             dhid = dhid.astype(BF16)
             dh[rows, :] = dhid
             dn2[rows, :] += mm_nt(dhid, w1[l, :, lanes])
-            return inner
-        lax.fori_loop(ZERO, ALL_ROWS // BLOCK, block, ZERO)
         g1 = mm(n2t[...], dh[...])
         for r in range(CH // STEP8):
             for k in range(TWO):
@@ -650,7 +647,7 @@
     return run
 
 
-def step_kernel(x0, labels, pack, own, stat, gath, x1, x2, x3, d, dn2, n2, dbf, n2t, dt, mix, uch, ma1, mb1, ma2, mb2, col, vrow, v2, bd, srow, pool, gsum, gb1, acc2, rowsum, colsum, flat, w1, w2, slab, head, small, stage, leaving, t0, t1, t2, t3, msg, box, ag_send, ag_recv, rs_send, rs_recv, stage_sem, load_sem, tiny_send, tiny_recv, done):
+def step_kernel(x0, labels, pack, own, stat, gath, x1, x2, x3, d, dn2, n2, dbf, n2t, dt, mix, ma1, mb1, ma2, mb2, col, vrow, v2, bd, srow, pool, gsum, gb1, acc2, rowsum, colsum, flat, w1, w2, slab, head, small, leaving, t0, t1, t2, t3, msg, box, ag_send, ag_recv, rs_send, rs_recv, stage_sem, load_sem, tiny_send, tiny_recv, late_send, late_recv, done, late, late_box):
     where = place()
     me, coords, core, neighbours, partner = where
     load = pltpu.make_async_copy(pack, gath.at[coords[ZERO], coords[ONE], coords[TWO], core], load_sem)
@@ -665,15 +662,16 @@
     rest.start()
     first.finish()
     mats = (ma1, mb1, ma2, mb2, col)
-    unflatten_layer(gath, ZERO, flat, stage, stage_sem, w1, w2, slab)
+    unflatten_layer(gath, ZERO, flat, (x3, n2, dbf, mix), stage_sem, w1, w2, slab)
     prep_layer(ZERO, slab, vrow, bd, v2, *mats)
     uq, dq = mix.at[ZERO:FOUR * TH, :], mix.at[FOUR * TH:EIGHT * TH, :]
+    uch = mix.at[FOUR * TH:FOUR * TH + FOUR * QROWS, :]
     uh, dh = mix.at[ZERO:ALL_ROWS, ZERO:CHUNK], mix.at[ZERO:ALL_ROWS, CHUNK:TWO * CHUNK]
     acc1 = bd.at[ZERO:QROWS, :]
     forward_layer(ZERO, x0, x1, x2, vrow, ma1, ma2, col, w1, w2, uq, uch, at({ONE: lambda: rest.step(ZERO), THREE: lambda: rest.step(ONE), SEVEN: lambda: rest.step(TWO)}))
     rest.finish()
-    unflatten_layer(gath, ONE, flat, stage, stage_sem, w1, w2, slab)
-    unflatten_head(gath, stage, stage_sem, head, small)
+    unflatten_layer(gath, ONE, flat, (x3, n2, dbf, mix), stage_sem, w1, w2, slab)
+    unflatten_head(gath, (x3, n2, dbf, mix), stage_sem, head, small)
     prep_layer(ONE, slab, vrow, bd, v2, *mats)
     forward_layer(ONE, x2, x3, n2, vrow, ma1, ma2, col, w1, w2, uq, uch, no_hook)
     head_pass(n2, labels, small, head, d, pool, srow, gsum, flat)
@@ -694,29 +692,54 @@
         return lambda: work.step(phase)
 
     h, r1, r0 = reduces
-    plans = [
-        (ONE, x2, x3, {-ONE: go(h, ZERO), ONE: go(h, ONE), TWO: go(h, TWO), FOUR: both(go(h, THREE), done_one(h))}, {}, r1),
-        (ZERO, x0, x1, {-ONE: go(r1, ZERO), FOUR: go(r1, ONE), SEVEN: go(r1, TWO)}, {TWO: both(go(r1, THREE), done_one(r1))}, r0),
-    ]
+    back = (d, vrow, w1, w2, n2, dbf, n2t, dt, uh, dh, dn2, flat, gsum, gb1)
+    tok = (d, vrow, dn2, ma1, mb1, ma2, mb2, uq, dq, acc1, acc2, rowsum, colsum, gsum)
+    small_parts = (flat, acc1, acc2, rowsum, colsum, gsum, gb1, v2)
     h.start()
-    for l, x_in, x_mid, channel_plan, token_plan, after in plans:
-        channel_back(l, x_mid, d, vrow, w1, w2, n2, dbf, n2t, dt, uh, dh, dn2, flat, gsum, gb1, at(channel_plan))
-        token_back(l, x_in, x_mid, d, vrow, dn2, ma1, mb1, ma2, mb2, uq, dq, acc1, acc2, rowsum, colsum, gsum, at(token_plan))
-        small_flat(l, flat, acc1, acc2, rowsum, colsum, gsum, gb1, v2)
-        pl.semaphore_wait(done, FOUR)
-        after.start()
-    for phase in range(FOUR):
-        r0.step(phase)
+    channel_back(ONE, x3, *back, at({-ONE: go(h, ZERO), ONE: go(h, ONE), TWO: go(h, TWO), FOUR: both(go(h, THREE), done_one(h))}))
+    token_back(ONE, x2, x3, *tok, no_hook)
+    small_flat(ONE, *small_parts)
+    pl.semaphore_wait(done, FOUR)
+    r1.start()
+    channel_back(ZERO, x1, *back, at({-ONE: go(r1, ZERO), FOUR: go(r1, ONE), SIX: go(r1, TWO)}))
+    r1.step(THREE)
+    done_one(r1)()
+    pl.semaphore_wait(done, FOUR)
+    r0.start()
+    token_back(ZERO, x0, x1, *tok, at({TWO: go(r0, ZERO)}))
+    small_flat(ZERO, *small_parts)
+    late[ZERO, ZERO:QVALID, :] = flat[ZERO:QVALID, :]
+    late[ZERO, QVALID:240, :] = flat[ROW_VEC:FLAT_ROWS, :]
+    hops = [partner, neighbours[TWO], neighbours[ONE], neighbours[ZERO]]
+
+    def exchange(value, box_ref, sems, n):
+        return pltpu.make_async_remote_copy(src_ref=value.at[n % TWO], dst_ref=box_ref.at[n], send_sem=sems[ZERO].at[n], recv_sem=sems[ONE].at[n], device_id=(hops[n],), device_id_type=MESH_ID)
+
+    def late_copy(n):
+        return exchange(late, late_box, (late_send, late_recv), n)
+    late_copy(ZERO).start()
+    r0.step(ONE)
+    for n in range(FOUR):
+        late_copy(n).wait()
+        late[(n + ONE) % TWO] = late[n % TWO] + late_box[n]
+        if n < THREE:
+            late_copy(n + ONE).start()
+        if n == TWO:
+            r0.step(TWO)
+    r0.step(THREE)
     r0.finish()
+    own[ZERO:QVALID, :] = jnp.where(me == ZERO, late[ZERO, ZERO:QVALID, :], own[ZERO:QVALID, :])
+    last = ROW_VEC - 15 * SHARD_ROWS
+    own[last:SHARD_ROWS, :] = jnp.where(me == 15, late[ZERO, QVALID:240, :], own[last:SHARD_ROWS, :])
     for l in range(TWO):
         own[l * SLOT_ROWS + SHARD_ROWS:l * SLOT_ROWS + SLOT_ROWS, :] = jnp.zeros((ONE, LANES), F32)
     msg[ZERO] = jnp.broadcast_to(jnp.sum(square_sum(own, ZERO, SMALL_OFF + EIGHT)), (STEP8, LANES))
-    for n, device in enumerate([partner, neighbours[TWO], neighbours[ONE], neighbours[ZERO]]):
-        copy = pltpu.make_async_remote_copy(src_ref=msg.at[n], dst_ref=box.at[n], send_sem=tiny_send.at[n], recv_sem=tiny_recv.at[n], device_id=(device,), device_id_type=MESH_ID)
+    for n in range(FOUR):
+        copy = exchange(msg, box, (tiny_send, tiny_recv), n)
         copy.start()
         copy.wait()
-        msg[n + ONE] = msg[n] + box[n]
-    stat[ZERO] = msg[FOUR]
+        msg[(n + ONE) % TWO] = msg[n % TWO] + box[n]
+    stat[ZERO] = msg[ZERO]
     stat[ONE] = own[SMALL_OFF + EIGHT:SMALL_OFF + SIXTEEN, :]
 
 
@@ -734,14 +757,14 @@
         out_shape=(jax.ShapeDtypeStruct((AG_ROWS, LANES), F32), jax.ShapeDtypeStruct((TWO, STEP8, LANES), F32), jax.ShapeDtypeStruct((TWO, TWO, TWO, TWO, AG_ROWS, LANES), BF16)),
         in_specs=[vmem] * THREE,
         out_specs=(vmem, vmem, pl.BlockSpec(memory_space=pl.ANY)),
-        scratch_shapes=[act, act, act, wide, wide, act, act, across, across, pltpu.VMEM((EIGHT * TH, CH), BF16), pltpu.VMEM((QROWS, HID), BF16),
+        scratch_shapes=[act, act, act, wide, wide, act, act, across, across, pltpu.VMEM((EIGHT * TH, CH), BF16),
                         tall, flat_mat, flat_mat, tall, pltpu.VMEM((TWO, QROWS, LANES), F32), pltpu.VMEM((TWO, STEP8, HID), F32), pltpu.VMEM((IMAGES, LANES), F32), pltpu.VMEM((TWO * LANES, FOUR * TH), F32),
                         pltpu.VMEM((STEP8, CLASS_PAD), F32), pltpu.VMEM((IMAGES, CH), F32), pltpu.VMEM((FIVE, STEP8, CH), F32), pltpu.VMEM((STEP8, HID), F32), acc,
                         pltpu.VMEM((FOUR * TH, LANES), F32), pltpu.VMEM((TWO * LANES, LANES), F32), pltpu.VMEM((FLAT_ROWS + SIXTEEN, LANES), F32),
                         pltpu.VMEM((TWO, CH, HID), BF16), pltpu.VMEM((TWO, HID, CH), BF16), pltpu.VMEM((TWO, SLAB_ROWS, LANES), F32), pltpu.VMEM((CH, CLASS_PAD), BF16), pltpu.VMEM((SIXTEEN, LANES), F32),
-                        pltpu.VMEM((TWO, SLOT_ROWS, LANES), BF16), pltpu.VMEM((TWO, TWO, TWO, SLOT_ROWS, LANES), F32), pltpu.VMEM((TWO, TWO, TWO, SLOT_ROWS, LANES), F32), pltpu.VMEM((TWO, TWO, SLOT_ROWS, LANES), F32), pltpu.VMEM((TWO, SLOT_ROWS, LANES), F32), pltpu.VMEM((SLOT_ROWS, LANES), F32),
-                        pltpu.VMEM((FIVE, STEP8, LANES), F32), pltpu.VMEM((FOUR, STEP8, LANES), F32),
-                        dma((42,)), dma((42,)), dma((12,)), dma((12,)), dma((TWO,)), dma, dma((FOUR,)), dma((FOUR,)), pltpu.SemaphoreType.REGULAR],
+                        pltpu.VMEM((TWO, TWO, TWO, SLOT_ROWS, LANES), F32), pltpu.VMEM((TWO, TWO, TWO, SLOT_ROWS, LANES), F32), pltpu.VMEM((TWO, TWO, SLOT_ROWS, LANES), F32), pltpu.VMEM((TWO, SLOT_ROWS, LANES), F32), pltpu.VMEM((SLOT_ROWS, LANES), F32),
+                        pltpu.VMEM((TWO, STEP8, LANES), F32), pltpu.VMEM((FOUR, STEP8, LANES), F32),
+                        dma((42,)), dma((42,)), dma((12,)), dma((12,)), dma((SIXTEEN,)), dma, dma((FOUR,)), dma((FOUR,)), dma((FOUR,)), dma((FOUR,)), pltpu.SemaphoreType.REGULAR, pltpu.VMEM((TWO, SLAB_ROWS, LANES), F32), pltpu.VMEM((FOUR, SLAB_ROWS, LANES), F32)],
         compiler_params=pltpu.CompilerParams(collective_id=ZERO, has_side_effects=True, vmem_limit_bytes=67043328),
         name='train_step',
     )(x0, labels, pack)

time: 352 us -> 293 us (0.83)
  Pallas kernels: 326 us -> 269 us
    pallas_call x1, Pallas kernels: 326 us -> 269 us  [train_step(): pl.pallas_call(step_kernel, out_shape=(jax.ShapeDtypeStruct((AG_ROWS, LAN...]
where the time goes in v4:
time: 293 us
  Pallas kernels  269 us (92%)
  other arithmetic  10.9 us (4%)
  local copies, waits for them, and re-layouts  9.64 us (3%)
  between operations  3.33 us (1%)
    pallas_call x1, Pallas kernels, train_step(): pl.pallas_call(step_kernel, out_shape=(jax.ShapeDtypeStruct((AG_ROWS, LAN...  269 us
    sub x3, other arithmetic, adam_update(): master - LEARN_RATE * (m_hat / (jnp.sqrt(v_hat) + ADAM_EPS) + decay_rate...  9.47 us

profile of v4, /device:TPU:0, one launch (start us, length us, event | category | flops | bytes accessed | tf_op | source)
XLA Modules:
  0.0 292.6 jit_solution(13633217616239458539)
XLA Ops:
  0.6 2.3 copy.23
  3.0 0.5 reshape.69
  3.5 0.0 copy-start
  3.5 1.4 pad.16
  4.8 0.2 copy-done
  5.0 0.4 convert_element_type.17
  5.4 0.0 copy-start.4
  5.4 0.0 copy-start.6
  5.4 0.9 reshape.71
  6.3 0.0 copy-start.5
  6.4 0.0 copy-done.4
  6.4 0.0 copy-done.6
  6.5 0.9 fusion.4.pack
  7.3 0.0 copy-done.5
  7.3 0.7 broadcast_in_dim.15.labels
  8.0 268.8 %train_step.1 = (f32[2352,128]{1,0:T(8,128)}, f32[2,8,128]{2,1,0:T(8,128)}, bf16[2,2,2,2,2352,128]{5,4,3,2,1,0:T(8,128)(2,1)}) custom-call(bf16[1664,512]{1,0:T(8,128)(2,1)} %bitcast.38, s32[32,128]{1,0:T(8,128)} %broadcast_in_dim.15.labels, bf16[2352,128]{1,0:T(8,128)(2,1)} %fusion.4.pack), custom_call_target="tpu_custom_call" | custom-call | tf_op jit(solution)/shard_map/train_step/pallas_call | solution.py:755
  276.8 0.0 copy-start.2
  276.8 1.3 fusion.14
  278.8 1.2 multiply_subtract_fusion.2
  280.0 0.9 slice.25
  281.0 1.8 multiply_subtract_fusion.1
  282.8 0.0 copy-done.2
  282.8 0.1 slice.22
  282.9 0.0 copy-start.1
  282.9 0.0 copy-start.3
  282.9 0.1 fusion.1
  283.0 0.1 fusion.5
  283.1 1.0 copy-done.1
  284.1 0.3 copy-done.3
  284.4 6.4 %multiply_subtract_fusion = (f32[2,132992]{1,0:T(2,128)}, f32[2,132992]{1,0:T(2,128)}, f32[2,132992]{1,0:T(2,128)}) fusion(f32[2,132992]{1,0:T(2,128)S(1)} %copy-done.1, f32[132992]{0:T(1024)S(1)} %fusion.5, f32[1,2,1039,128]{3,2,1,0:T(8,128)S(1)} %fusion.1, f32[2,132992]{1,0:T(2,128)S(1)} %copy-done.3, f32[2,132992]{1,0:T(2,128)} %param.19), kind=kLoop, calls=%fused_computation.8 | loop fusion | flops 3989760 | bytes 7979520 | tf_op jit(solution)/shard_map/sub | solution.py:786
  (5 shorter events, 0.1 us)
Async XLA Ops:
  3.5 1.5 copy-start
  5.4 1.0 copy-start.4
  5.4 1.0 copy-start.6
  6.3 1.0 copy-start.5
  276.8 6.0 %copy-start.2 = (f32[2352,128]{1,0:T(8,128)S(1)}, f32[2352,128]{1,0:T(8,128)}, u32[]{:S(2)}) copy-start(f32[2352,128]{1,0:T(8,128)} %get-tuple-element.13) | copy-start | bytes 3612676
  282.9 1.2 copy-start.1
  282.9 1.5 copy-start.3

commit v5 on v4

--- a/solution.py
+++ b/solution.py
@@ -36,7 +36,9 @@
 F32 = jnp.float32
 BF16 = jnp.bfloat16
 
+DEVICES = 16
 SHARD_ROWS = 1039
+UPDATE_ROWS = 130
 SLOT_ROWS = 1040
 ROW_C1 = 196
 ROW_C2 = 8388
@@ -60,11 +62,11 @@
     return me, coords, core, neighbours, partner
 
 
-def enter_barrier(neighbours, partner):
+def enter_barrier(me):
     barrier = pltpu.get_barrier_semaphore()
-    for other in list(neighbours) + [partner]:
-        pl.semaphore_signal(barrier, inc=ONE, device_id=(other,), device_id_type=MESH_ID)
-    pl.semaphore_wait(barrier, FOUR)
+    for k in range(ONE, DEVICES):
+        pl.semaphore_signal(barrier, inc=ONE, device_id=((me + k) % DEVICES,), device_id_type=MESH_ID)
+    pl.semaphore_wait(barrier, DEVICES - ONE)
 
 
 def slot_view(buf, coords, core, free_axes, row0, rows):
@@ -281,6 +283,10 @@
 ALL_ROWS = QUADS * QROWS
 CHUNK = 256
 BLOCK = 416
+TOK_ROWS = 256
+TOK_LANES = 256
+FWD_ROWS = 256
+FWD_LANES = 512
 CLASSES = 1000
 GLOBAL_IMAGES = 512.0
 LN_EPS = 1e-6
@@ -408,8 +414,9 @@
         rows = pl.ds(aligned(q, QROWS), QROWS)
         xq = x_in[rows, :].astype(F32)
         n = token_input(xq, vrow, l)[TWO]
-        for i in range(FOUR):
-            uq[TH * i:TH * i + TH, :] = gelu(mm(ma1[l, TH * i:TH * i + TH, :], n))
+        for lane0 in range(ZERO, CH, FWD_LANES):
+            for row0 in range(ZERO, FOUR * TH, FWD_ROWS):
+                uq[row0:row0 + FWD_ROWS, lane0:lane0 + FWD_LANES] = gelu(mm(ma1[l, row0:row0 + FWD_ROWS, :], n[:, lane0:lane0 + FWD_LANES]))
         y = mm(ma2[l], uq[...])
         x1 = (xq + (y + jnp.concatenate([col[l]] * FOUR, axis=ONE))).astype(BF16)
         x_mid[rows, :] = x1
@@ -560,16 +567,18 @@
         colsum[ZERO:QROWS, :] += part
         d_bf = d_after.astype(BF16)
         xh, scale, n = token_input(x_in[rows, :].astype(F32), vrow, l)
-        for i in range(FOUR):
-            part = slice(TH * i, TH * i + TH)
-            u, slope = gelu_both(mm(ma1[l, part, :], n))
-            uq[part, :] = u
-            dhid = mm(mb2[l, part, :], d_bf).astype(BF16).astype(F32) * slope
-            total = dhid[:, ZERO:LANES]
-            for k in range(ONE, FOUR):
-                total = total + dhid[:, LANES * k:LANES * k + LANES]
-            rowsum[part, :] += total
-            dq_ref[part, :] = dhid.astype(BF16)
+        for lane0 in range(ZERO, CH, TOK_LANES):
+            lanes = slice(lane0, lane0 + TOK_LANES)
+            for row0 in range(ZERO, FOUR * TH, TOK_ROWS):
+                part = slice(row0, row0 + TOK_ROWS)
+                u, slope = gelu_both(mm(ma1[l, part, :], n[:, lanes]))
+                uq[part, lanes] = u
+                dhid = mm(mb2[l, part, :], d_bf[:, lanes]).astype(BF16).astype(F32) * slope
+                total = dhid[:, ZERO:LANES]
+                for k in range(ONE, TOK_LANES // LANES):
+                    total = total + dhid[:, LANES * k:LANES * k + LANES]
+                rowsum[part, :] += total
+                dq_ref[part, lanes] = dhid.astype(BF16)
         acc1[...] += mm_nt(n, dq_ref[...])
         acc2[...] += mm_nt(d_bf, uq[...])
         dy = mm(mb1[l], dq_ref[...]).astype(BF16).astype(F32)
@@ -647,12 +656,12 @@
     return run
 
 
-def step_kernel(x0, labels, pack, own, stat, gath, x1, x2, x3, d, dn2, n2, dbf, n2t, dt, mix, ma1, mb1, ma2, mb2, col, vrow, v2, bd, srow, pool, gsum, gb1, acc2, rowsum, colsum, flat, w1, w2, slab, head, small, leaving, t0, t1, t2, t3, msg, box, ag_send, ag_recv, rs_send, rs_recv, stage_sem, load_sem, tiny_send, tiny_recv, late_send, late_recv, done, late, late_box):
+def step_kernel(x0, labels, pack, own, stat, gath, x1, x2, x3, d, dn2, n2, dbf, n2t, dt, mix, ma1, mb1, ma2, mb2, col, vrow, v2, bd, srow, pool, gsum, gb1, acc2, rowsum, colsum, flat, w1, w2, slab, head, small, leaving, t0, t1, t2, t3, box, ag_send, ag_recv, rs_send, rs_recv, stage_sem, load_sem, tiny_send, tiny_recv, late_send, late_recv, done, late, late_box):
     where = place()
     me, coords, core, neighbours, partner = where
     load = pltpu.make_async_copy(pack, gath.at[coords[ZERO], coords[ONE], coords[TWO], core], load_sem)
     load.start()
-    enter_barrier(neighbours, partner)
+    enter_barrier(me)
     load.wait()
     first = Gather(gath, where, ((ZERO, 352), (352, 352), (704, 336)), ag_send, ag_recv, ZERO)
     rest = Gather(gath, where, ((1040, 448), (1488, 432), (1920, 432)), ag_send, ag_recv, 21)
@@ -717,29 +726,37 @@
 
     def late_copy(n):
         return exchange(late, late_box, (late_send, late_recv), n)
-    late_copy(ZERO).start()
-    r0.step(ONE)
-    for n in range(FOUR):
+    def late_step(n):
         late_copy(n).wait()
         late[(n + ONE) % TWO] = late[n % TWO] + late_box[n]
         if n < THREE:
             late_copy(n + ONE).start()
-        if n == TWO:
-            r0.step(TWO)
+    late_copy(ZERO).start()
+    late_step(ZERO)
+    r0.step(ONE)
+    late_step(ONE)
+    r0.step(TWO)
+    late_step(TWO)
     r0.step(THREE)
+    late_step(THREE)
     r0.finish()
     own[ZERO:QVALID, :] = jnp.where(me == ZERO, late[ZERO, ZERO:QVALID, :], own[ZERO:QVALID, :])
     last = ROW_VEC - 15 * SHARD_ROWS
     own[last:SHARD_ROWS, :] = jnp.where(me == 15, late[ZERO, QVALID:240, :], own[last:SHARD_ROWS, :])
     for l in range(TWO):
         own[l * SLOT_ROWS + SHARD_ROWS:l * SLOT_ROWS + SLOT_ROWS, :] = jnp.zeros((ONE, LANES), F32)
-    msg[ZERO] = jnp.broadcast_to(jnp.sum(square_sum(own, ZERO, SMALL_OFF + EIGHT)), (STEP8, LANES))
-    for n in range(FOUR):
-        copy = exchange(msg, box, (tiny_send, tiny_recv), n)
-        copy.start()
-        copy.wait()
-        msg[(n + ONE) % TWO] = msg[n % TWO] + box[n]
-    stat[ZERO] = msg[ZERO]
+    box[me] = jnp.broadcast_to(jnp.sum(square_sum(own, ZERO, SMALL_OFF + EIGHT)), (STEP8, LANES))
+
+    def tell(k):
+        return pltpu.make_async_remote_copy(src_ref=box.at[me], dst_ref=box.at[me], send_sem=tiny_send.at[k], recv_sem=tiny_recv.at[k], device_id=((me + k) % DEVICES,), device_id_type=MESH_ID)
+    for k in range(ONE, DEVICES):
+        tell(k).start()
+    for k in range(ONE, DEVICES):
+        tell(k).wait()
+    total = box[ZERO]
+    for k in range(ONE, DEVICES):
+        total = total + box[k]
+    stat[ZERO] = total
     stat[ONE] = own[SMALL_OFF + EIGHT:SMALL_OFF + SIXTEEN, :]
 
 
@@ -763,8 +780,8 @@
                         pltpu.VMEM((FOUR * TH, LANES), F32), pltpu.VMEM((TWO * LANES, LANES), F32), pltpu.VMEM((FLAT_ROWS + SIXTEEN, LANES), F32),
                         pltpu.VMEM((TWO, CH, HID), BF16), pltpu.VMEM((TWO, HID, CH), BF16), pltpu.VMEM((TWO, SLAB_ROWS, LANES), F32), pltpu.VMEM((CH, CLASS_PAD), BF16), pltpu.VMEM((SIXTEEN, LANES), F32),
                         pltpu.VMEM((TWO, TWO, TWO, SLOT_ROWS, LANES), F32), pltpu.VMEM((TWO, TWO, TWO, SLOT_ROWS, LANES), F32), pltpu.VMEM((TWO, TWO, SLOT_ROWS, LANES), F32), pltpu.VMEM((TWO, SLOT_ROWS, LANES), F32), pltpu.VMEM((SLOT_ROWS, LANES), F32),
-                        pltpu.VMEM((TWO, STEP8, LANES), F32), pltpu.VMEM((FOUR, STEP8, LANES), F32),
-                        dma((42,)), dma((42,)), dma((12,)), dma((12,)), dma((SIXTEEN,)), dma, dma((FOUR,)), dma((FOUR,)), dma((FOUR,)), dma((FOUR,)), pltpu.SemaphoreType.REGULAR, pltpu.VMEM((TWO, SLAB_ROWS, LANES), F32), pltpu.VMEM((FOUR, SLAB_ROWS, LANES), F32)],
+                        pltpu.VMEM((DEVICES, STEP8, LANES), F32),
+                        dma((42,)), dma((42,)), dma((12,)), dma((12,)), dma((SIXTEEN,)), dma, dma((DEVICES,)), dma((DEVICES,)), dma((FOUR,)), dma((FOUR,)), pltpu.SemaphoreType.REGULAR, pltpu.VMEM((TWO, SLAB_ROWS, LANES), F32), pltpu.VMEM((FOUR, SLAB_ROWS, LANES), F32)],
         compiler_params=pltpu.CompilerParams(collective_id=ZERO, has_side_effects=True, vmem_limit_bytes=67043328),
         name='train_step',
     )(x0, labels, pack)
@@ -786,6 +803,43 @@
     master_new = master - LEARN_RATE * (m_hat / (jnp.sqrt(v_hat) + ADAM_EPS) + decay_rate * master)
     return master_new, moment_new, second_new
 
+def adam_kernel(lp, lm, lv, hp, hm, hv, sp, sm, sv, own, stat, lp_o, lm_o, lv_o, hp_o, hm_o, hv_o, sp_o, sm_o, sv_o, loss, grad):
+    step = pl.program_id(ZERO)
+    clip = F_ONE / jnp.maximum(F_ONE, jnp.sqrt(stat[ZERO, ZERO:ONE, ZERO:ONE]))
+    for l in range(TWO):
+        for r in range(UPDATE_ROWS):
+            grad[l:l + ONE, LANES * r:LANES * r + LANES] = own[pl.ds(l * SLOT_ROWS + UPDATE_ROWS * step + r, ONE), :]
+    block = (TWO, UPDATE_ROWS * LANES)
+    spot = iota(block, ONE) + (UPDATE_ROWS * LANES) * step + SHARD_ROWS * LANES * lax.axis_index('fsdp')
+    decay = jnp.where(spot < ROW_VEC * LANES, WEIGHT_DECAY, F_ZERO)
+    lp_o[...], lm_o[...], lv_o[...] = adam_update(lp[...], grad[...] * clip, lm[...], lv[...], decay)
+
+    @pl.when(step == ZERO)
+    def _():
+        for j in range(EIGHT):
+            lanes = slice(LANES * j, min(LANES * j + LANES, CLASSES))
+            g = own[HEAD_OFF + IMAGES * j:HEAD_OFF + IMAGES * j + IMAGES, ZERO:lanes.stop - lanes.start] * clip
+            hp_o[:, lanes], hm_o[:, lanes], hv_o[:, lanes] = adam_update(hp[:, lanes], g, hm[:, lanes], hv[:, lanes], WEIGHT_DECAY)
+        sp_o[...], sm_o[...], sv_o[...] = adam_update(sp[...], own[SMALL_OFF:SMALL_OFF + ONE, :] * clip, sm[...], sv[...], F_ZERO)
+        loss[...] = stat[ONE] / GLOBAL_IMAGES
+
+
+def update(lp, lm, lv, hp, hm, hv, sp, sm, sv, own, stat):
+    piece = pl.BlockSpec((TWO, UPDATE_ROWS * LANES), lambda i: (ZERO, i))
+
+    def whole(x):
+        return pl.BlockSpec(x.shape, lambda i: (ZERO,) * x.ndim)
+    tile = jax.ShapeDtypeStruct((STEP8, LANES), F32)
+    return pl.pallas_call(
+        adam_kernel,
+        grid=(pl.cdiv(SHARD_ROWS, UPDATE_ROWS),),
+        out_shape=tuple(jax.ShapeDtypeStruct(x.shape, F32) for x in (lp, lm, lv, hp, hm, hv, sp, sm, sv)) + (tile,),
+        in_specs=[piece] * THREE + [whole(x) for x in (hp, hm, hv, sp, sm, sv, own, stat)],
+        out_specs=(piece,) * THREE + tuple(whole(x) for x in (hp, hm, hv, sp, sm, sv, tile)),
+        scratch_shapes=[pltpu.VMEM((TWO, UPDATE_ROWS * LANES), F32)],
+        name='update',
+    )(lp, lm, lv, hp, hm, hv, sp, sm, sv, own, stat)
+
 
 def solution(mesh):
     row_spec = P('fsdp')
@@ -794,24 +848,16 @@
     out_specs = (P(),) + in_specs[TWO:]
 
     def device_step(act_in, labels, layer_p, head_w, small_p, layer_m, head_m, small_m, layer_v, head_v, small_v):
-        mat_len = ROW_VEC * LANES
         quads = jnp.pad(act_in.reshape(QUADS, QVALID, CH), ((ZERO, ZERO), (ZERO, QROWS - QVALID), (ZERO, ZERO))).reshape(ALL_ROWS, CH)
         layer_bf = jnp.pad(layer_p.astype(BF16).reshape(TWO, SHARD_ROWS, LANES), ((ZERO, ZERO), (ZERO, ONE), (ZERO, ZERO)))
         head_bf = jnp.pad(head_w.astype(BF16), ((ZERO, ZERO), (ZERO, CLASS_PAD - CLASSES))).reshape(IMAGES, EIGHT, LANES).transpose(ONE, ZERO, TWO).reshape(TH, LANES)
         small_bf = jnp.pad(small_p.astype(BF16).reshape(ONE, LANES), ((ZERO, 15), (ZERO, ZERO)))
         pack = jnp.concatenate([layer_bf.reshape(TWO * SLOT_ROWS, LANES), head_bf, small_bf])
         own, stat, _ = train_step(quads, jnp.broadcast_to(labels[:, None], (IMAGES, LANES)), pack)
-        layer_g = own[:HEAD_OFF].reshape(TWO, SLOT_ROWS, LANES)[:, :SHARD_ROWS].reshape(TWO, SHARD_ROWS * LANES)
-        head_g = own[HEAD_OFF:SMALL_OFF].reshape(EIGHT, IMAGES, LANES).transpose(ONE, ZERO, TWO).reshape(IMAGES, CLASS_PAD)[:, :CLASSES]
-        small_g = own[SMALL_OFF]
-        loss_value = stat[ONE, ZERO, ZERO] / GLOBAL_IMAGES
-        clip_scale = F_ONE / jnp.maximum(F_ONE, jnp.sqrt(stat[ZERO, ZERO, ZERO]))
-        shard_len = layer_p.shape[ONE]
-        flat_pos = lax.axis_index('fsdp') * shard_len + jnp.arange(shard_len)
-        layer_decay = jnp.where(flat_pos < mat_len, WEIGHT_DECAY, F_ZERO)[None, :]
-        new_lp, new_lm, new_lv = adam_update(layer_p, layer_g * clip_scale, layer_m, layer_v, layer_decay)
-        new_hw, new_hm, new_hv = adam_update(head_w, head_g * clip_scale, head_m, head_v, WEIGHT_DECAY)
-        new_sp, new_sm, new_sv = adam_update(small_p, small_g * clip_scale, small_m, small_v, F_ZERO)
+        flat_small = [x.reshape(ONE, LANES) for x in (small_p, small_m, small_v)]
+        new_lp, new_lm, new_lv, new_hw, new_hm, new_hv, new_sp, new_sm, new_sv, loss = update(layer_p, layer_m, layer_v, head_w, head_m, head_v, *flat_small, own, stat)
+        new_sp, new_sm, new_sv = [x.reshape(LANES) for x in (new_sp, new_sm, new_sv)]
+        loss_value = loss[ZERO, ZERO]
         return (loss_value, new_lp, new_hw, new_sp, new_lm, new_hm, new_sm, new_lv, new_hv, new_sv)
 
     return jax.shard_map(device_step, mesh=mesh, in_specs=in_specs, out_specs=out_specs, check_vma=False)

time: 293 us -> 278 us (0.949)
  other arithmetic: 10.9 us -> 3.89 us
  Pallas kernels: 269 us -> 266 us
    pallas_call x1, Pallas kernels: 269 us -> 257 us  [train_step(): pl.pallas_call(step_kernel, out_shape=(jax.ShapeDtypeStruct((AG_ROWS, LAN...]
    sub x3 -> x0, other arithmetic: 9.47 us -> none  [adam_update(): master - LEARN_RATE * (m_hat / (jnp.sqrt(v_hat) + ADAM_EPS) + decay_rate...]
    pallas_call x0 -> x1, Pallas kernels: none -> 8.92 us  [update(): pl.pallas_call(adam_kernel, grid=(pl.cdiv(SHARD_ROWS, UPDATE_ROWS),), out...]
where the time goes in v5:
time: 278 us
  Pallas kernels  266 us (96%)
  local copies, waits for them, and re-layouts  6.94 us (2%)
  other arithmetic  3.89 us (1%)
    pallas_call x1, Pallas kernels, train_step(): pl.pallas_call(step_kernel, out_shape=(jax.ShapeDtypeStruct((AG_ROWS, LAN...  257 us
    pallas_call x1, Pallas kernels, update(): pl.pallas_call(adam_kernel, grid=(pl.cdiv(SHARD_ROWS, UPDATE_ROWS),), out...  8.92 us

profile of v5, /device:TPU:0, one launch (start us, length us, event | category | flops | bytes accessed | tf_op | source)
XLA Modules:
  0.0 277.8 jit_solution(4855403222524730473)
XLA Ops:
  0.6 0.7 convert_bitcast_fusion
  1.3 1.3 broadcast_in_dim.2.labels
  2.6 0.9 convert_element_type.18
  3.6 1.5 convert_element_type.17
  5.0 0.9 reshape.65
  5.9 0.0 copy-start
  6.0 0.9 fusion.1.pack
  6.9 0.7 copy-done
  7.6 0.9 copy.22
  8.5 0.5 reshape.63
  9.0 1.4 pad.16
  10.3 257.3 %train_step.1 = (f32[2352,128]{1,0:T(8,128)}, f32[2,8,128]{2,1,0:T(8,128)}, bf16[2,2,2,2,2352,128]{5,4,3,2,1,0:T(8,128)(2,1)}) custom-call(bf16[1664,512]{1,0:T(8,128)(2,1)} %bitcast.19, s32[32,128]{1,0:T(8,128)} %broadcast_in_dim.2.labels, bf16[2352,128]{1,0:T(8,128)(2,1)} %fusion.1.pack), custom_call_target="tpu_custom_call" | custom-call | tf_op jit(solution)/shard_map/train_step/pallas_call | solution.py:772
  267.6 8.9 %update.1 = (f32[2,132992]{1,0:T(2,128)}, f32[2,132992]{1,0:T(2,128)}, f32[2,132992]{1,0:T(2,128)}, f32[32,1000]{1,0:T(8,128)}, f32[32,1000]{1,0:T(8,128)}, /*in...) custom-call(f32[2,132992]{1,0:T(2,128)} %lp.1, ...), custom_call_target="tpu_custom_call" | custom-call | tf_op jit(solution)/shard_map/update/pallas_call | solution.py:833
  276.6 1.2 slice.3
  (2 shorter events, 0.1 us)
Async XLA Ops:
  5.9 1.6 copy-start
